TPU v7x, 128 devices: a whole 4x4x4 slice. The times are simulated.
128 devices in a mesh: row: 8 (over y, core), col: 16 (over x, z).
Axes of the slice: x: 4, y: 4, z: 4, core: 2. Of those that a mesh axis runs over, the one named last changes fastest.
Arguments:
- observed: bfloat16 [128, 512, 188], P('row', 'col'), may hold values from -6 to 6
- library: bfloat16 [188, 2048], replicated, may hold values from -0.125 to 0.125
- warm: bfloat16 [128, 512, 2048], P('row', 'col'), may hold values from 0 to 1
- match_peer: int32 [32, 16, 8], P('row', 'col'), may hold values from 0 to 15
- match_slot: int32 [32, 16, 8], P('row', 'col'), may hold values from 0 to 1
- match_count: int32 [32, 16], P('row', 'col'), may hold values from 1 to 8
- match_weight: float32 [32, 16, 8], P('row', 'col'), may hold values from 0.1 to 10
- wanted: int32 [8, 256, 2], P('row', 'col'), may hold values from 0 to 3
- threshold: float32 [2048], replicated, may hold values from 0.02 to 0.2
Outputs:
- abundance: bfloat16 [128, 512, 2048], P('row', 'col')
- misfit: float32 [128, 512, 188], P('row', 'col')
Inputs may be any that keep to these rules, and one draw needn't show every extreme that they name: `match_peer`: col index along the device's own col group. `wanted`: every device names exactly 2 blocks, repeats allowed, of every device of its col group, itself included.
All inputs are finite; a program needn't handle non-finite values.
Results may differ from a plain program's by a relative error of at most 0.0025.
The roundings to bfloat16 on the way count: a program that leaves them out, or rounds other values in their place, can miss the bound.
Values may be sent and summed in bfloat16 or wider, within the bound.
No kernel may reach another device: no remote copies, remote signals or barrier semaphores. Data moves between devices by JAX's collectives and lax.ppermute only.
A program may use at most 192 MiB of HBM per device.

v0:
```python
import functools

import jax
import jax.numpy as jnp
from jax import lax
from jax.experimental import pallas as pl
from jax.experimental.pallas import tpu as pltpu
from jax.sharding import PartitionSpec as P

BLOCK_ROWS = 4
MU = 1.0
GAMMA = 0.6
ETA = 0.3
TOTAL = 1.0 + GAMMA + ETA
LANES = 128
BANDS_PAD = 256
CODE_SCALE = 64000.0
CODE_SHIFT = 32768.0
MIB = 1024 * 1024

F32 = jnp.float32
BF16 = jnp.bfloat16


def params(limit_mib):
    return pltpu.CompilerParams(vmem_limit_bytes=limit_mib * MIB)


def cost(flops, moved):
    return pl.CostEstimate(flops=flops, bytes_accessed=moved, transcendentals=0)


def times_transposed(left, right):
    return lax.dot_general(
        left, right, (((1,), (1,)), ((), ())), preferred_element_type=F32
    )


def encode_fixed(value):
    return jnp.round(value * CODE_SCALE - CODE_SHIFT).astype(jnp.int32).astype(jnp.int16)


def decode_fixed(code):
    return (code.astype(jnp.int32).astype(F32) + CODE_SHIFT) * (1.0 / CODE_SCALE)


def encode_float(value):
    return value.astype(BF16)


def decode_float(code):
    return code.astype(F32)


def spread_kernel(tile_ref, out_ref):
    for p in range(out_ref.shape[0]):
        out_ref[p] = tile_ref[:, p * LANES : (p + 1) * LANES]


def spread(tile, peers):
    pixels, atoms = tile.shape
    step = pixels // 8
    return pl.pallas_call(
        spread_kernel,
        grid=(8,),
        in_specs=[pl.BlockSpec((step, atoms), lambda i: (i, 0))],
        out_specs=pl.BlockSpec((peers, step, LANES), lambda i: (0, i, 0)),
        out_shape=jax.ShapeDtypeStruct((peers, pixels, LANES), tile.dtype),
        compiler_params=params(16),
        cost_estimate=cost(pixels * atoms, 4 * pixels * atoms),
        name="spread",
    )(tile)


def inverse_kernel(lib_ref, inv_ref):
    size = lib_ref.shape[0]
    lib = lib_ref[...]
    rows = lax.broadcasted_iota(jnp.int32, (size, size), 0)
    cols = lax.broadcasted_iota(jnp.int32, (size, size), 1)
    eye = (rows == cols).astype(F32)
    gram = times_transposed(lib, lib) + MU * eye
    bound = jnp.max(jnp.sum(jnp.abs(gram), axis=1, keepdims=True))
    inv_ref[...] = eye * (2.0 / (1.0 + bound))

    def exact(a, b):
        return jnp.dot(a, b, precision=lax.Precision.HIGHEST, preferred_element_type=F32)

    def unfinished(state):
        count, worst = state
        return jnp.logical_and(count < 22, worst > 1e-4)

    def improve(state):
        count, _ = state
        x = inv_ref[...]
        rest = eye - exact(gram, x)
        inv_ref[...] = x + exact(x, rest)
        return count + 1, jnp.max(jnp.sum(jnp.abs(rest), axis=1, keepdims=True))

    lax.while_loop(unfinished, improve, (jnp.int32(0), jnp.float32(1.0)))


def gram_inverse(lib):
    size = lib.shape[0]
    return pl.pallas_call(
        inverse_kernel,
        out_shape=jax.ShapeDtypeStruct((size, size), F32),
        compiler_params=params(16),
        cost_estimate=cost(10 * 12 * size**3, 4 * size * size),
        name="inverse",
    )(lib)


def solve_kernel(first, *refs):
    if first:
        obs, lib, inv, thr, z, up, down, left, right, parts, primal = refs[:11]
        padded, base, low, back = refs[11:]
    else:
        obs, lib, inv, thr, z, up, down, left, right, old_parts, old_primal, mix, parts = refs[:13]
        padded, base, low, back = refs[13:]
    i = pl.program_id(0)
    peers, pixels, _ = z.shape
    row = up.shape[1]
    block = obs.shape[0]

    @pl.when(i == 0)
    def _():
        padded[:, :row] = up[...]
        padded[:, row : row + pixels] = z[...]
        padded[:, row + pixels :] = down[...]

    at = pl.multiple_of(i * block, block)
    base[...] = jnp.dot(obs[...], lib[...], preferred_element_type=F32)
    for p in range(peers):
        lanes = slice(p * LANES, (p + 1) * LANES)
        value = base[:, lanes] + MU * padded[p, pl.ds(at + row, block), :].astype(F32)
        if not first:
            mixed = decode_fixed(mix[p])
            fresh = jnp.maximum(old_parts[:, lanes] + (GAMMA / TOTAL) * mixed, 0.0)
            value = value + MU * (fresh - old_primal[:, lanes])
        low[:, lanes] = value.astype(BF16)
    small = times_transposed(low[...], lib[...])
    solved = jnp.dot(
        small, inv[...], precision=lax.Precision.HIGHEST, preferred_element_type=F32
    )
    back[...] = jnp.dot(solved.astype(BF16), lib[...], preferred_element_type=F32)
    place = lax.broadcasted_iota(jnp.int32, (block, LANES), 0) % row
    for p in range(peers):
        lanes = slice(p * LANES, (p + 1) * LANES)
        here = padded[p, pl.ds(at + row, block), :].astype(F32)
        above = padded[p, pl.ds(at, block), :].astype(F32)
        below = padded[p, pl.ds(at + 2 * row, block), :].astype(F32)

        def edge(halo):
            return jnp.concatenate(
                [
                    jnp.broadcast_to(halo[0, k : k + 1, lanes], (row, LANES))
                    for k in range(block // row)
                ],
                axis=0,
            )

        before = jnp.where(place == 0, edge(left), pltpu.roll(here, 1, 0))
        after = jnp.where(place == row - 1, edge(right), pltpu.roll(here, block - 1, 0))
        spatial = 0.25 * (above + below + before + after)
        unmixed = (base[:, lanes] + MU * here - back[:, lanes]) / MU
        if first:
            primal[:, lanes] = unmixed
        parts[:, lanes] = (unmixed + ETA * spatial) * (1.0 / TOTAL) - thr[:, lanes]


def solve(first, obs, lib, inv, thr, z, halos, carried=()):
    peers, pixels, _ = z.shape
    atoms = lib.shape[1]
    up, down, left, right = halos
    row = up.shape[1]
    block = BLOCK_ROWS * row
    steps = pixels // block
    whole = lambda a: pl.BlockSpec(a.shape, lambda i, n=a.ndim: (0,) * n)
    tile = pl.BlockSpec((block, atoms), lambda i: (i, 0))
    piece = pl.BlockSpec((peers, block, LANES), lambda i: (0, i, 0))
    side = pl.BlockSpec((1, BLOCK_ROWS, atoms), lambda i: (i, 0, 0))
    full = jax.ShapeDtypeStruct((pixels, atoms), F32)
    return pl.pallas_call(
        functools.partial(solve_kernel, first),
        grid=(steps,),
        in_specs=[
            pl.BlockSpec((block, obs.shape[1]), lambda i: (i, 0)),
            whole(lib), whole(inv), whole(thr), whole(z), whole(up), whole(down), side, side,
        ]
        + ([] if first else [tile, tile, piece]),
        out_specs=[tile, tile] if first else tile,
        out_shape=[full, full] if first else full,
        scratch_shapes=[
            pltpu.VMEM((peers, pixels + 2 * row, LANES), BF16),
            pltpu.VMEM((block, atoms), F32),
            pltpu.VMEM((block, atoms), BF16),
            pltpu.VMEM((block, atoms), F32),
        ],
        compiler_params=params(34),
        cost_estimate=cost(6 * pixels * atoms * BANDS_PAD, 16 * pixels * atoms),
        name="solve_first" if first else "solve_second",
    )(obs, lib, inv, thr, z, up, down, left, right, *carried)


def mix_kernel(encode, matches, place_ref, weight_ref, z_ref, out_ref):
    def one(t, carry):
        total = None
        for k in range(matches):
            term = z_ref[place_ref[t * matches + k]].astype(F32) * weight_ref[t * matches + k]
            total = term if total is None else total + term
        out_ref[t] = encode(total)
        return carry

    lax.fori_loop(0, out_ref.shape[0], one, 0)


def mix(encode, dtype, place, weight, z, matches, block):
    peers, pixels, _ = z.shape
    blocks = peers * pixels // block
    out = pl.pallas_call(
        functools.partial(mix_kernel, encode, matches),
        in_specs=[
            pl.BlockSpec(memory_space=pltpu.SMEM),
            pl.BlockSpec(memory_space=pltpu.SMEM),
            pl.BlockSpec(memory_space=pltpu.VMEM),
        ],
        out_specs=pl.BlockSpec(memory_space=pltpu.VMEM),
        out_shape=jax.ShapeDtypeStruct((blocks, block, LANES), dtype),
        compiler_params=params(16),
        cost_estimate=cost(2 * matches * blocks * block * LANES, 4 * blocks * block * LANES),
        name="mix",
    )(place, weight, z.reshape(blocks, block, LANES))
    return out.reshape(peers, pixels, LANES)


def fresh_kernel(parts, mix_ref, out_ref):
    for p in range(out_ref.shape[0]):
        lanes = slice(p * LANES, (p + 1) * LANES)
        mixed = decode_fixed(mix_ref[p])
        out_ref[p] = jnp.maximum(parts[:, lanes] + (GAMMA / TOTAL) * mixed, 0.0).astype(BF16)


def fresh_pieces(parts, mixed):
    peers, pixels, _ = mixed.shape
    atoms = parts.shape[1]
    step = pixels // 8
    piece = pl.BlockSpec((peers, step, LANES), lambda i: (0, i, 0))
    return pl.pallas_call(
        fresh_kernel,
        grid=(8,),
        in_specs=[pl.BlockSpec((step, atoms), lambda i: (i, 0)), piece],
        out_specs=piece,
        out_shape=jax.ShapeDtypeStruct((peers, pixels, LANES), BF16),
        compiler_params=params(16),
        cost_estimate=cost(4 * pixels * atoms, 8 * pixels * atoms),
        name="fresh",
    )(parts, mixed)


def final_kernel(parts, mix_ref, obs, lib, out_ref, misfit_ref):
    for p in range(mix_ref.shape[0]):
        lanes = slice(p * LANES, (p + 1) * LANES)
        mixed = decode_float(mix_ref[p])
        out_ref[:, lanes] = jnp.maximum(
            parts[:, lanes] + (GAMMA / TOTAL) * mixed, 0.0
        ).astype(BF16)
    rebuilt = times_transposed(out_ref[...], lib[...])
    misfit_ref[...] = (obs[...].astype(F32) - rebuilt)[:, : misfit_ref.shape[1]]


def final(parts, mixed, obs, lib, bands):
    peers, pixels, _ = mixed.shape
    atoms = parts.shape[1]
    step = pixels // 4
    tile = lambda n: pl.BlockSpec((step, n), lambda i: (i, 0))
    return pl.pallas_call(
        final_kernel,
        grid=(4,),
        in_specs=[
            tile(atoms),
            pl.BlockSpec((peers, step, LANES), lambda i: (0, i, 0)),
            tile(obs.shape[1]),
            pl.BlockSpec(lib.shape, lambda i: (0, 0)),
        ],
        out_specs=[tile(atoms), tile(bands)],
        out_shape=[
            jax.ShapeDtypeStruct((pixels, atoms), BF16),
            jax.ShapeDtypeStruct((pixels, bands), F32),
        ],
        compiler_params=params(16),
        cost_estimate=cost(2 * pixels * atoms * BANDS_PAD, 8 * pixels * atoms),
        name="final",
    )(parts, mixed, obs, lib)


def match_table(peer, slot, count, weight, wanted, blocks):
    matches = weight.shape[1]
    slots = wanted.shape[1]
    ranks = jnp.arange(matches, dtype=jnp.int32)
    masked = jnp.where(ranks[None, :] < count[:, None], weight, 0.0)
    share = masked / jnp.sum(masked, axis=1, keepdims=True)
    column = peer * slots + slot
    same = column[:, :, None] == column[:, None, :]
    merged = jnp.sum(jnp.where(same, share[:, None, :], 0.0), axis=2).astype(BF16).astype(F32)
    again = jnp.any(same & (ranks[None, None, :] < ranks[None, :, None]), axis=2)
    coef = jnp.where(again, 0.0, merged)
    asked = wanted.reshape(-1)
    targets = jnp.arange(asked.shape[0], dtype=jnp.int32)
    chosen = jnp.sum(
        jnp.where(column[:, :, None] == targets[None, None, :], asked[None, None, :], 0), axis=2
    )
    place = peer * blocks + chosen
    return jnp.concatenate([coef.reshape(-1), place.astype(F32).reshape(-1)])


def shifted(array, axis, up):
    peers = lax.axis_size(axis)
    pairs = [(k, k + 1) for k in range(peers - 1)]
    return lax.ppermute(array, axis, pairs if up else [(b, a) for a, b in pairs])


def exchanged(pieces):
    return lax.all_to_all(pieces, "col", 0, 0, tiled=True)


def side_rows(column, blocks):
    atoms = column.shape[-1]
    return column.astype(F32).reshape(blocks, -1, atoms)


def local(
    observed, library, warm, match_peer, match_slot, match_count, match_weight, wanted, threshold
):
    tile_rows, tile_cols, atoms = warm.shape
    bands = library.shape[0]
    pixels = tile_rows * tile_cols
    blocks = tile_rows // BLOCK_ROWS
    block = BLOCK_ROWS * tile_cols
    peers = lax.axis_size("col")
    matches = match_weight.shape[2]

    pieces = spread(warm.reshape(pixels, atoms), peers)
    strip = exchanged(pieces)

    table = match_table(
        match_peer[:, 0], match_slot[:, 0], match_count[:, 0], match_weight[:, 0], wanted[0], blocks
    )
    tables = lax.all_gather(table, "col")
    half = table.shape[0] // 2
    weight = tables[:, :half].reshape(-1)
    place = tables[:, half:].astype(jnp.int32).reshape(-1)

    halos = (
        shifted(pieces[:, pixels - tile_cols :], "row", True),
        shifted(pieces[:, :tile_cols], "row", False),
        side_rows(shifted(warm[:, -1], "col", True), blocks),
        side_rows(shifted(warm[:, 0], "col", False), blocks),
    )
    lib = jnp.pad(library, ((0, BANDS_PAD - bands), (0, 0)))
    obs = jnp.pad(observed.reshape(pixels, bands), ((0, 0), (0, BANDS_PAD - bands)))
    inv = gram_inverse(lib)
    thr = threshold[None, :]
    parts, primal = solve(True, obs, lib, inv, thr, pieces, halos)

    mixed = exchanged(mix(encode_fixed, jnp.int16, place, weight, strip, matches, block))
    pieces = fresh_pieces(parts, mixed)
    strip = exchanged(pieces)

    sides = pieces.reshape(peers, tile_rows, tile_cols, LANES)
    by_row = lambda a: jnp.moveaxis(a, 0, 1).reshape(tile_rows, atoms)
    halos = (
        shifted(pieces[:, pixels - tile_cols :], "row", True),
        shifted(pieces[:, :tile_cols], "row", False),
        side_rows(by_row(shifted(sides[:, :, -1], "col", True)), blocks),
        side_rows(by_row(shifted(sides[:, :, 0], "col", False)), blocks),
    )
    parts = solve(False, obs, lib, inv, thr, pieces, halos, (parts, primal, mixed))

    mixed = exchanged(mix(encode_float, BF16, place, weight, strip, matches, block))
    abundance, misfit = final(parts, mixed, obs, lib, bands)
    return (
        abundance.reshape(tile_rows, tile_cols, atoms),
        misfit.reshape(tile_rows, tile_cols, bands),
    )


def solution(mesh):
    return jax.shard_map(
        local,
        mesh=mesh,
        in_specs=(
            P("row", "col", None),
            P(),
            P("row", "col", None),
            P("row", "col", None),
            P("row", "col", None),
            P("row", "col"),
            P("row", "col", None),
            P("row", "col", None),
            P(),
        ),
        out_specs=(P("row", "col", None), P("row", "col", None)),
        check_vma=False,
    )
```

profile of v0, /device:TPU:2, one launch (start us, length us, event | category | flops | bytes accessed | tf_op | source)
XLA Modules:
  0.0 235.5 jit_solution(11496960005638710302)
XLA Ops:
  0.6 1.6 copy-done.12
  2.2 3.1 %spread.1.refs_4_ = bf16[16,512,128]{2,1,0:T(8,128)(2,1)} custom-call(bf16[512,2048]{1,0:T(8,128)(2,1)S(1)} %bitcast.36), custom_call_target="tpu_custom_call" | custom-call | flops 1048576 | bytes 4194304 | tf_op jit(solution)/shard_map/spread/pallas_call | solution.py:63
  5.3 8.5 %all-to-all-start = ((bf16[16,512,128]{2,1,0:T(8,128)(2,1)}), bf16[16,512,128]{2,1,0:T(8,128)(2,1)S(1)}, u32[]{:S(2)}, u32[]{:S(2)}) async-start(bf16[16,512,128]{2,1,0:T(8,128)(2,1)} %spread.1.refs_4_), calls=%async_computation | async-start | bytes 4194304 | tf_op jit(solution)/shard_map/all_to_all | solution.py:323
  13.8 0.2 select_reduce_fusion.1
  14.0 0.2 fusion.1
  14.3 0.2 fusion
  14.5 0.1 select_n.27
  14.6 0.1 copy.21
  14.7 0.1 broadcast_in_dim.54
  14.8 0.2 select_reduce_fusion
  15.0 0.1 reduce_sum.32
  15.1 0.1 mul.26
  15.2 0.6 dynamic-slice
  16.4 0.2 maximum_dynamic-update-slice_fusion
  16.6 48.7 %all-reduce.2 = f32[1024]{0:T(1024)S(1)} all-reduce(f32[1024]{0:T(1024)S(1)} %maximum_dynamic-update-slice_fusion), channel_id=2, replica_groups=mesh['row'=8,'col'=16] {'col'}, use_global_device_ids=true, to_apply=%add.2 | all-reduce | flops 1024 | bytes 8192
  65.7 5.0 %mix.2 = s16[64,128,128]{2,1,0:T(8,128)(2,1)S(1)} custom-call(s32[512]{0:T(512)S(1)} %reshape.143.place_ref, f32[512]{0:T(512)S(1)} %reshape.144.weight_ref, bf16[64,128,128]{2,1,0:T(8,128)(2,1)S(1)} %bitcast.32), custom_call_target="tpu_custom_call" | custom-call | flops 16777216 | bytes 4194304 | tf_op jit(solution)/shard_map/mix/pallas_call | solution.py:220
  70.7 1.3 copy-done.9
  72.1 9.1 %all-to-all-start.1 = ((s16[16,512,128]{2,1,0:T(8,128)(2,1)}), s16[16,512,128]{2,1,0:T(8,128)(2,1)S(1)}, u32[]{:S(2)}, u32[]{:S(2)}) async-start(s16[16,512,128]{2,1,0:T(8,128)(2,1)} %bitcast.34), calls=%async_computation.1 | async-start | bytes 4194304 | tf_op jit(solution)/shard_map/all_to_all | solution.py:323
  81.2 1.7 fusion.6
  82.8 1.9 collective-permute-start
  84.8 1.3 collective-permute-start.1
  86.1 1.4 fusion.5
  87.5 3.4 %collective-permute-start.2 = (bf16[16,2048]{1,0:T(8,128)(2,1)S(1)}, bf16[16,2048]{1,0:T(8,128)(2,1)}, u32[]{:S(2)}, u32[]{:S(2)}) collective-permute-start(bf16[16,2048]{1,0:T(8,128)(2,1)S(1)} %bitcast.44), channel_id=1, source_target_pairs={{0,1},{1,2},{2,3},{3,4},{4,5},{5,6},{6,7},{7,8},{8,9},{9,10},{10,1... | collective-permute-start | bytes 196616 | tf_op jit(solution)/shard_map/ppermute | solution.py:319
  90.9 0.7 copy.34
  91.6 4.6 %collective-permute-start.3 = (bf16[16,2048]{1,0:T(8,128)(2,1)}, bf16[16,2048]{1,0:T(8,128)(2,1)}, u32[]{:S(2)}, u32[]{:S(2)}) collective-permute-start(bf16[16,2048]{1,0:T(8,128)(2,1)} %bitcast.29), channel_id=1, source_target_pairs={{1,0},{2,1},{3,2},{4,3},{5,4},{6,5},{7,6},{8,7},{9,8},{10,9},{11,1... | collective-permute-start | bytes 196616 | tf_op jit(solution)/shard_map/ppermute | solution.py:319
  96.1 1.2 pad.9.lib_ref.refs_1_.lib
  97.4 7.3 %inverse.1.refs_2_ = f32[256,256]{1,0:T(8,128)S(1)} custom-call(bf16[256,2048]{1,0:T(8,128)(2,1)S(1)} %pad.9.lib_ref.refs_1_.lib), custom_call_target="tpu_custom_call" | custom-call | flops 2013265920 | bytes 262144 | tf_op jit(solution)/shard_map/inverse/pallas_call | solution.py:104
  104.7 0.7 copy-done.14
  105.5 0.9 reshape.153.refs_7_
  106.4 1.5 reshape.155.refs_8_
  108.0 0.9 copy-done.15
  108.9 0.9 copy-done.17
  109.8 9.1 %solve_first.1 = (f32[512,2048]{1,0:T(8,128)S(1)}, f32[512,2048]{1,0:T(8,128)S(1)}) custom-call(bf16[512,256]{1,0:T(8,128)(2,1)S(1)} %pad.8.refs_0_.obs, bf16[256,2048]{1,0:T(8,128)(2,1)S(1)} %pad.9.lib_ref.refs_1_.lib, f32[256,256]{1,0:T(8,128)S(1)} %copy-done.15, f32[1,2048]{1,0:T(1,128)S(1)} %bitcast.37, bf16[16,512,128]{2,1,0:T(8,128)(2,1)} %spread.1.refs_4_, ...), custom_call_target="tpu_custom_call" | custom-call | flops 1610612736 | bytes 16777216 | tf_op jit(solution)/shard_map/solve_first/pallas_call | solution.py:183
  118.9 2.0 copy-done.3
  120.9 2.0 copy-done.10
  122.9 1.3 copy-done
  124.2 1.6 copy-done.1
  125.8 2.2 copy-done.4
  128.0 1.4 fresh.1.refs_4_
  129.4 31.8 %all_to_all.20 = bf16[16,512,128]{2,1,0:T(8,128)(2,1)S(1)} all-to-all(bf16[16,512,128]{2,1,0:T(8,128)(2,1)S(1)} %fresh.1.refs_4_), channel_id=1, replica_groups=mesh['row'=8,'col'=16] {'col'}, dimensions={0} | all-to-all | bytes 4194304 | tf_op jit(solution)/shard_map/all_to_all | solution.py:323
  161.2 4.4 %mix.3 = bf16[64,128,128]{2,1,0:T(8,128)(2,1)S(1)} custom-call(s32[512]{0:T(512)S(1)} %reshape.143.place_ref, f32[512]{0:T(512)S(1)} %reshape.144.weight_ref, bf16[64,128,128]{2,1,0:T(8,128)(2,1)S(1)} %bitcast.35), custom_call_target="tpu_custom_call" | custom-call | flops 16777216 | bytes 4194304 | tf_op jit(solution)/shard_map/mix/pallas_call | solution.py:220
  165.7 1.3 copy-done.8
  167.0 6.2 %all-to-all-start.3 = ((bf16[16,512,128]{2,1,0:T(8,128)(2,1)}), bf16[16,512,128]{2,1,0:T(8,128)(2,1)}, u32[]{:S(2)}, u32[]{:S(2)}) async-start(bf16[16,512,128]{2,1,0:T(8,128)(2,1)} %bitcast.33), calls=%async_computation.3 | async-start | bytes 4194304 | tf_op jit(solution)/shard_map/all_to_all | solution.py:323
  173.1 0.2 fusion.3
  173.4 3.4 %collective-permute-start.6 = (bf16[16,16,128]{2,0,1:T(8,128)(2,1)S(1)}, bf16[16,16,128]{2,0,1:T(8,128)(2,1)S(1)}, u32[]{:S(2)}, u32[]{:S(2)}) collective-permute-start(bf16[16,16,128]{2,0,1:T(8,128)(2,1)S(1)} %bitcast.43), channel_id=1, source_target_pairs={{0,1},{1,2},{2,3},{3,4},{4,5},{5,6},{6,7},{7,8},{8,9},{9,10},{10,1... | collective-permute-start | bytes 196616 | tf_op jit(solution)/shard_map/ppermute | solution.py:319
  176.8 0.7 fusion.4
  177.5 0.7 copy.32
  178.2 4.6 %collective-permute-start.7 = (bf16[16,16,128]{2,0,1:T(8,128)(2,1)}, bf16[16,16,128]{2,0,1:T(8,128)(2,1)}, u32[]{:S(2)}, u32[]{:S(2)}) collective-permute-start(bf16[16,16,128]{2,0,1:T(8,128)(2,1)} %bitcast.27), channel_id=1, source_target_pairs={{1,0},{2,1},{3,2},{4,3},{5,4},{6,5},{7,6},{8,7},{9,8},{10,9},{11,1... | collective-permute-start | bytes 196616 | tf_op jit(solution)/shard_map/ppermute | solution.py:319
  182.8 2.6 %collective-permute-start.4 = (bf16[16,32,128]{2,1,0:T(8,128)(2,1)}, bf16[16,32,128]{2,1,0:T(8,128)(2,1)}, u32[]{:S(2)}, u32[]{:S(2)}) collective-permute-start(bf16[16,32,128]{2,1,0:T(8,128)(2,1)} %get-tuple-element.13), channel_id=1, source_target_pairs={{0,16},{16,32},{32,48},{48,64},{64,80},{80,96},{96,112},{1,17},{17... | collective-permute-start | bytes 393224 | tf_op jit(solution)/shard_map/ppermute | solution.py:319
  185.4 1.3 collective-permute-start.5
  186.7 18.7 %collective-permute-done.6 = bf16[16,16,128]{2,0,1:T(8,128)(2,1)S(1)} collective-permute-done((bf16[16,16,128]{2,0,1:T(8,128)(2,1)S(1)}, bf16[16,16,128]{2,0,1:T(8,128)(2,1)S(1)}, u32[]{:S(2)}, u32[]{:S(2)}) %collective-permute-start.6) | collective-permute-done | bytes 65568 | tf_op jit(solution)/shard_map/ppermute | solution.py:319
  205.4 0.7 convert_bitcast_fusion.1
  206.1 0.9 reshape.156.refs_7_
  207.1 1.5 convert_bitcast_fusion
  208.6 1.6 reshape.157.refs_8_
  210.2 1.6 copy-done.2
  211.8 2.2 copy-done.5
  214.0 2.2 copy-done.11
  216.1 0.9 copy-done.13
  217.0 0.9 copy-done.16
  218.0 8.9 %solve_second.1.parts = f32[512,2048]{1,0:T(8,128)S(1)} custom-call(bf16[512,256]{1,0:T(8,128)(2,1)S(1)} %pad.8.refs_0_.obs, bf16[256,2048]{1,0:T(8,128)(2,1)S(1)} %pad.9.lib_ref.refs_1_.lib, f32[256,256]{1,0:T(8,128)S(1)} %copy-done.16, f32[1,2048]{1,0:T(1,128)S(1)} %bitcast.38, bf16[16,512,128]{2,1,0:T(8,128)(2,1)S(1)} %fresh.1.refs_4_, ...), custom_call_target="tpu_custom_call" | custom-call | flops 1610612736 | bytes 16777216 | tf_op jit(solution)/shard_map/solve_second/pallas_call | solution.py:183
  226.9 2.0 copy-done.6
  228.9 2.2 copy-done.7
  231.1 4.5 %final.1 = (bf16[512,2048]{1,0:T(8,128)(2,1)}, f32[512,188]{1,0:T(8,128)}) custom-call(f32[512,2048]{1,0:T(8,128)S(1)} %copy-done.7, bf16[16,512,128]{2,1,0:T(8,128)(2,1)} %all-to-all-done.3.mix_ref, bf16[512,256]{1,0:T(8,128)(2,1)S(1)} %pad.8.refs_0_.obs, bf16[256,2048]{1,0:T(8,128)(2,1)S(1)} %pad.9.lib_ref.refs_1_.lib), custom_call_target="tpu_custom_call" | custom-call | flops 536870912 | bytes 8388608 | tf_op jit(solution)/shard_map/final/pallas_call | solution.py:276
  (57 shorter events, 0.7 us)
Async XLA Ops:
  0.6 1.6 copy-start.12
  5.3 8.5 %copy-start.20 = (f32[4,1,8]{2,1,0:T(1,128)S(1)}, f32[4,1,8]{2,1,0:T(1,128)}, u32[]{:S(2)}) copy-start(f32[4,1,8]{2,1,0:T(1,128)} %param.15) | copy-start | bytes 388
  5.3 8.5 %copy-start.21 = (s32[4,1]{0,1:T(1,128)S(1)}, s32[4,1]{0,1:T(1,128)}, u32[]{:S(2)}) copy-start(s32[4,1]{0,1:T(1,128)} %param.14) | copy-start | bytes 52
  5.3 8.7 %copy-start.22 = (s32[4,1,8]{2,1,0:T(1,128)S(1)}, s32[4,1,8]{2,1,0:T(1,128)}, u32[]{:S(2)}) copy-start(s32[4,1,8]{2,1,0:T(1,128)} %param.13) | copy-start | bytes 388
  5.3 8.7 %copy-start.23 = (s32[4,1,8]{2,1,0:T(1,128)S(1)}, s32[4,1,8]{2,1,0:T(1,128)}, u32[]{:S(2)}) copy-start(s32[4,1,8]{2,1,0:T(1,128)} %param.12) | copy-start | bytes 388
  5.3 9.3 %copy-start.24 = (s32[1,16,2]{1,2,0:T(2,128)S(1)}, s32[1,16,2]{1,2,0:T(2,128)}, u32[]{:S(2)}) copy-start(s32[1,16,2]{1,2,0:T(2,128)} %param.16) | copy-start | bytes 388
  5.3 9.8 %copy-start.25 = (u32[128]{0:T(128)S(1)}, u32[128]{0:T(128)}, u32[]{:S(2)}) copy-start(u32[128]{0:T(128)} %constant.23) | copy-start | bytes 1540
  5.3 60.3 %all-to-all-start = ((bf16[16,512,128]{2,1,0:T(8,128)(2,1)}), bf16[16,512,128]{2,1,0:T(8,128)(2,1)S(1)}, u32[]{:S(2)}, u32[]{:S(2)}) async-start(bf16[16,512,128]{2,1,0:T(8,128)(2,1)} %spread.1.refs_4_), calls=%async_computation | async-start | bytes 4194304 | tf_op jit(solution)/shard_map/all_to_all | solution.py:323
  70.7 1.4 copy-start.9
  72.1 50.9 %all-to-all-start.1 = ((s16[16,512,128]{2,1,0:T(8,128)(2,1)}), s16[16,512,128]{2,1,0:T(8,128)(2,1)S(1)}, u32[]{:S(2)}, u32[]{:S(2)}) async-start(s16[16,512,128]{2,1,0:T(8,128)(2,1)} %bitcast.34), calls=%async_computation.1 | async-start | bytes 4194304 | tf_op jit(solution)/shard_map/all_to_all | solution.py:323
  82.8 25.1 %collective-permute-start = (bf16[16,32,128]{2,1,0:T(8,128)(2,1)}, bf16[16,32,128]{2,1,0:T(8,128)(2,1)}, u32[]{:S(2)}, u32[]{:S(2)}) collective-permute-start(bf16[16,32,128]{2,1,0:T(8,128)(2,1)} %get-tuple-element.17), channel_id=1, source_target_pairs={{0,16},{16,32},{32,48},{48,64},{64,80},{80,96},{96,112},{1,17},{17... | collective-permute-start | bytes 393224 | tf_op jit(solution)/shard_map/ppermute | solution.py:319
  84.8 23.2 %collective-permute-start.1 = (bf16[16,32,128]{2,1,0:T(8,128)(2,1)}, bf16[16,32,128]{2,1,0:T(8,128)(2,1)}, u32[]{:S(2)}, u32[]{:S(2)}) collective-permute-start(bf16[16,32,128]{2,1,0:T(8,128)(2,1)} %get-tuple-element.16), channel_id=1, source_target_pairs={{16,0},{32,16},{48,32},{64,48},{80,64},{96,80},{112,96},{17,1},{33... | collective-permute-start | bytes 393224 | tf_op jit(solution)/shard_map/ppermute | solution.py:319
  87.5 18.0 %collective-permute-start.2 = (bf16[16,2048]{1,0:T(8,128)(2,1)S(1)}, bf16[16,2048]{1,0:T(8,128)(2,1)}, u32[]{:S(2)}, u32[]{:S(2)}) collective-permute-start(bf16[16,2048]{1,0:T(8,128)(2,1)S(1)} %bitcast.44), channel_id=1, source_target_pairs={{0,1},{1,2},{2,3},{3,4},{4,5},{5,6},{6,7},{7,8},{8,9},{9,10},{10,1... | collective-permute-start | bytes 196616 | tf_op jit(solution)/shard_map/ppermute | solution.py:319
  91.6 14.8 %collective-permute-start.3 = (bf16[16,2048]{1,0:T(8,128)(2,1)}, bf16[16,2048]{1,0:T(8,128)(2,1)}, u32[]{:S(2)}, u32[]{:S(2)}) collective-permute-start(bf16[16,2048]{1,0:T(8,128)(2,1)} %bitcast.29), channel_id=1, source_target_pairs={{1,0},{2,1},{3,2},{4,3},{5,4},{6,5},{7,6},{8,7},{9,8},{10,9},{11,1... | collective-permute-start | bytes 196616 | tf_op jit(solution)/shard_map/ppermute | solution.py:319
  97.4 8.1 %copy-start.19 = (bf16[16,32,188]{2,1,0:T(8,128)(2,1)S(1)}, bf16[16,32,188]{2,1,0:T(8,128)(2,1)}, u32[]{:S(2)}) copy-start(bf16[16,32,188]{2,1,0:T(8,128)(2,1)} %param.9) | copy-start | bytes 577540
  97.4 10.5 %copy-start.18 = (f32[2048]{0:T(1024)S(1)}, f32[2048]{0:T(1024)}, u32[]{:S(2)}) copy-start(f32[2048]{0:T(1024)} %param.17) | copy-start | bytes 24580
  104.7 0.7 copy-start.14
  108.0 1.0 copy-start.15
  108.9 0.9 copy-start.17
  118.9 2.0 copy-start.3
  120.9 2.0 copy-start.10
  122.9 1.3 copy-start
  124.2 1.6 copy-start.1
  125.8 2.2 copy-start.4
  165.7 1.3 copy-start.8
  167.0 61.9 %all-to-all-start.3 = ((bf16[16,512,128]{2,1,0:T(8,128)(2,1)}), bf16[16,512,128]{2,1,0:T(8,128)(2,1)}, u32[]{:S(2)}, u32[]{:S(2)}) async-start(bf16[16,512,128]{2,1,0:T(8,128)(2,1)} %bitcast.33), calls=%async_computation.3 | async-start | bytes 4194304 | tf_op jit(solution)/shard_map/all_to_all | solution.py:323
  173.4 32.0 %collective-permute-start.6 = (bf16[16,16,128]{2,0,1:T(8,128)(2,1)S(1)}, bf16[16,16,128]{2,0,1:T(8,128)(2,1)S(1)}, u32[]{:S(2)}, u32[]{:S(2)}) collective-permute-start(bf16[16,16,128]{2,0,1:T(8,128)(2,1)S(1)} %bitcast.43), channel_id=1, source_target_pairs={{0,1},{1,2},{2,3},{3,4},{4,5},{5,6},{6,7},{7,8},{8,9},{9,10},{10,1... | collective-permute-start | bytes 196616 | tf_op jit(solution)/shard_map/ppermute | solution.py:319
  178.2 28.9 %collective-permute-start.7 = (bf16[16,16,128]{2,0,1:T(8,128)(2,1)}, bf16[16,16,128]{2,0,1:T(8,128)(2,1)}, u32[]{:S(2)}, u32[]{:S(2)}) collective-permute-start(bf16[16,16,128]{2,0,1:T(8,128)(2,1)} %bitcast.27), channel_id=1, source_target_pairs={{1,0},{2,1},{3,2},{4,3},{5,4},{6,5},{7,6},{8,7},{9,8},{10,9},{11,1... | collective-permute-start | bytes 196616 | tf_op jit(solution)/shard_map/ppermute | solution.py:319
  182.8 27.4 %collective-permute-start.4 = (bf16[16,32,128]{2,1,0:T(8,128)(2,1)}, bf16[16,32,128]{2,1,0:T(8,128)(2,1)}, u32[]{:S(2)}, u32[]{:S(2)}) collective-permute-start(bf16[16,32,128]{2,1,0:T(8,128)(2,1)} %get-tuple-element.13), channel_id=1, source_target_pairs={{0,16},{16,32},{32,48},{48,64},{64,80},{80,96},{96,112},{1,17},{17... | collective-permute-start | bytes 393224 | tf_op jit(solution)/shard_map/ppermute | solution.py:319
  185.4 24.8 %collective-permute-start.5 = (bf16[16,32,128]{2,1,0:T(8,128)(2,1)}, bf16[16,32,128]{2,1,0:T(8,128)(2,1)}, u32[]{:S(2)}, u32[]{:S(2)}) collective-permute-start(bf16[16,32,128]{2,1,0:T(8,128)(2,1)} %get-tuple-element.12), channel_id=1, source_target_pairs={{16,0},{32,16},{48,32},{64,48},{80,64},{96,80},{112,96},{17,1},{33... | collective-permute-start | bytes 393224 | tf_op jit(solution)/shard_map/ppermute | solution.py:319
  210.2 1.6 copy-start.2
  211.8 2.2 copy-start.5
  213.9 2.2 copy-start.11
  216.1 0.9 copy-start.13
  217.0 0.9 copy-start.16
  226.9 2.0 copy-start.6
  228.9 2.2 copy-start.7
where the time goes:
time: 237 us; the launch traced here: 236 us
  blocking collectives  80.5 us (34%)
  starting transfers between devices  46.7 us (20%)
  Pallas kernels  43.7 us (18%)
  local copies, waits for them, and re-layouts  40.9 us (17%)
  waiting for transfers between devices  18.8 us (8%)
  other arithmetic  3.33 us (1%)
    unnamed x1, blocking collectives  48.7 us
    all_to_all x1, blocking collectives, exchanged(): return lax.all_to_all(pieces, 'col', 0, 0, tiled=True)  31.8 us
    unnamed x59, local copies, waits for them, and re-layouts  30 us
    all_to_all x3, starting transfers between devices, exchanged(): return lax.all_to_all(pieces, 'col', 0, 0, tiled=True)  23.7 us
    ppermute x8, starting transfers between devices, shifted(): lax.ppermute(array, axis, pairs if up else [(b, a) for a, b in pairs])  23 us
    ppermute x8, waiting for transfers between devices, shifted(): lax.ppermute(array, axis, pairs if up else [(b, a) for a, b in pairs])  18.7 us
    pallas_call x2, Pallas kernels, solve(): pl.pallas_call(functools.partial(solve_kernel, first), grid=(steps,), in_...  17.9 us
    pallas_call x2, Pallas kernels, mix(): pl.pallas_call(functools.partial(mix_kernel, encode, matches), in_specs=[...  9.48 us
  transfers between devices with their start and end apart: 11, of which 1 were waited for; matrix products, arithmetic and copies ran while one was open for 7% of the time, Pallas kernels for 11%

commit v1 on v0

v1 whole, which is shorter than its diff:
```python
import functools

import jax
import jax.numpy as jnp
from jax import lax
from jax.experimental import pallas as pl
from jax.experimental.pallas import tpu as pltpu
from jax.sharding import PartitionSpec as P


BLOCK_ROWS = 4
MU = 1.0
GAMMA = 0.6
ETA = 0.3
TOTAL = 1.0 + GAMMA + ETA
LANES = 128
BANDS_PAD = 256
CODE_SCALE = 64000.0
CODE_SHIFT = 32768.0
GROUP = 8
STEPS = 8
WIDE = 2
TABLE_ROWS = 16
MIB = 1024 * 1024

F32 = jnp.float32
BF16 = jnp.bfloat16


def cost(flops, moved):
    return pl.CostEstimate(flops=flops, bytes_accessed=moved, transcendentals=0)


def times_transposed(left, right):
    return lax.dot_general(
        left, right, (((1,), (1,)), ((), ())), preferred_element_type=F32
    )


def encode_fixed(value):
    return jnp.round(value * CODE_SCALE - CODE_SHIFT).astype(jnp.int32).astype(jnp.int16)


def decode_fixed(code):
    return (code.astype(jnp.int32).astype(F32) + CODE_SHIFT) * (1.0 / CODE_SCALE)


def encode_float(value):
    return value.astype(BF16)


def decode_float(code):
    return code.astype(F32)


def spread_kernel(
    blocks, asked_at, peer_at, slot_at, count_at, weight_at, tile, out,
    held, asked, peer, slot, count, weight, rows, table, small, come, go, extra,
):
    peers, pixels, _ = held.shape
    tables = (
        (asked_at, asked), (peer_at, peer), (slot_at, slot), (count_at, count), (weight_at, weight),
    )
    for k, (source, target) in enumerate(tables):
        pltpu.make_async_copy(source, target, small.at[k]).start()
    for p in range(peers):
        lanes = pl.ds(p * LANES, LANES)
        pltpu.make_async_copy(tile.at[:, lanes], held.at[p], come.at[p]).start()
    for k, (source, target) in enumerate(tables):
        pltpu.make_async_copy(source, target, small.at[k]).wait()
    slots = asked.shape[1]
    matches = weight.shape[2]
    ranks = lax.broadcasted_iota(jnp.int32, (1, matches), 1)
    rows[...] = jnp.zeros_like(rows)
    for j in range(weight.shape[0]):
        masked = jnp.where(ranks < count[:, j : j + 1], weight[j], 0.0)
        share = masked / jnp.sum(masked, axis=1, keepdims=True)
        column = peer[j] * slots + slot[j]
        total = jnp.zeros_like(share)
        again = jnp.zeros_like(share)
        for k in range(matches):
            same = column == column[:, k : k + 1]
            total = total + jnp.where(same, share[:, k : k + 1], 0.0)
            again = again + jnp.where(jnp.logical_and(same, ranks > k), 1.0, 0.0)
        chosen = jnp.zeros_like(column)
        for q in range(peers):
            for k in range(slots):
                named = asked[0, k : k + 1, q : q + 1]
                chosen = chosen + jnp.where(column == q * slots + k, named, 0)
        place = peer[j] * blocks + chosen
        rows[j : j + 1, :matches] = jnp.where(again > 0.0, 0.0, total)
        at = j + weight.shape[0]
        rows[at : at + 1, :matches] = place.astype(F32)
    table[...] = rows[...].astype(BF16)
    for p in range(peers):
        pltpu.make_async_copy(table, out.at[p, pl.ds(pixels, TABLE_ROWS), :], extra.at[p]).start()
    for p in range(peers):
        lanes = pl.ds(p * LANES, LANES)
        pltpu.make_async_copy(tile.at[:, lanes], held.at[p], come.at[p]).wait()
        pltpu.make_async_copy(held.at[p], out.at[p, pl.ds(0, pixels), :], go.at[p]).start()
    for p in range(peers):
        pltpu.make_async_copy(table, out.at[p, pl.ds(pixels, TABLE_ROWS), :], extra.at[p]).wait()
        pltpu.make_async_copy(held.at[p], out.at[p, pl.ds(0, pixels), :], go.at[p]).wait()


def spread(tile, peers, peer, slot, count, weight, wanted):
    pixels, atoms = tile.shape
    inputs = (wanted.transpose(0, 2, 1), peer, slot, count.T, weight, tile)
    inputs = tuple(pltpu.with_memory_space_constraint(a, pltpu.HBM) for a in inputs)
    return pl.pallas_call(
        functools.partial(spread_kernel, weight.shape[0]),
        in_specs=[pl.BlockSpec(memory_space=pltpu.HBM)] * len(inputs),
        out_specs=pl.BlockSpec(memory_space=pltpu.HBM),
        out_shape=pltpu.HBM((peers, pixels + TABLE_ROWS, LANES), tile.dtype),
        scratch_shapes=[
            pltpu.VMEM((peers, pixels, LANES), tile.dtype),
            *(pltpu.VMEM(a.shape, a.dtype) for a in inputs[:-1]),
            pltpu.VMEM((TABLE_ROWS, LANES), F32),
            pltpu.VMEM((TABLE_ROWS, LANES), BF16),
            pltpu.SemaphoreType.DMA((len(inputs) - 1,)),
            pltpu.SemaphoreType.DMA((peers,)),
            pltpu.SemaphoreType.DMA((peers,)),
            pltpu.SemaphoreType.DMA((peers,)),
        ],
        compiler_params=pltpu.CompilerParams(vmem_limit_bytes=16 * MIB),
        cost_estimate=cost(pixels * atoms, 4 * pixels * atoms),
        name="spread",
    )(*inputs)


def inverse_kernel(lib_ref, inv_ref):
    size = lib_ref.shape[0]
    lib = lib_ref[...]
    rows = lax.broadcasted_iota(jnp.int32, (size, size), 0)
    cols = lax.broadcasted_iota(jnp.int32, (size, size), 1)
    eye = (rows == cols).astype(F32)
    gram = times_transposed(lib, lib) + MU * eye
    bound = jnp.max(jnp.sum(jnp.abs(gram), axis=1, keepdims=True))
    inv_ref[...] = eye * (2.0 / (1.0 + bound))

    def exact(a, b):
        return jnp.dot(a, b, precision=lax.Precision.HIGHEST, preferred_element_type=F32)

    def unfinished(state):
        count, worst = state
        return jnp.logical_and(count < 22, worst > 1e-4)

    def improve(state):
        count, _ = state
        x = inv_ref[...]
        rest = eye - exact(gram, x)
        inv_ref[...] = x + exact(x, rest)
        return count + 1, jnp.max(jnp.sum(jnp.abs(rest), axis=1, keepdims=True))

    lax.while_loop(unfinished, improve, (jnp.int32(0), jnp.float32(1.0)))


def gram_inverse(lib):
    size = lib.shape[0]
    return pl.pallas_call(
        inverse_kernel,
        out_shape=jax.ShapeDtypeStruct((size, size), F32),
        cost_estimate=cost(10 * 12 * size**3, 4 * size * size),
        compiler_params=pltpu.CompilerParams(vmem_limit_bytes=63 * MIB),
        name="inverse",
    )(lib)


def solve_kernel(first, *refs):
    if first:
        obs, lib, inv, thr, z, up, down, left, right, parts, primal = refs[:11]
        padded, base, low, back = refs[11:]
    else:
        obs, lib, inv, thr, z, up, down, left, right, old_parts, old_primal, mix, parts = refs[:13]
        padded, base, low, back = refs[13:]
    i = pl.program_id(0)
    peers, pixels, _ = z.shape
    row = up.shape[1]
    block = obs.shape[0]
    pixels = padded.shape[1] - 2 * row

    @pl.when(i == 0)
    def _():
        padded[:, :row] = up[...]
        padded[:, row : row + pixels] = z[:, :pixels]
        padded[:, row + pixels :] = down[...]

    at = pl.multiple_of(i * block, block)
    base[...] = jnp.dot(obs[...], lib[...], preferred_element_type=F32)
    for p in range(peers):
        lanes = slice(p * LANES, (p + 1) * LANES)
        value = base[:, lanes] + MU * padded[p, pl.ds(at + row, block), :].astype(F32)
        if not first:
            mixed = decode_fixed(mix[p])
            fresh = jnp.maximum(old_parts[:, lanes] + (GAMMA / TOTAL) * mixed, 0.0)
            value = value + MU * (fresh - old_primal[:, lanes])
        low[:, lanes] = value.astype(BF16)
    small = times_transposed(low[...], lib[...])
    solved = jnp.dot(
        small, inv[...], precision=lax.Precision.HIGHEST, preferred_element_type=F32
    )
    back[...] = jnp.dot(solved.astype(BF16), lib[...], preferred_element_type=F32)
    place = lax.broadcasted_iota(jnp.int32, (block, LANES), 0) % row
    for p in range(peers):
        lanes = slice(p * LANES, (p + 1) * LANES)
        here = padded[p, pl.ds(at + row, block), :].astype(F32)
        above = padded[p, pl.ds(at, block), :].astype(F32)
        below = padded[p, pl.ds(at + 2 * row, block), :].astype(F32)

        def edge(halo):
            return jnp.concatenate(
                [
                    jnp.broadcast_to(halo[0, k : k + 1, lanes], (row, LANES))
                    for k in range(block // row)
                ],
                axis=0,
            )

        before = jnp.where(place == 0, edge(left), pltpu.roll(here, 1, 0))
        after = jnp.where(place == row - 1, edge(right), pltpu.roll(here, block - 1, 0))
        spatial = 0.25 * (above + below + before + after)
        unmixed = (base[:, lanes] + MU * here - back[:, lanes]) / MU
        if first:
            primal[:, lanes] = unmixed
        parts[:, lanes] = (unmixed + ETA * spatial) * (1.0 / TOTAL) - thr[:, lanes]


def solve(first, obs, lib, inv, thr, z, halos, carried=()):
    peers = z.shape[0]
    pixels = obs.shape[0]
    atoms = lib.shape[1]
    up, down, left, right = halos
    row = up.shape[1]
    block = BLOCK_ROWS * row
    steps = pixels // block
    whole = lambda a: pl.BlockSpec(a.shape, lambda i, n=a.ndim: (0,) * n)
    tile = pl.BlockSpec((block, atoms), lambda i: (i, 0))
    piece = pl.BlockSpec((peers, block, LANES), lambda i: (0, i, 0))
    side = pl.BlockSpec((1, BLOCK_ROWS, atoms), lambda i: (i, 0, 0))
    full = jax.ShapeDtypeStruct((pixels, atoms), F32)
    return pl.pallas_call(
        functools.partial(solve_kernel, first),
        grid=(steps,),
        in_specs=[
            pl.BlockSpec((block, obs.shape[1]), lambda i: (i, 0)),
            whole(lib), whole(inv), whole(thr), whole(z), whole(up), whole(down), side, side,
        ]
        + ([] if first else [tile, tile, piece]),
        out_specs=[tile, tile] if first else tile,
        out_shape=[full, full] if first else full,
        scratch_shapes=[
            pltpu.VMEM((peers, pixels + 2 * row, LANES), BF16),
            pltpu.VMEM((block, atoms), F32),
            pltpu.VMEM((block, atoms), BF16),
            pltpu.VMEM((block, atoms), F32),
        ],
        cost_estimate=cost(6 * pixels * atoms * BANDS_PAD, 16 * pixels * atoms),
        compiler_params=pltpu.CompilerParams(vmem_limit_bytes=63 * MIB),
        name="solve_first" if first else "solve_second",
    )(obs, lib, inv, thr, z, up, down, left, right, *carried)


def mix_kernel(encode, matches, place_ref, weight_ref, z_ref, out_ref):
    first = pl.program_id(0) * out_ref.shape[0]
    block = out_ref.shape[1]
    per = z_ref.shape[1] // block

    def one(t, carry):
        total = None
        for k in range(matches):
            at = (first + t) * matches + k
            place = place_ref[at]
            rows = pl.ds(pl.multiple_of((place % per) * block, block), block)
            term = z_ref[place // per, rows, :].astype(F32) * weight_ref[at]
            total = term if total is None else total + term
        out_ref[t] = encode(total)
        return carry

    lax.fori_loop(0, out_ref.shape[0], one, 0)


def mix(encode, dtype, place, weight, z, matches, block):
    peers = z.shape[0]
    pixels = z.shape[1] // block * block
    blocks = peers * pixels // block
    out = pl.pallas_call(
        functools.partial(mix_kernel, encode, matches),
        grid=(blocks // GROUP,),
        in_specs=[
            pl.BlockSpec(memory_space=pltpu.SMEM),
            pl.BlockSpec(memory_space=pltpu.SMEM),
            pl.BlockSpec(memory_space=pltpu.VMEM),
        ],
        out_specs=pl.BlockSpec((GROUP, block, LANES), lambda i: (i, 0, 0)),
        out_shape=pltpu.HBM((blocks, block, LANES), dtype),
        cost_estimate=cost(2 * matches * blocks * block * LANES, 4 * blocks * block * LANES),
        compiler_params=pltpu.CompilerParams(vmem_limit_bytes=48 * MIB),
        name="mix",
    )(place, weight, z)
    return out.reshape(peers, pixels, LANES)


def fresh_kernel(parts, mixed, out, held, code, made, come, came, go):
    step = parts.shape[0] // STEPS
    reads, writes = [], []
    for i in range(STEPS):
        at = pl.ds(i * step, step)
        reads.append(
            (
                pltpu.make_async_copy(parts.at[at, :], held.at[at, :], come.at[i]),
                pltpu.make_async_copy(mixed.at[:, at, :], code.at[:, at, :], came.at[i]),
            )
        )
        writes.append(pltpu.make_async_copy(made.at[:, at, :], out.at[:, at, :], go.at[i]))
    for pair in reads:
        for copy in pair:
            copy.start()
    for i in range(STEPS):
        for copy in reads[i]:
            copy.wait()
        at = pl.ds(i * step, step)
        for p in range(out.shape[0]):
            lanes = slice(p * LANES, (p + 1) * LANES)
            value = held[at, lanes] + (GAMMA / TOTAL) * decode_fixed(code[p, at, :])
            made[p, at, :] = jnp.maximum(value, 0.0).astype(BF16)
        writes[i].start()
    for copy in writes:
        copy.wait()


def fresh_pieces(parts, mixed):
    peers, pixels, _ = mixed.shape
    atoms = parts.shape[1]
    hbm = pl.BlockSpec(memory_space=pltpu.HBM)
    return pl.pallas_call(
        fresh_kernel,
        in_specs=[hbm, hbm],
        out_specs=hbm,
        out_shape=pltpu.HBM((peers, pixels, LANES), BF16),
        scratch_shapes=[
            pltpu.VMEM((pixels, atoms), F32),
            pltpu.VMEM((peers, pixels, LANES), mixed.dtype),
            pltpu.VMEM((peers, pixels, LANES), BF16),
            pltpu.SemaphoreType.DMA((STEPS,)),
            pltpu.SemaphoreType.DMA((STEPS,)),
            pltpu.SemaphoreType.DMA((STEPS,)),
        ],
        compiler_params=pltpu.CompilerParams(vmem_limit_bytes=63 * MIB),
        cost_estimate=cost(4 * pixels * atoms, 8 * pixels * atoms),
        name="fresh",
    )(parts, mixed)


def final_kernel(
    parts, mixed, obs, turned, out, misfit,
    held, code, made, rest, seen, spectra, come, came, go, went, side,
):
    step = parts.shape[0] // STEPS
    wide = WIDE * step
    reads, writes = [], []
    for i in range(STEPS):
        at = pl.ds(i * step, step)
        reads.append(
            (
                pltpu.make_async_copy(parts.at[at, :], held.at[at, :], come.at[i]),
                pltpu.make_async_copy(mixed.at[:, at, :], code.at[:, at, :], came.at[i]),
            )
        )
        writes.append(pltpu.make_async_copy(made.at[at, :], out.at[at, :], go.at[i]))
    others = (
        pltpu.make_async_copy(turned, spectra, side.at[0]),
        pltpu.make_async_copy(obs, seen, side.at[1]),
    )
    for i, pair in enumerate(reads):
        for copy in pair:
            copy.start()
        if i == 0:
            for copy in others:
                copy.start()
    for i in range(STEPS):
        for copy in reads[i]:
            copy.wait()
        at = pl.ds(i * step, step)
        for p in range(mixed.shape[0]):
            lanes = slice(p * LANES, (p + 1) * LANES)
            value = held[at, lanes] + (GAMMA / TOTAL) * decode_float(code[p, at, :])
            made[at, lanes] = jnp.maximum(value, 0.0).astype(BF16)
        writes[i].start()
        if i == 0:
            for copy in others:
                copy.wait()
        if (i + 1) % WIDE == 0:
            k = i // WIDE
            rows = pl.ds(k * wide, wide)
            rebuilt = jnp.dot(made[rows, :], spectra[...], preferred_element_type=F32)
            rest[rows, :] = (seen[rows, :].astype(F32) - rebuilt)[:, : rest.shape[1]]
            writes.append(
                pltpu.make_async_copy(rest.at[rows, :], misfit.at[rows, :], went.at[k])
            )
            writes[-1].start()
    for copy in writes:
        copy.wait()


def final(parts, mixed, obs, turned, bands):
    peers, pixels, _ = mixed.shape
    atoms = parts.shape[1]
    hbm = pl.BlockSpec(memory_space=pltpu.HBM)
    return pl.pallas_call(
        final_kernel,
        in_specs=[hbm, hbm, hbm, hbm],
        out_specs=[hbm, hbm],
        out_shape=[pltpu.HBM((pixels, atoms), BF16), pltpu.HBM((pixels, bands), F32)],
        scratch_shapes=[
            pltpu.VMEM((pixels, atoms), F32),
            pltpu.VMEM((peers, pixels, LANES), mixed.dtype),
            pltpu.VMEM((pixels, atoms), BF16),
            pltpu.VMEM((pixels, bands), F32),
            pltpu.VMEM(obs.shape, obs.dtype),
            pltpu.VMEM(turned.shape, turned.dtype),
            pltpu.SemaphoreType.DMA((STEPS,)),
            pltpu.SemaphoreType.DMA((STEPS,)),
            pltpu.SemaphoreType.DMA((STEPS,)),
            pltpu.SemaphoreType.DMA((STEPS // WIDE,)),
            pltpu.SemaphoreType.DMA((2,)),
        ],
        compiler_params=pltpu.CompilerParams(vmem_limit_bytes=63 * MIB),
        cost_estimate=cost(2 * pixels * atoms * BANDS_PAD, 8 * pixels * atoms),
        name="final",
    )(parts, mixed, obs, turned)


def shifted(array, axis, up):
    peers = lax.axis_size(axis)
    pairs = [(k, k + 1) for k in range(peers - 1)]
    return lax.ppermute(array, axis, pairs if up else [(b, a) for a, b in pairs])


def exchanged(pieces):
    return lax.all_to_all(pieces, "col", 0, 0, tiled=True)


def shifted_edges(pieces, tile_rows, tile_cols):
    peers = pieces.shape[0]
    pixels = tile_rows * tile_cols
    sides = pieces[:, :pixels].reshape(peers, tile_rows, tile_cols, LANES)
    up = shifted(pieces[:, pixels - tile_cols : pixels], "row", True)
    down = shifted(pieces[:, :tile_cols], "row", False)
    left = shifted(sides[:, :, -1], "col", True)
    right = shifted(sides[:, :, 0], "col", False)

    def side_rows(column):
        rows = jnp.moveaxis(column.astype(F32), 0, 1)
        return rows.reshape(tile_rows // BLOCK_ROWS, BLOCK_ROWS, -1)

    return up, down, side_rows(left), side_rows(right)


def local(
    observed, library, warm, match_peer, match_slot, match_count, match_weight, wanted, threshold
):
    tile_rows, tile_cols, atoms = warm.shape
    bands = library.shape[0]
    pixels = tile_rows * tile_cols
    blocks = tile_rows // BLOCK_ROWS
    block = BLOCK_ROWS * tile_cols
    peers = lax.axis_size("col")
    matches = match_weight.shape[2]

    pieces = spread(
        warm.reshape(pixels, atoms), peers,
        match_peer, match_slot, match_count, match_weight, wanted,
    )
    strip = exchanged(pieces)
    halos = shifted_edges(pieces, tile_rows, tile_cols)
    lib = jnp.pad(library, ((0, BANDS_PAD - bands), (0, 0)))
    obs = jnp.pad(observed.reshape(pixels, bands), ((0, 0), (0, BANDS_PAD - bands)))
    inv = gram_inverse(lib)
    thr = threshold[None, :]

    tables = strip[:, pixels : pixels + 2 * blocks, :matches].astype(F32)
    weight = tables[:, :blocks].reshape(-1)
    place = tables[:, blocks:].astype(jnp.int32).reshape(-1)
    sums = mix(encode_fixed, jnp.int16, place, weight, strip, matches, block)
    mixed = exchanged(sums)
    parts, primal = solve(True, obs, lib, inv, thr, pieces, halos)
    pieces = fresh_pieces(parts, mixed)
    strip = exchanged(pieces)
    halos = shifted_edges(pieces, tile_rows, tile_cols)
    sums = mix(encode_float, BF16, place, weight, strip, matches, block)
    mixed_again = exchanged(sums)
    parts = solve(False, obs, lib, inv, thr, pieces, halos, (parts, primal, mixed))
    abundance, misfit = final(parts, mixed_again, obs, lib.T, bands)
    return (
        abundance.reshape(tile_rows, tile_cols, atoms),
        misfit.reshape(tile_rows, tile_cols, bands),
    )


def solution(mesh):
    return jax.shard_map(
        local,
        mesh=mesh,
        in_specs=(
            P("row", "col", None),
            P(),
            P("row", "col", None),
            P("row", "col", None),
            P("row", "col", None),
            P("row", "col"),
            P("row", "col", None),
            P("row", "col", None),
            P(),
        ),
        out_specs=(P("row", "col", None), P("row", "col", None)),
        check_vma=False,
    )
```

time: 237 us -> 193 us (0.81)
  local copies, waits for them, and re-layouts: 40.9 us -> 13.7 us
  Pallas kernels: 43.7 us -> 59.6 us
  starting transfers between devices: 46.7 us -> 32.5 us
  blocking collectives: 80.5 us -> 70.4 us
  waiting for transfers between devices: 18.8 us -> 14.2 us
  other arithmetic: 3.33 us -> 0.06 us
    unnamed x1 -> x0, blocking collectives: 48.7 us -> none
    all_to_all x1 -> x2, blocking collectives: 31.8 us -> 70.4 us  [exchanged(): return lax.all_to_all(pieces, 'col', 0, 0, tiled=True)]
    unnamed x59 -> x22, local copies, waits for them, and re-layouts: 30 us -> 3.55 us
    all_to_all x3 -> x2, starting transfers between devices: 23.7 us -> 11.3 us  [exchanged(): return lax.all_to_all(pieces, 'col', 0, 0, tiled=True)]
    pallas_call x5, Pallas kernels: 18.4 us -> 27.5 us  [the longest x2 13.2 us: mix(): pl.pallas_call(functools.partial(mix_kernel, encode, matches), grid=(bloc...]
    pallas_call x2, Pallas kernels: 17.9 us -> 22.8 us  [solve(): pl.pallas_call(functools.partial(solve_kernel, first), grid=(steps,), in_...]
    ppermute x8, waiting for transfers between devices: 18.7 us -> 14.2 us  [shifted(): lax.ppermute(array, axis, pairs if up else [(b, a) for a, b in pairs])]
    convert_element_type x2 -> x0, local copies, waits for them, and re-layouts: 2.54 us -> none  [side_rows(): return column.astype(F32).reshape(blocks, -1, atoms)]
  transfers between devices with their start and end apart: 11 -> 10, of which waited for: 1 -> 2; matrix products, arithmetic and copies ran while one was open for 7% -> 5% of each run, Pallas kernels for 11% -> 17%
where the time goes in v1:
time: 193 us; the launch traced here: 192 us
  blocking collectives  70.4 us (36%)
  Pallas kernels  59.6 us (31%)
  starting transfers between devices  32.5 us (17%)
  waiting for transfers between devices  14.2 us (7%)
  local copies, waits for them, and re-layouts  13.7 us (7%)
    all_to_all x2, blocking collectives, exchanged(): return lax.all_to_all(pieces, 'col', 0, 0, tiled=True)  70.4 us
    pallas_call x2, Pallas kernels, solve(): pl.pallas_call(functools.partial(solve_kernel, first), grid=(steps,), in_...  22.8 us
    ppermute x8, starting transfers between devices, shifted(): lax.ppermute(array, axis, pairs if up else [(b, a) for a, b in pairs])  21.3 us
    ppermute x8, waiting for transfers between devices, shifted(): lax.ppermute(array, axis, pairs if up else [(b, a) for a, b in pairs])  14.2 us
    pallas_call x2, Pallas kernels, mix(): pl.pallas_call(functools.partial(mix_kernel, encode, matches), grid=(bloc...  13.2 us
    all_to_all x2, starting transfers between devices, exchanged(): return lax.all_to_all(pieces, 'col', 0, 0, tiled=True)  11.3 us
    pallas_call x1, Pallas kernels, gram_inverse(): pl.pallas_call(inverse_kernel, out_shape=jax.ShapeDtypeStruct((size, size...  9.29 us
    pallas_call x1, Pallas kernels, final(): pl.pallas_call(final_kernel, in_specs=[hbm, hbm, hbm, hbm], out_specs=[hb...  5.9 us
  transfers between devices with their start and end apart: 10, of which 2 were waited for; matrix products, arithmetic and copies ran while one was open for 5% of the time, Pallas kernels for 17%

profile of v1, /device:TPU:2, one launch (start us, length us, event | category | flops | bytes accessed | tf_op | source)
XLA Modules:
  0.0 191.5 jit_solution(12233495062320030385)
XLA Ops:
  0.6 4.0 %spread.1.refs_4_ = bf16[16,528,128]{2,1,0:T(8,128)(2,1)} custom-call(s32[1,2,16]{2,1,0:T(2,128)} %bitcast.45, s32[4,1,8]{2,1,0:T(1,128)} %peer_at.1, s32[4,1,8]{2,1,0:T(1,128)} %slot_at.1, s32[1,4]{1,0:T(1,128)} %bitcast.46, f32[4,1,8]{2,1,0:T(1,128)} %weight_at.1, bf16[512,2048]{1,0:T(8,128)(2,1)} %bitcast.37), custom_call_target="tpu_custom_call" | custom-call | flops 1048576 | bytes 4194304 | tf_op jit(solution)/shard_map/spread/pallas_call | solution.py:110
  4.7 36.3 %all_to_all.20.z_ref = bf16[16,528,128]{2,1,0:T(8,128)(2,1)S(1)} all-to-all(bf16[16,528,128]{2,1,0:T(8,128)(2,1)} %spread.1.refs_4_), channel_id=1, replica_groups=mesh['row'=8,'col'=16] {'col'}, dimensions={0} | all-to-all | bytes 4325376 | tf_op jit(solution)/shard_map/all_to_all | solution.py:440
  41.0 0.1 reshape.61.place_ref
  41.1 0.1 reshape.62.weight_ref
  41.2 6.8 %mix.2 = s16[64,128,128]{2,1,0:T(8,128)(2,1)} custom-call(s32[512]{0:T(512)S(1)} %reshape.61.place_ref, f32[512]{0:T(512)S(1)} %reshape.62.weight_ref, bf16[16,528,128]{2,1,0:T(8,128)(2,1)S(1)} %all_to_all.20.z_ref), custom_call_target="tpu_custom_call" | custom-call | flops 16777216 | bytes 4194304 | tf_op jit(solution)/shard_map/mix/pallas_call | solution.py:286
  48.0 5.7 %all-to-all-start.1 = ((s16[16,512,128]{2,1,0:T(8,128)(2,1)}), s16[16,512,128]{2,1,0:T(8,128)(2,1)}, u32[]{:S(2)}, u32[]{:S(2)}) async-start(s16[16,512,128]{2,1,0:T(8,128)(2,1)} %bitcast.35), calls=%async_computation.1 | async-start | bytes 4194304 | tf_op jit(solution)/shard_map/all_to_all | solution.py:440
  53.7 0.0 slice-start
  53.7 0.0 copy-start
  53.7 0.0 copy-start.3
  53.7 1.6 slice-done
  55.2 0.2 fusion.3
  55.5 3.4 %collective-permute-start.2 = (bf16[16,16,128]{2,0,1:T(8,128)(2,1)S(1)}, bf16[16,16,128]{2,0,1:T(8,128)(2,1)S(1)}, u32[]{:S(2)}, u32[]{:S(2)}) collective-permute-start(bf16[16,16,128]{2,0,1:T(8,128)(2,1)S(1)} %bitcast.40), channel_id=1, source_target_pairs={{0,1},{1,2},{2,3},{3,4},{4,5},{5,6},{6,7},{7,8},{8,9},{9,10},{10,1... | collective-permute-start | bytes 196616 | tf_op jit(solution)/shard_map/ppermute | solution.py:436
  59.0 4.6 %collective-permute-start.3 = (bf16[16,16,128]{2,0,1:T(8,128)(2,1)S(1)}, bf16[16,16,128]{2,0,1:T(8,128)(2,1)S(1)}, u32[]{:S(2)}, u32[]{:S(2)}) collective-permute-start(bf16[16,16,128]{2,0,1:T(8,128)(2,1)S(1)} %bitcast.39), channel_id=1, source_target_pairs={{1,0},{2,1},{3,2},{4,3},{5,4},{6,5},{7,6},{8,7},{9,8},{10,9},{11,1... | collective-permute-start | bytes 196616 | tf_op jit(solution)/shard_map/ppermute | solution.py:436
  63.5 0.0 copy-done
  63.6 1.3 collective-permute-start
  64.9 1.3 collective-permute-start.1
  66.2 0.0 copy-done.3
  66.2 0.5 copy.19
  66.7 0.0 copy-start.1
  66.7 1.0 copy-done.1
  67.7 0.5 copy.35
  68.2 1.1 pad.9.clone.lib_ref.refs_1_
  69.3 0.0 copy-start.4
  69.3 9.3 %inverse.1.refs_2_ = f32[256,256]{1,0:T(8,128)} custom-call(bf16[256,2048]{1,0:T(8,128)(2,1)} %pad.9.clone.lib_ref.refs_1_), custom_call_target="tpu_custom_call" | custom-call | flops 2013265920 | bytes 262144 | tf_op jit(solution)/shard_map/inverse/pallas_call | solution.py:160
  78.6 0.0 copy-done.4
  78.6 0.7 pad.8.refs_0_.obs
  79.3 0.8 collective-permute-done.2
  80.2 0.7 reshape.73.refs_7_
  80.9 0.0 collective-permute-done.3
  80.9 0.7 reshape.75.refs_8_
  81.6 0.0 collective-permute-done.refs_5_
  81.6 0.0 copy-start.7
  81.6 0.0 collective-permute-done.1.refs_6_
  81.6 0.6 copy-done.7
  82.3 11.0 %solve_first.1 = (f32[512,2048]{1,0:T(8,128)}, f32[512,2048]{1,0:T(8,128)}) custom-call(bf16[512,256]{1,0:T(8,128)(2,1)} %pad.8.refs_0_.obs, bf16[256,2048]{1,0:T(8,128)(2,1)} %pad.9.clone.lib_ref.refs_1_, f32[256,256]{1,0:T(8,128)} %inverse.1.refs_2_, f32[1,2048]{1,0:T(1,128)} %bitcast.43, bf16[16,528,128]{2,1,0:T(8,128)(2,1)} %spread.1.refs_4_, ...), custom_call_target="tpu_custom_call" | custom-call | flops 1610612736 | bytes 16777216 | tf_op jit(solution)/shard_map/solve_first/pallas_call | solution.py:241
  93.2 0.0 all-to-all-done.1.mixed.refs_11_
  93.3 4.3 %fresh.1.refs_4_ = bf16[16,512,128]{2,1,0:T(8,128)(2,1)} custom-call(f32[512,2048]{1,0:T(8,128)} %get-tuple-element.6.parts.refs_9_, s16[16,512,128]{2,1,0:T(8,128)(2,1)} %all-to-all-done.1.mixed.refs_11_), custom_call_target="tpu_custom_call" | custom-call | flops 4194304 | bytes 8388608 | tf_op jit(solution)/shard_map/fresh/pallas_call | solution.py:335
  97.5 34.1 %all_to_all.21.z_ref = bf16[16,512,128]{2,1,0:T(8,128)(2,1)S(1)} all-to-all(bf16[16,512,128]{2,1,0:T(8,128)(2,1)} %fresh.1.refs_4_), channel_id=1, replica_groups=mesh['row'=8,'col'=16] {'col'}, dimensions={0} | all-to-all | bytes 4194304 | tf_op jit(solution)/shard_map/all_to_all | solution.py:440
  131.6 6.5 %mix.3 = bf16[64,128,128]{2,1,0:T(8,128)(2,1)} custom-call(s32[512]{0:T(512)S(1)} %reshape.61.place_ref, f32[512]{0:T(512)S(1)} %reshape.62.weight_ref, bf16[16,512,128]{2,1,0:T(8,128)(2,1)S(1)} %all_to_all.21.z_ref), custom_call_target="tpu_custom_call" | custom-call | flops 16777216 | bytes 4194304 | tf_op jit(solution)/shard_map/mix/pallas_call | solution.py:286
  138.1 0.0 copy-start.2
  138.1 5.6 %all-to-all-start.3 = ((bf16[16,512,128]{2,1,0:T(8,128)(2,1)}), bf16[16,512,128]{2,1,0:T(8,128)(2,1)}, u32[]{:S(2)}, u32[]{:S(2)}) async-start(bf16[16,512,128]{2,1,0:T(8,128)(2,1)} %bitcast.36), calls=%async_computation.3 | async-start | bytes 4194304 | tf_op jit(solution)/shard_map/all_to_all | solution.py:440
  143.7 0.0 copy-done.2
  143.7 1.1 pad_bitcast_fusion.turned
  144.9 1.4 fusion.1
  146.3 3.4 %collective-permute-start.6 = (bf16[16,16,128]{2,0,1:T(8,128)(2,1)S(1)}, bf16[16,16,128]{2,0,1:T(8,128)(2,1)S(1)}, u32[]{:S(2)}, u32[]{:S(2)}) collective-permute-start(bf16[16,16,128]{2,0,1:T(8,128)(2,1)S(1)} %bitcast.41), channel_id=1, source_target_pairs={{0,1},{1,2},{2,3},{3,4},{4,5},{5,6},{6,7},{7,8},{8,9},{9,10},{10,1... | collective-permute-start | bytes 196616 | tf_op jit(solution)/shard_map/ppermute | solution.py:436
  149.7 1.0 fusion.2
  150.8 4.6 %collective-permute-start.7 = (bf16[16,16,128]{2,0,1:T(8,128)(2,1)S(1)}, bf16[16,16,128]{2,0,1:T(8,128)(2,1)S(1)}, u32[]{:S(2)}, u32[]{:S(2)}) collective-permute-start(bf16[16,16,128]{2,0,1:T(8,128)(2,1)S(1)} %bitcast.42), channel_id=1, source_target_pairs={{1,0},{2,1},{3,2},{4,3},{5,4},{6,5},{7,6},{8,7},{9,8},{10,9},{11,1... | collective-permute-start | bytes 196616 | tf_op jit(solution)/shard_map/ppermute | solution.py:436
  155.4 1.3 collective-permute-start.4
  156.7 1.5 collective-permute-start.5
  158.2 13.3 %collective-permute-done.6 = bf16[16,16,128]{2,0,1:T(8,128)(2,1)S(1)} collective-permute-done((bf16[16,16,128]{2,0,1:T(8,128)(2,1)S(1)}, bf16[16,16,128]{2,0,1:T(8,128)(2,1)S(1)}, u32[]{:S(2)}, u32[]{:S(2)}) %collective-permute-start.6) | collective-permute-done | bytes 65568 | tf_op jit(solution)/shard_map/ppermute | solution.py:436
  171.5 0.7 reshape.77.refs_7_
  172.2 0.0 collective-permute-done.7
  172.2 0.7 reshape.79.refs_8_
  172.9 0.0 collective-permute-done.4.refs_5_
  172.9 0.0 copy-start.5
  172.9 0.0 collective-permute-done.5.refs_6_
  172.9 0.0 copy-start.6
  172.9 0.7 copy-done.5
  173.6 0.1 copy-done.6
  173.6 11.8 %solve_second.1.parts = f32[512,2048]{1,0:T(8,128)} custom-call(bf16[512,256]{1,0:T(8,128)(2,1)} %pad.8.refs_0_.obs, bf16[256,2048]{1,0:T(8,128)(2,1)} %pad.9.clone.lib_ref.refs_1_, f32[256,256]{1,0:T(8,128)} %inverse.1.refs_2_, f32[1,2048]{1,0:T(1,128)} %bitcast.44, bf16[16,512,128]{2,1,0:T(8,128)(2,1)} %fresh.1.refs_4_, bf16[16,32,128]{2,1,0:T(8,128)(2,1)} %copy-done.5, ...), custom_call_target="tpu_custom_call" | custom-call | flops 1610612736 | bytes 16777216 | tf_op jit(solution)/shard_map/solve_second/pallas_call | solution.py:241
  185.4 0.0 all-to-all-done.3.mixed
  185.5 5.9 %final.1 = (bf16[512,2048]{1,0:T(8,128)(2,1)}, f32[512,188]{1,0:T(8,128)}) custom-call(f32[512,2048]{1,0:T(8,128)} %solve_second.1.parts, bf16[16,512,128]{2,1,0:T(8,128)(2,1)} %all-to-all-done.3.mixed, bf16[512,256]{1,0:T(8,128)(2,1)} %pad.8.refs_0_.obs, bf16[2048,256]{1,0:T(8,128)(2,1)} %pad_bitcast_fusion.turned), custom_call_target="tpu_custom_call" | custom-call | flops 536870912 | bytes 8388608 | tf_op jit(solution)/shard_map/final/pallas_call | solution.py:409
  (11 shorter events, 0.3 us)
Async XLA Ops:
  48.0 45.3 %all-to-all-start.1 = ((s16[16,512,128]{2,1,0:T(8,128)(2,1)}), s16[16,512,128]{2,1,0:T(8,128)(2,1)}, u32[]{:S(2)}, u32[]{:S(2)}) async-start(s16[16,512,128]{2,1,0:T(8,128)(2,1)} %bitcast.35), calls=%async_computation.1 | async-start | bytes 4194304 | tf_op jit(solution)/shard_map/all_to_all | solution.py:440
  53.7 1.6 slice-start
  53.7 9.9 %copy-start = (bf16[16,528,128]{2,1,0:T(8,128)(2,1)S(1)}, bf16[16,528,128]{2,1,0:T(8,128)(2,1)}, u32[]{:S(2)}) copy-start(bf16[16,528,128]{2,1,0:T(8,128)(2,1)} %spread.1.refs_4_) | copy-start | bytes 6488068
  53.7 12.5 %copy-start.3 = (bf16[188,2048]{1,0:T(8,128)(2,1)S(1)}, bf16[188,2048]{1,0:T(8,128)(2,1)}, u32[]{:S(2)}) copy-start(bf16[188,2048]{1,0:T(8,128)(2,1)} %param.10) | copy-start | bytes 2310148
  55.5 24.7 %collective-permute-start.2 = (bf16[16,16,128]{2,0,1:T(8,128)(2,1)S(1)}, bf16[16,16,128]{2,0,1:T(8,128)(2,1)S(1)}, u32[]{:S(2)}, u32[]{:S(2)}) collective-permute-start(bf16[16,16,128]{2,0,1:T(8,128)(2,1)S(1)} %bitcast.40), channel_id=1, source_target_pairs={{0,1},{1,2},{2,3},{3,4},{4,5},{5,6},{6,7},{7,8},{8,9},{9,10},{10,1... | collective-permute-start | bytes 196616 | tf_op jit(solution)/shard_map/ppermute | solution.py:436
  59.0 21.9 %collective-permute-start.3 = (bf16[16,16,128]{2,0,1:T(8,128)(2,1)S(1)}, bf16[16,16,128]{2,0,1:T(8,128)(2,1)S(1)}, u32[]{:S(2)}, u32[]{:S(2)}) collective-permute-start(bf16[16,16,128]{2,0,1:T(8,128)(2,1)S(1)} %bitcast.39), channel_id=1, source_target_pairs={{1,0},{2,1},{3,2},{4,3},{5,4},{6,5},{7,6},{8,7},{9,8},{10,9},{11,1... | collective-permute-start | bytes 196616 | tf_op jit(solution)/shard_map/ppermute | solution.py:436
  63.6 18.0 %collective-permute-start = (bf16[16,32,128]{2,1,0:T(8,128)(2,1)S(1)}, bf16[16,32,128]{2,1,0:T(8,128)(2,1)S(1)}, u32[]{:S(2)}, u32[]{:S(2)}) collective-permute-start(bf16[16,32,128]{2,1,0:T(8,128)(2,1)S(1)} %get-tuple-element.11), channel_id=1, source_target_pairs={{0,16},{16,32},{32,48},{48,64},{64,80},{80,96},{96,112},{1,17},{17... | collective-permute-start | bytes 393224 | tf_op jit(solution)/shard_map/ppermute | solution.py:436
  64.9 16.7 %collective-permute-start.1 = (bf16[16,32,128]{2,1,0:T(8,128)(2,1)S(1)}, bf16[16,32,128]{2,1,0:T(8,128)(2,1)}, u32[]{:S(2)}, u32[]{:S(2)}) collective-permute-start(bf16[16,32,128]{2,1,0:T(8,128)(2,1)S(1)} %get-tuple-element.10), channel_id=1, source_target_pairs={{16,0},{32,16},{48,32},{64,48},{80,64},{96,80},{112,96},{17,1},{33... | collective-permute-start | bytes 393224 | tf_op jit(solution)/shard_map/ppermute | solution.py:436
  66.7 1.0 copy-start.1
  69.3 9.3 %copy-start.4 = (bf16[16,32,188]{2,1,0:T(8,128)(2,1)S(1)}, bf16[16,32,188]{2,1,0:T(8,128)(2,1)}, u32[]{:S(2)}) copy-start(bf16[16,32,188]{2,1,0:T(8,128)(2,1)} %param.9) | copy-start | bytes 577540
  81.6 0.7 copy-start.7
  138.1 5.6 %copy-start.2 = (bf16[188,2048]{0,1:T(8,128)(2,1)S(1)}, bf16[188,2048]{0,1:T(8,128)(2,1)}, u32[]{:S(2)}) copy-start(bf16[188,2048]{0,1:T(8,128)(2,1)} %copy-done.1) | copy-start | bytes 2310148
  138.1 47.4 %all-to-all-start.3 = ((bf16[16,512,128]{2,1,0:T(8,128)(2,1)}), bf16[16,512,128]{2,1,0:T(8,128)(2,1)}, u32[]{:S(2)}, u32[]{:S(2)}) async-start(bf16[16,512,128]{2,1,0:T(8,128)(2,1)} %bitcast.36), calls=%async_computation.3 | async-start | bytes 4194304 | tf_op jit(solution)/shard_map/all_to_all | solution.py:440
  146.3 25.1 %collective-permute-start.6 = (bf16[16,16,128]{2,0,1:T(8,128)(2,1)S(1)}, bf16[16,16,128]{2,0,1:T(8,128)(2,1)S(1)}, u32[]{:S(2)}, u32[]{:S(2)}) collective-permute-start(bf16[16,16,128]{2,0,1:T(8,128)(2,1)S(1)} %bitcast.41), channel_id=1, source_target_pairs={{0,1},{1,2},{2,3},{3,4},{4,5},{5,6},{6,7},{7,8},{8,9},{9,10},{10,1... | collective-permute-start | bytes 196616 | tf_op jit(solution)/shard_map/ppermute | solution.py:436
  150.8 21.4 %collective-permute-start.7 = (bf16[16,16,128]{2,0,1:T(8,128)(2,1)S(1)}, bf16[16,16,128]{2,0,1:T(8,128)(2,1)S(1)}, u32[]{:S(2)}, u32[]{:S(2)}) collective-permute-start(bf16[16,16,128]{2,0,1:T(8,128)(2,1)S(1)} %bitcast.42), channel_id=1, source_target_pairs={{1,0},{2,1},{3,2},{4,3},{5,4},{6,5},{7,6},{8,7},{9,8},{10,9},{11,1... | collective-permute-start | bytes 196616 | tf_op jit(solution)/shard_map/ppermute | solution.py:436
  155.4 17.5 %collective-permute-start.4 = (bf16[16,32,128]{2,1,0:T(8,128)(2,1)S(1)}, bf16[16,32,128]{2,1,0:T(8,128)(2,1)S(1)}, u32[]{:S(2)}, u32[]{:S(2)}) collective-permute-start(bf16[16,32,128]{2,1,0:T(8,128)(2,1)S(1)} %get-tuple-element.15), channel_id=1, source_target_pairs={{0,16},{16,32},{32,48},{48,64},{64,80},{80,96},{96,112},{1,17},{17... | collective-permute-start | bytes 393224 | tf_op jit(solution)/shard_map/ppermute | solution.py:436
  156.7 16.2 %collective-permute-start.5 = (bf16[16,32,128]{2,1,0:T(8,128)(2,1)S(1)}, bf16[16,32,128]{2,1,0:T(8,128)(2,1)S(1)}, u32[]{:S(2)}, u32[]{:S(2)}) collective-permute-start(bf16[16,32,128]{2,1,0:T(8,128)(2,1)S(1)} %get-tuple-element.14), channel_id=1, source_target_pairs={{16,0},{32,16},{48,32},{64,48},{80,64},{96,80},{112,96},{17,1},{33... | collective-permute-start | bytes 393224 | tf_op jit(solution)/shard_map/ppermute | solution.py:436
  172.9 0.7 copy-start.5
  172.9 0.7 copy-start.6

commit v2 on v1

v2 whole, which is shorter than its diff:
```python
import functools

import jax
import jax.numpy as jnp
from jax import lax
from jax.experimental import pallas as pl
from jax.experimental.pallas import tpu as pltpu
from jax.sharding import PartitionSpec as P


BLOCK_ROWS = 4
BLOCKS = 4
MU = 1.0
GAMMA = 0.6
ETA = 0.3
TOTAL = 1.0 + GAMMA + ETA
LANES = 128
BANDS_PAD = 192
CODE_SCALE = 64000.0
CODE_SHIFT = 32768.0
STEPS = 8
AHEAD = 5
WIDE = 2
TABLE_ROWS = 16
MIB = 1024 * 1024

F32 = jnp.float32
BF16 = jnp.bfloat16


def cost(flops, moved):
    return pl.CostEstimate(flops=flops, bytes_accessed=moved, transcendentals=0)


def times_transposed(left, right):
    return lax.dot_general(
        left, right, (((1,), (1,)), ((), ())), preferred_element_type=F32
    )


def encode_fixed(value):
    return jnp.round(value * CODE_SCALE - CODE_SHIFT).astype(jnp.int32).astype(jnp.int16)


def decode_fixed(code):
    return (code.astype(jnp.int32).astype(F32) + CODE_SHIFT) * (1.0 / CODE_SCALE)


def encode_float(value):
    return value.astype(BF16)


def decode_float(code):
    return code.astype(F32)


def swapped(a, b):
    low = lax.broadcasted_iota(jnp.int32, a.shape, 1) < 4
    first = jnp.where(low, a, pltpu.roll(b, 4, 1))
    second = jnp.where(low, pltpu.roll(a, 4, 1), b)
    return first, second


def weave(parts):
    f0, s0 = swapped(parts[0], parts[1])
    f1, s1 = swapped(parts[2], parts[3])
    tiles = [t[v] for v in range(f0.shape[0]) for t in (f0, f1, s0, s1)]
    return jnp.concatenate(tiles, axis=0)


def unweave(rows):
    tiles = rows.reshape(-1, 4, 8, LANES)
    b0, b1 = swapped(tiles[:, 0], tiles[:, 2])
    b2, b3 = swapped(tiles[:, 1], tiles[:, 3])
    return b0, b1, b2, b3


def halves(rows):
    return rows.reshape(-1, 8, LANES)


def spread_kernel(
    asked_at, peer_at, slot_at, count_at, weight_at, tile, out,
    held, made, asked, peer, slot, count, weight, rows, table, small, come, go, extra,
):
    blocks, block, _ = held.shape
    peers = made.shape[0]
    pixels = blocks * block
    step = block // STEPS
    for i in range(STEPS):
        at = pl.ds(i * step, step)
        pltpu.make_async_copy(tile.at[:, at, :], held.at[:, at, :], come.at[i]).start()
    tables = (
        (asked_at, asked), (peer_at, peer), (slot_at, slot), (count_at, count), (weight_at, weight),
    )
    for k, (source, target) in enumerate(tables):
        pltpu.make_async_copy(source, target, small.at[k]).start()
    for k, (source, target) in enumerate(tables):
        pltpu.make_async_copy(source, target, small.at[k]).wait()
    slots = asked.shape[1]
    matches = weight.shape[2]
    stacked = lambda ref: jnp.concatenate([ref[j] for j in range(blocks)], axis=0)
    peer, slot, weight = stacked(peer), stacked(slot), stacked(weight)
    live = jnp.concatenate([count[:, j : j + 1] for j in range(blocks)], axis=0)
    ranks = lax.broadcasted_iota(jnp.int32, (blocks, matches), 1)
    spots = lax.broadcasted_iota(jnp.int32, (blocks, LANES), 1)
    masked = jnp.where(ranks < live, weight, 0.0)
    share = masked / jnp.sum(masked, axis=1, keepdims=True)
    column = peer * slots + slot
    total = jnp.zeros_like(share)
    again = jnp.zeros_like(share)
    for k in range(matches):
        same = column == column[:, k : k + 1]
        total = total + jnp.where(same, share[:, k : k + 1], 0.0)
        again = again + jnp.where(jnp.logical_and(same, ranks > k), 1.0, 0.0)
    coef = jnp.where(again > 0.0, 0.0, total.astype(BF16).astype(F32))
    chosen = jnp.zeros_like(column)
    for q in range(peers):
        for k in range(slots):
            named = asked[0, k : k + 1, q : q + 1]
            chosen = chosen + jnp.where(column == q * slots + k, named, 0)
    place = peer * blocks + chosen
    line = jnp.zeros((blocks, LANES), F32)
    for k in range(matches):
        line = line + jnp.where(spots == place[:, k : k + 1], coef[:, k : k + 1], 0.0)
    high = line.astype(BF16).astype(F32)
    rows[...] = jnp.zeros_like(rows)
    rows[:blocks, :] = high
    rows[blocks : 2 * blocks, :] = line - high
    table[...] = rows[...].astype(BF16)
    for p in range(peers):
        pltpu.make_async_copy(table, out.at[p, pl.ds(pixels, TABLE_ROWS), :], extra.at[p]).start()
    for i in range(STEPS):
        at = pl.ds(i * step, step)
        pltpu.make_async_copy(tile.at[:, at, :], held.at[:, at, :], come.at[i]).wait()
        into = pl.ds(i * step * blocks, step * blocks)
        for p in range(peers):
            lanes = slice(p * LANES, (p + 1) * LANES)
            parts = [halves(held[j, at, lanes].astype(F32)) for j in range(blocks)]
            made[p, into, :] = weave(parts).astype(BF16)
        pltpu.make_async_copy(made.at[:, into, :], out.at[:, into, :], go.at[i]).start()
    for i in range(STEPS):
        into = pl.ds(i * step * blocks, step * blocks)
        pltpu.make_async_copy(made.at[:, into, :], out.at[:, into, :], go.at[i]).wait()
    for p in range(peers):
        pltpu.make_async_copy(table, out.at[p, pl.ds(pixels, TABLE_ROWS), :], extra.at[p]).wait()


def spread(tile, blocks, peers, peer, slot, count, weight, wanted):
    pixels, atoms = tile.shape
    shaped = tile.reshape(blocks, pixels // blocks, atoms)
    inputs = (wanted.transpose(0, 2, 1), peer, slot, count.T, weight, shaped)
    inputs = tuple(pltpu.with_memory_space_constraint(a, pltpu.HBM) for a in inputs)
    return pl.pallas_call(
        spread_kernel,
        in_specs=[pl.BlockSpec(memory_space=pltpu.HBM)] * len(inputs),
        out_specs=pl.BlockSpec(memory_space=pltpu.HBM),
        out_shape=pltpu.HBM((peers, pixels + TABLE_ROWS, LANES), tile.dtype),
        scratch_shapes=[
            pltpu.VMEM(shaped.shape, tile.dtype),
            pltpu.VMEM((peers, pixels, LANES), tile.dtype),
            *(pltpu.VMEM(a.shape, a.dtype) for a in inputs[:-1]),
            pltpu.VMEM((TABLE_ROWS, LANES), F32),
            pltpu.VMEM((TABLE_ROWS, LANES), BF16),
            pltpu.SemaphoreType.DMA((len(inputs) - 1,)),
            pltpu.SemaphoreType.DMA((STEPS,)),
            pltpu.SemaphoreType.DMA((STEPS,)),
            pltpu.SemaphoreType.DMA((peers,)),
        ],
        compiler_params=pltpu.CompilerParams(vmem_limit_bytes=16 * MIB),
        cost_estimate=cost(pixels * atoms, 4 * pixels * atoms),
        name="spread",
    )(*inputs)


def inverse_kernel(lib_ref, inv_ref):
    size = lib_ref.shape[0]
    lib = lib_ref[...]
    rows = lax.broadcasted_iota(jnp.int32, (size, size), 0)
    cols = lax.broadcasted_iota(jnp.int32, (size, size), 1)
    eye = (rows == cols).astype(F32)
    gram = times_transposed(lib, lib) + MU * eye
    bound = jnp.max(jnp.sum(jnp.abs(gram), axis=1, keepdims=True))
    inv_ref[...] = eye * (2.0 / (1.0 + bound))

    def exact(a, b):
        return jnp.dot(a, b, precision=lax.Precision.HIGHEST, preferred_element_type=F32)

    def unfinished(state):
        count, worst = state
        return jnp.logical_and(count < 22, worst > 1e-4)

    def improve(state):
        count, _ = state
        x = inv_ref[...]
        rest = eye - exact(gram, x)
        inv_ref[...] = x + exact(x, rest)
        return count + 1, jnp.max(jnp.sum(jnp.abs(rest), axis=1, keepdims=True))

    lax.while_loop(unfinished, improve, (jnp.int32(0), jnp.float32(1.0)))


def gram_inverse(lib):
    size = lib.shape[0]
    return pl.pallas_call(
        inverse_kernel,
        out_shape=jax.ShapeDtypeStruct((size, size), F32),
        cost_estimate=cost(10 * 12 * size**3, 4 * size * size),
        compiler_params=pltpu.CompilerParams(vmem_limit_bytes=63 * MIB),
        name="inverse",
    )(lib)


def solve_kernel(first, *refs):
    if first:
        obs, lib, inv, thr, z, up, down, left, right, parts, primal = refs[:11]
        padded, base, low, back = refs[11:]
    else:
        obs, lib, inv, thr, z, up, down, left, right, old_parts, old_primal, code, parts = refs[:13]
        padded, base, low, back, mix = refs[13:]
    i = pl.program_id(0)
    row = up.shape[0]
    block = obs.shape[0]
    peers = padded.shape[0]
    pixels = padded.shape[1] - 2 * row

    @pl.when(i == 0)
    def _():
        for p in range(peers):
            lanes = slice(p * LANES, (p + 1) * LANES)
            padded[p, :row, :] = up[:, lanes]
            padded[p, row + pixels :, :] = down[:, lanes]
            if first:
                padded[p, row : row + pixels, :] = z[:, lanes]

        def natural(p, carry):
            for k in range(STEPS):
                at = slice(k * pixels // STEPS, (k + 1) * pixels // STEPS)
                for j, rows in enumerate(unweave(z[p, at, :].astype(F32))):
                    to = j * block + k * block // STEPS
                    rows = rows.reshape(-1, LANES)
                    padded[p, row + to : row + to + rows.shape[0], :] = rows.astype(BF16)
                for j, rows in enumerate(unweave(decode_fixed(code[p, at, :]))):
                    to = j * block + k * block // STEPS
                    rows = rows.reshape(-1, LANES)
                    mix[p, to : to + rows.shape[0], :] = (GAMMA / TOTAL) * rows
            return carry

        if not first:
            lax.fori_loop(0, peers, natural, 0)

    at = pl.multiple_of(i * block, block)
    base[...] = jnp.dot(obs[...], lib[...], preferred_element_type=F32)
    for p in range(peers):
        lanes = slice(p * LANES, (p + 1) * LANES)
        value = base[:, lanes] + MU * padded[p, pl.ds(at + row, block), :].astype(F32)
        if not first:
            fresh = jnp.maximum(old_parts[:, lanes] + mix[p, pl.ds(at, block), :], 0.0)
            value = value + MU * (fresh - old_primal[:, lanes])
        low[:, lanes] = value.astype(BF16)
    small = times_transposed(low[...], lib[...])
    solved = jnp.dot(
        small, inv[...], precision=lax.Precision.HIGHEST, preferred_element_type=F32
    )
    back[...] = jnp.dot(solved.astype(BF16), lib[...], preferred_element_type=F32)
    place = lax.broadcasted_iota(jnp.int32, (block, LANES), 0) % row
    for p in range(peers):
        lanes = slice(p * LANES, (p + 1) * LANES)
        here = padded[p, pl.ds(at + row, block), :].astype(F32)
        above = padded[p, pl.ds(at, block), :].astype(F32)
        below = padded[p, pl.ds(at + 2 * row, block), :].astype(F32)

        def edge(halo):
            return jnp.concatenate(
                [
                    jnp.broadcast_to(halo[0, k : k + 1, lanes], (row, LANES))
                    for k in range(block // row)
                ],
                axis=0,
            )

        before = jnp.where(place == 0, edge(left), pltpu.roll(here, 1, 0))
        after = jnp.where(place == row - 1, edge(right), pltpu.roll(here, block - 1, 0))
        spatial = 0.25 * (above + below + before + after)
        unmixed = (base[:, lanes] + MU * here - back[:, lanes]) / MU
        if first:
            primal[:, lanes] = unmixed
        parts[:, lanes] = (unmixed + ETA * spatial) * (1.0 / TOTAL) - thr[:, lanes]


def solve(first, obs, lib, inv, thr, z, halos, carried=()):
    pixels = obs.shape[0]
    atoms = lib.shape[1]
    peers = atoms // LANES
    up, down, left, right = halos
    row = up.shape[0]
    block = BLOCK_ROWS * row
    steps = pixels // block
    whole = lambda a: pl.BlockSpec(a.shape, lambda i, n=a.ndim: (0,) * n)
    tile = pl.BlockSpec((block, atoms), lambda i: (i, 0))
    side = pl.BlockSpec((1, BLOCK_ROWS, atoms), lambda i: (i, 0, 0))
    full = jax.ShapeDtypeStruct((pixels, atoms), F32)
    return pl.pallas_call(
        functools.partial(solve_kernel, first),
        grid=(steps,),
        in_specs=[
            pl.BlockSpec((block, obs.shape[1]), lambda i: (i, 0)),
            whole(lib), whole(inv), whole(thr), whole(z), whole(up), whole(down), side, side,
        ]
        + ([] if first else [tile, tile, whole(carried[2])]),
        out_specs=[tile, tile] if first else tile,
        out_shape=[full, full] if first else full,
        scratch_shapes=[
            pltpu.VMEM((peers, pixels + 2 * row, LANES), BF16),
            pltpu.VMEM((block, atoms), F32),
            pltpu.VMEM((block, atoms), BF16),
            pltpu.VMEM((block, atoms), F32),
        ]
        + ([] if first else [pltpu.VMEM((peers, pixels, LANES), F32)]),
        cost_estimate=cost(6 * pixels * atoms * BANDS_PAD, 16 * pixels * atoms),
        compiler_params=pltpu.CompilerParams(vmem_limit_bytes=63 * MIB),
        name="solve_first" if first else "solve_second",
    )(obs, lib, inv, thr, z, up, down, left, right, *carried)


def weights_of(tables):
    size, spots = tables.shape
    rows = lax.broadcasted_iota(jnp.int32, (2 * size, size), 0)
    cols = lax.broadcasted_iota(jnp.int32, (2 * size, size), 1)
    inner = rows % size
    line = inner // 16 * 16 + inner % 16 // 4 + BLOCKS * (rows // size)
    pick = jnp.where(cols == line, 1.0, 0.0).astype(BF16)
    lines = jnp.dot(pick, tables, preferred_element_type=F32).astype(BF16)
    spot = lax.broadcasted_iota(jnp.int32, (spots, size), 0)
    col = lax.broadcasted_iota(jnp.int32, (spots, size), 1)
    widen = jnp.where(spot == col // 4, 1.0, 0.0).astype(BF16)
    wide = jnp.dot(lines, widen, preferred_element_type=F32)
    return jnp.where(rows % 4 == cols % 4, wide, 0.0).astype(BF16)


def mix_steps(encode, weights, z, out, made, go):
    peers, pixels, _ = made.shape
    size = peers * 16
    step = pixels // STEPS

    def rows_of(i):
        return pl.ds(pl.multiple_of(i * step, step), step)

    def one(i, carry):
        for k in range(0, step, 32):
            at = i * step + k
            tiles = [
                z[:, pl.ds(pl.multiple_of(at + d, 16), 16), :].reshape(size, LANES) for d in (0, 16)
            ]
            both = jnp.dot(
                weights[...], jnp.concatenate(tiles, axis=1), preferred_element_type=F32
            )
            coded = encode(both[:size] + both[size:])
            for d in (0, 1):
                made[:, pl.ds(pl.multiple_of(at + 16 * d, 16), 16), :] = coded[
                    :, d * LANES : (d + 1) * LANES
                ].reshape(peers, 16, LANES)
        rows = rows_of(i)
        pltpu.make_async_copy(made.at[:, rows, :], out.at[:, rows, :], go.at[i]).start()
        return carry

    lax.fori_loop(0, STEPS, one, 0)
    for i in range(STEPS):
        rows = pl.ds(i * step, step)
        pltpu.make_async_copy(made.at[:, rows, :], out.at[:, rows, :], go.at[i]).wait()


def mix_first_kernel(encode, z, out, table, made, weights, go, kept):
    pixels = made.shape[1]
    weights[...] = weights_of(z[:, pixels:, :].reshape(-1, LANES))
    keep = pltpu.make_async_copy(weights, table, kept)
    keep.start()
    mix_steps(encode, weights, z, out, made, go)
    keep.wait()


def mix_second_kernel(encode, weights, z, out, made, go):
    mix_steps(encode, weights, z, out, made, go)


def mix(encode, dtype, z, weights=None):
    peers = z.shape[0]
    pixels = z.shape[1] // LANES * LANES
    size = peers * 16
    hbm = pl.BlockSpec(memory_space=pltpu.HBM)
    vmem = pl.BlockSpec(memory_space=pltpu.VMEM)
    shape = pltpu.HBM((peers, pixels, LANES), dtype)
    made = pltpu.VMEM((peers, pixels, LANES), dtype)
    go = pltpu.SemaphoreType.DMA((STEPS,))
    first = weights is None
    return pl.pallas_call(
        functools.partial(mix_first_kernel if first else mix_second_kernel, encode),
        in_specs=[vmem] if first else [vmem, vmem],
        out_specs=[hbm, hbm] if first else hbm,
        out_shape=[shape, pltpu.HBM((2 * size, size), BF16)] if first else shape,
        scratch_shapes=[made, pltpu.VMEM((2 * size, size), BF16), go, pltpu.SemaphoreType.DMA]
        if first
        else [made, go],
        compiler_params=pltpu.CompilerParams(vmem_limit_bytes=48 * MIB),
        cost_estimate=cost(4 * size * pixels // 16 * LANES * size, 4 * peers * pixels * LANES),
        name="mix",
    )(*(() if first else (weights,)), z)


def fresh_kernel(
    parts, mixed, out, top_at, bottom_at, left_at, right_at,
    held, code, made, top, bottom, side, left, right, come, came, go, gone,
):
    blocks, block, _ = held.shape
    peers = made.shape[0]
    step = block // STEPS
    row = top.shape[0]
    reads, writes = [], []
    for i in range(STEPS):
        at = pl.ds(i * step, step)
        woven = pl.ds(i * step * blocks, step * blocks)
        reads.append(
            (
                pltpu.make_async_copy(parts.at[:, at, :], held.at[:, at, :], come.at[i]),
                pltpu.make_async_copy(mixed.at[:, woven, :], code.at[:, woven, :], came.at[i]),
            )
        )
        writes.append(pltpu.make_async_copy(made.at[:, woven, :], out.at[:, woven, :], go.at[i]))
    edges = ((top, top_at), (bottom, bottom_at), (left, left_at), (right, right_at))
    edges = [pltpu.make_async_copy(a, b, gone.at[k]) for k, (a, b) in enumerate(edges)]
    for pair in reads[:AHEAD]:
        for copy in pair:
            copy.start()
    for i in range(STEPS):
        for copy in reads[i]:
            copy.wait()
        if i + AHEAD < STEPS:
            for copy in reads[i + AHEAD]:
                copy.start()
        first = i * step
        at = slice(first, first + step)
        woven = slice(first * blocks, (first + step) * blocks)
        for p in range(peers):
            lanes = slice(p * LANES, (p + 1) * LANES)
            sums = unweave(decode_fixed(code[p, woven, :]))
            values = [
                jnp.maximum(halves(held[j, at, lanes]) + (GAMMA / TOTAL) * sums[j], 0.0)
                for j in range(blocks)
            ]
            made[p, woven, :] = weave(values).astype(BF16)
            if first < row:
                top[at, lanes] = values[0].reshape(step, LANES).astype(BF16)
            if first >= block - row:
                into = slice(first - block + row, first - block + row + step)
                bottom[into, lanes] = values[-1].reshape(step, LANES).astype(BF16)
            for j in range(blocks):
                line = j * BLOCK_ROWS + first // row
                if first % row == 0:
                    side[0, line : line + 1, lanes] = values[j][0, :1, :]
                if (first + step) % row == 0:
                    side[1, line : line + 1, lanes] = values[j][-1, 7:, :]
        writes[i].start()
    left[...] = side[0].astype(BF16)
    right[...] = side[1].astype(BF16)
    for copy in edges:
        copy.start()
    for copy in edges + writes:
        copy.wait()


def fresh_pieces(parts, mixed, tile_rows, tile_cols):
    peers, pixels, _ = mixed.shape
    atoms = parts.shape[1]
    hbm = pl.BlockSpec(memory_space=pltpu.HBM)
    shaped = parts.reshape(BLOCKS, pixels // BLOCKS, atoms)
    ends = ((tile_cols, atoms), (tile_cols, atoms), (tile_rows, atoms), (tile_rows, atoms))
    return pl.pallas_call(
        fresh_kernel,
        in_specs=[hbm, hbm],
        out_specs=[hbm] * 5,
        out_shape=[pltpu.HBM((peers, pixels, LANES), BF16)] + [pltpu.HBM(a, BF16) for a in ends],
        scratch_shapes=[
            pltpu.VMEM(shaped.shape, F32),
            pltpu.VMEM((peers, pixels, LANES), mixed.dtype),
            pltpu.VMEM((peers, pixels, LANES), BF16),
            pltpu.VMEM(ends[0], BF16),
            pltpu.VMEM(ends[1], BF16),
            pltpu.VMEM((2, tile_rows, atoms), F32),
            pltpu.VMEM(ends[2], BF16),
            pltpu.VMEM(ends[3], BF16),
            pltpu.SemaphoreType.DMA((STEPS,)),
            pltpu.SemaphoreType.DMA((STEPS,)),
            pltpu.SemaphoreType.DMA((STEPS,)),
            pltpu.SemaphoreType.DMA((4,)),
        ],
        compiler_params=pltpu.CompilerParams(vmem_limit_bytes=63 * MIB),
        cost_estimate=cost(4 * pixels * atoms, 8 * pixels * atoms),
        name="fresh",
    )(shaped, mixed)


def final_kernel(
    parts, mixed, obs, turned, out, misfit,
    held, code, made, rest, seen, spectra, come, came, go, went, side,
):
    blocks, block, atoms = held.shape
    step = block // STEPS
    wide = WIDE * step
    bands = rest.shape[2]
    reads, writes = [], []
    for i in range(STEPS):
        at = pl.ds(i * step, step)
        woven = pl.ds(i * step * blocks, step * blocks)
        reads.append(
            (
                pltpu.make_async_copy(parts.at[:, at, :], held.at[:, at, :], come.at[i]),
                pltpu.make_async_copy(mixed.at[:, woven, :], code.at[:, woven, :], came.at[i]),
            )
        )
        writes.append(pltpu.make_async_copy(made.at[:, at, :], out.at[:, at, :], go.at[i]))
    others = (
        pltpu.make_async_copy(turned, spectra, side.at[0]),
        pltpu.make_async_copy(obs, seen, side.at[1]),
    )
    for i, pair in enumerate(reads[:AHEAD]):
        for copy in pair:
            copy.start()
        if i == 0:
            for copy in others:
                copy.start()
    for i in range(STEPS):
        for copy in reads[i]:
            copy.wait()
        if i + AHEAD < STEPS:
            for copy in reads[i + AHEAD]:
                copy.start()
        at = slice(i * step, (i + 1) * step)
        woven = slice(i * step * blocks, (i + 1) * step * blocks)
        for p in range(mixed.shape[0]):
            lanes = slice(p * LANES, (p + 1) * LANES)
            sums = unweave(decode_float(code[p, woven, :]))
            for j in range(blocks):
                value = halves(held[j, at, lanes]) + (GAMMA / TOTAL) * sums[j]
                made[j, at, lanes] = jnp.maximum(value, 0.0).reshape(step, LANES).astype(BF16)
        writes[i].start()
        if i == 0:
            for copy in others:
                copy.wait()
        if (i + 1) % WIDE == 0:
            k = i // WIDE
            rows = pl.ds(k * wide, wide)
            rebuilt = jnp.dot(
                made[:, k * wide : (k + 1) * wide, :].reshape(blocks * wide, atoms),
                spectra[...],
                preferred_element_type=F32,
            )
            for j in range(blocks):
                real = seen[j, k * wide : (k + 1) * wide, :].astype(F32)
                less = real - rebuilt[j * wide : (j + 1) * wide]
                rest[j, k * wide : (k + 1) * wide, :] = less[:, :bands]
            writes.append(
                pltpu.make_async_copy(rest.at[:, rows, :], misfit.at[:, rows, :], went.at[k])
            )
            writes[-1].start()
    for copy in writes:
        copy.wait()


def final(parts, mixed, obs, turned, bands):
    peers, pixels, _ = mixed.shape
    atoms = parts.shape[1]
    by_block = lambda a: a.reshape(BLOCKS, pixels // BLOCKS, a.shape[1])
    parts, obs = by_block(parts), by_block(obs)
    hbm = pl.BlockSpec(memory_space=pltpu.HBM)
    left = (BLOCKS, pixels // BLOCKS, bands)
    return pl.pallas_call(
        final_kernel,
        in_specs=[hbm, hbm, hbm, hbm],
        out_specs=[hbm, hbm],
        out_shape=[pltpu.HBM(parts.shape, BF16), pltpu.HBM(left, F32)],
        scratch_shapes=[
            pltpu.VMEM(parts.shape, F32),
            pltpu.VMEM((peers, pixels, LANES), mixed.dtype),
            pltpu.VMEM(parts.shape, BF16),
            pltpu.VMEM(left, F32),
            pltpu.VMEM(obs.shape, obs.dtype),
            pltpu.VMEM(turned.shape, turned.dtype),
            pltpu.SemaphoreType.DMA((STEPS,)),
            pltpu.SemaphoreType.DMA((STEPS,)),
            pltpu.SemaphoreType.DMA((STEPS,)),
            pltpu.SemaphoreType.DMA((STEPS // WIDE,)),
            pltpu.SemaphoreType.DMA((2,)),
        ],
        compiler_params=pltpu.CompilerParams(vmem_limit_bytes=63 * MIB),
        cost_estimate=cost(2 * pixels * atoms * BANDS_PAD, 8 * pixels * atoms),
        name="final",
    )(parts, mixed, obs, turned)


def shifted(array, axis, up):
    peers = lax.axis_size(axis)
    pairs = [(k, k + 1) for k in range(peers - 1)]
    return lax.ppermute(array, axis, pairs if up else [(b, a) for a, b in pairs])


def exchanged(pieces):
    return lax.all_to_all(pieces, "col", 0, 0, tiled=True)


def halos_of(top, bottom, left, right):
    up = shifted(bottom, "row", True)
    down = shifted(top, "row", False)
    before = shifted(right, "col", True)
    after = shifted(left, "col", False)
    by_block = lambda a: a.astype(F32).reshape(BLOCKS, BLOCK_ROWS, -1)
    return up, down, by_block(before), by_block(after)


def local(
    observed, library, warm, match_peer, match_slot, match_count, match_weight, wanted, threshold
):
    tile_rows, tile_cols, atoms = warm.shape
    bands = library.shape[0]
    pixels = tile_rows * tile_cols
    peers = lax.axis_size("col")
    flat = warm.reshape(pixels, atoms)

    pieces = spread(
        flat, BLOCKS, peers,
        match_peer, match_slot, match_count, match_weight, wanted,
    )
    strip = exchanged(pieces)
    halos = halos_of(warm[0], warm[-1], warm[:, 0], warm[:, -1])
    lib = jnp.pad(library, ((0, BANDS_PAD - bands), (0, 0)))
    obs = jnp.pad(observed.reshape(pixels, bands), ((0, 0), (0, BANDS_PAD - bands)))
    inv = gram_inverse(lib)
    thr = threshold[None, :]

    sums, weights = mix(encode_fixed, jnp.int16, strip)
    mixed = exchanged(sums)
    parts, primal = solve(True, obs, lib, inv, thr, flat, halos)
    pieces, *edges = fresh_pieces(parts, mixed, tile_rows, tile_cols)
    strip = exchanged(pieces)
    halos = halos_of(*edges)
    sums = mix(encode_float, BF16, strip, weights)
    mixed_again = exchanged(sums)
    parts = solve(False, obs, lib, inv, thr, pieces, halos, (parts, primal, mixed))
    abundance, misfit = final(parts, mixed_again, obs, lib.T, bands)
    return (
        abundance.reshape(tile_rows, tile_cols, atoms),
        misfit.reshape(tile_rows, tile_cols, bands),
    )


def solution(mesh):
    return jax.shard_map(
        local,
        mesh=mesh,
        in_specs=(
            P("row", "col", None),
            P(),
            P("row", "col", None),
            P("row", "col", None),
            P("row", "col", None),
            P("row", "col"),
            P("row", "col", None),
            P("row", "col", None),
            P(),
        ),
        out_specs=(P("row", "col", None), P("row", "col", None)),
        check_vma=False,
    )
```

time: 193 us -> 185 us (0.959)
  Pallas kernels: 59.6 us -> 52.5 us
  blocking collectives: 70.4 us -> 68.2 us
  waiting for transfers between devices: 14.2 us -> 16.3 us
  local copies, waits for them, and re-layouts: 13.7 us -> 11.6 us
    pallas_call x4, Pallas kernels: 21.6 us -> 15.2 us  [the longest x2 7.24 us: mix(): pl.pallas_call(functools.partial(mix_first_kernel if first else mix_secon...]
    slice x6 -> x1, local copies, waits for them, and re-layouts: 4.21 us -> 1.41 us  [local(): halos = halos_of(warm[0], warm[-1], warm[:, 0], warm[:, -1])]
    all_to_all x2, blocking collectives: 70.4 us -> 68.2 us  [exchanged(): return lax.all_to_all(pieces, 'col', 0, 0, tiled=True)]
    ppermute x8, waiting for transfers between devices: 14.2 us -> 16.3 us  [shifted(): lax.ppermute(array, axis, pairs if up else [(b, a) for a, b in pairs])]
where the time goes in v2:
time: 185 us; the launch traced here: 183 us
  blocking collectives  68.2 us (37%)
  Pallas kernels  52.5 us (28%)
  starting transfers between devices  33.7 us (18%)
  waiting for transfers between devices  16.3 us (9%)
  local copies, waits for them, and re-layouts  11.6 us (6%)
    all_to_all x2, blocking collectives, exchanged(): return lax.all_to_all(pieces, 'col', 0, 0, tiled=True)  68.2 us
    pallas_call x2, Pallas kernels, solve(): pl.pallas_call(functools.partial(solve_kernel, first), grid=(steps,), in_...  24.1 us
    ppermute x8, starting transfers between devices, shifted(): lax.ppermute(array, axis, pairs if up else [(b, a) for a, b in pairs])  21.3 us
    ppermute x8, waiting for transfers between devices, shifted(): lax.ppermute(array, axis, pairs if up else [(b, a) for a, b in pairs])  16.3 us
    all_to_all x2, starting transfers between devices, exchanged(): return lax.all_to_all(pieces, 'col', 0, 0, tiled=True)  12.4 us
    pallas_call x1, Pallas kernels, gram_inverse(): pl.pallas_call(inverse_kernel, out_shape=jax.ShapeDtypeStruct((size, size...  7.67 us
    pallas_call x2, Pallas kernels, mix(): pl.pallas_call(functools.partial(mix_first_kernel if first else mix_secon...  7.24 us
    pallas_call x1, Pallas kernels, final(): pl.pallas_call(final_kernel, in_specs=[hbm, hbm, hbm, hbm], out_specs=[hb...  5.48 us
  transfers between devices with their start and end apart: 10, of which 2 were waited for; matrix products, arithmetic and copies ran while one was open for 5% of the time, Pallas kernels for 17%

profile of v2, /device:TPU:2, one launch (start us, length us, event | category | flops | bytes accessed | tf_op | source)
XLA Modules:
  0.0 183.3 jit_solution(1551798742286969757)
XLA Ops:
  0.6 3.5 %spread.1 = bf16[16,528,128]{2,1,0:T(8,128)(2,1)} custom-call(s32[1,2,16]{2,1,0:T(2,128)} %bitcast.33, s32[4,1,8]{2,1,0:T(1,128)} %peer_at.1, s32[4,1,8]{2,1,0:T(1,128)} %slot_at.1, s32[1,4]{1,0:T(1,128)} %bitcast.34, f32[4,1,8]{2,1,0:T(1,128)} %weight_at.1, bf16[4,128,2048]{2,1,0:T(8,128)(2,1)} %bitcast.25), custom_call_target="tpu_custom_call" | custom-call | flops 1048576 | bytes 4194304 | tf_op jit(solution)/shard_map/spread/pallas_call | solution.py:154
  4.2 36.3 %all_to_all.20.z = bf16[16,528,128]{2,1,0:T(8,128)(2,1)S(1)} all-to-all(bf16[16,528,128]{2,1,0:T(8,128)(2,1)} %spread.1), channel_id=1, replica_groups=mesh['row'=8,'col'=16] {'col'}, dimensions={0} | all-to-all | bytes 4325376 | tf_op jit(solution)/shard_map/all_to_all | solution.py:607
  40.5 3.8 %mix.2 = (s16[16,512,128]{2,1,0:T(8,128)(2,1)}, bf16[512,256]{1,0:T(8,128)(2,1)}) custom-call(bf16[16,528,128]{2,1,0:T(8,128)(2,1)S(1)} %all_to_all.20.z), custom_call_target="tpu_custom_call" | custom-call | flops 1073741824 | bytes 4194304 | tf_op jit(solution)/shard_map/mix/pallas_call | solution.py:396
  44.3 0.0 copy-start.3
  44.3 5.8 %all-to-all-start.1 = ((s16[16,512,128]{2,1,0:T(8,128)(2,1)}), s16[16,512,128]{2,1,0:T(8,128)(2,1)}, u32[]{:S(2)}, u32[]{:S(2)}) async-start(s16[16,512,128]{2,1,0:T(8,128)(2,1)} %get-tuple-element.14), calls=%async_computation.1 | async-start | bytes 4194304 | tf_op jit(solution)/shard_map/all_to_all | solution.py:607
  50.1 1.0 slice_bitcast_fusion
  51.1 1.3 collective-permute-start
  52.4 1.3 collective-permute-start.1
  53.7 1.4 fusion
  55.1 3.4 %collective-permute-start.2 = (bf16[16,2048]{1,0:T(8,128)(2,1)S(1)}, bf16[16,2048]{1,0:T(8,128)(2,1)S(1)}, u32[]{:S(2)}, u32[]{:S(2)}) collective-permute-start(bf16[16,2048]{1,0:T(8,128)(2,1)S(1)} %bitcast.29), channel_id=1, source_target_pairs={{0,1},{1,2},{2,3},{3,4},{4,5},{5,6},{6,7},{7,8},{8,9},{9,10},{10,1... | collective-permute-start | bytes 196616 | tf_op jit(solution)/shard_map/ppermute | solution.py:603
  58.6 4.6 %collective-permute-start.3 = (bf16[16,2048]{1,0:T(8,128)(2,1)S(1)}, bf16[16,2048]{1,0:T(8,128)(2,1)S(1)}, u32[]{:S(2)}, u32[]{:S(2)}) collective-permute-start(bf16[16,2048]{1,0:T(8,128)(2,1)S(1)} %bitcast.30), channel_id=1, source_target_pairs={{1,0},{2,1},{3,2},{4,3},{5,4},{6,5},{7,6},{8,7},{9,8},{10,9},{11,1... | collective-permute-start | bytes 196616 | tf_op jit(solution)/shard_map/ppermute | solution.py:603
  63.2 0.0 copy-done.3
  63.2 0.5 copy.15
  63.7 0.0 copy-start.1
  63.7 1.0 copy-done.1
  64.7 0.5 copy.25
  65.2 0.9 pad.9.clone.lib_ref.refs_1_
  66.2 0.0 copy-done.4
  66.2 0.7 pad.8.refs_0_
  66.9 7.7 %inverse.1.refs_2_ = f32[192,192]{1,0:T(8,128)} custom-call(bf16[192,2048]{1,0:T(8,128)(2,1)} %pad.9.clone.lib_ref.refs_1_), custom_call_target="tpu_custom_call" | custom-call | flops 849346560 | bytes 147456 | tf_op jit(solution)/shard_map/inverse/pallas_call | solution.py:205
  74.6 2.0 %collective-permute-done.2 = bf16[16,2048]{1,0:T(8,128)(2,1)S(1)} collective-permute-done((bf16[16,2048]{1,0:T(8,128)(2,1)S(1)}, bf16[16,2048]{1,0:T(8,128)(2,1)S(1)}, u32[]{:S(2)}, u32[]{:S(2)}) %collective-permute-start.2) | collective-permute-done | bytes 65568 | tf_op jit(solution)/shard_map/ppermute | solution.py:603
  76.6 0.7 reshape.61.refs_7_
  77.3 0.0 collective-permute-done.3
  77.3 0.7 reshape.63.refs_8_
  78.0 0.0 collective-permute-done.refs_5_
  78.0 0.0 collective-permute-done.1.refs_6_
  78.0 0.0 copy-start.8
  78.1 0.6 copy-done.7
  78.7 0.0 copy-done.8
  78.7 10.7 %solve_first.1 = (f32[512,2048]{1,0:T(8,128)}, f32[512,2048]{1,0:T(8,128)}) custom-call(bf16[512,192]{1,0:T(8,128)(2,1)} %pad.8.refs_0_, bf16[192,2048]{1,0:T(8,128)(2,1)} %pad.9.clone.lib_ref.refs_1_, f32[192,192]{1,0:T(8,128)} %inverse.1.refs_2_, f32[1,2048]{1,0:T(1,128)} %bitcast.31, bf16[512,2048]{1,0:T(8,128)(2,1)} %bitcast.26, ...), custom_call_target="tpu_custom_call" | custom-call | flops 1207959552 | bytes 16777216 | tf_op jit(solution)/shard_map/solve_first/pallas_call | solution.py:303
  89.4 0.0 all-to-all-done.1.mixed.refs_11_
  89.4 4.5 %fresh.1 = (bf16[16,512,128]{2,1,0:T(8,128)(2,1)}, bf16[32,2048]{1,0:T(8,128)(2,1)}, bf16[32,2048]{1,0:T(8,128)(2,1)}, bf16[16,2048]{1,0:T(8,128)(2,1)}, bf16[16,2048]{1,0:T(8,128)(2,1)}) custom-call(f32[4,128,2048]{2,1,0:T(8,128)} %bitcast.23, s16[16,512,128]{2,1,0:T(8,128)(2,1)} %all-to-all-done.1.mixed.refs_11_), custom_call_target="tpu_custom_call" | custom-call | flops 4194304 | bytes 8388608 | tf_op jit(solution)/shard_map/fresh/pallas_call | solution.py:477
  93.9 0.0 copy-start
  93.9 31.9 %all_to_all.21.z = bf16[16,512,128]{2,1,0:T(8,128)(2,1)S(1)} all-to-all(bf16[16,512,128]{2,1,0:T(8,128)(2,1)} %get-tuple-element.15.refs_4_), channel_id=1, replica_groups=mesh['row'=8,'col'=16] {'col'}, dimensions={0} | all-to-all | bytes 4194304 | tf_op jit(solution)/shard_map/all_to_all | solution.py:607
  125.9 0.0 copy-done
  125.9 3.4 %mix.3 = bf16[16,512,128]{2,1,0:T(8,128)(2,1)} custom-call(bf16[512,256]{1,0:T(8,128)(2,1)S(1)} %copy-done, bf16[16,512,128]{2,1,0:T(8,128)(2,1)S(1)} %all_to_all.21.z), custom_call_target="tpu_custom_call" | custom-call | flops 1073741824 | bytes 4194304 | tf_op jit(solution)/shard_map/mix/pallas_call | solution.py:396
  129.3 0.0 copy-start.12
  129.3 0.0 copy-start.11
  129.3 0.0 copy-start.10
  129.3 0.0 copy-start.9
  129.4 0.0 copy-start.2
  129.4 6.6 %all-to-all-start.3 = ((bf16[16,512,128]{2,1,0:T(8,128)(2,1)}), bf16[16,512,128]{2,1,0:T(8,128)(2,1)}, u32[]{:S(2)}, u32[]{:S(2)}) async-start(bf16[16,512,128]{2,1,0:T(8,128)(2,1)} %mix.3), calls=%async_computation.3 | async-start | bytes 4194304 | tf_op jit(solution)/shard_map/all_to_all | solution.py:607
  136.0 0.0 copy-done.12
  136.0 3.4 %collective-permute-start.6 = (bf16[16,2048]{1,0:T(8,128)(2,1)S(1)}, bf16[16,2048]{1,0:T(8,128)(2,1)S(1)}, u32[]{:S(2)}, u32[]{:S(2)}) collective-permute-start(bf16[16,2048]{1,0:T(8,128)(2,1)S(1)} %copy-done.12), channel_id=1, source_target_pairs={{0,1},{1,2},{2,3},{3,4},{4,5},{5,6},{6,7},{7,8},{8,9},{9,10},{10,1... | collective-permute-start | bytes 196616 | tf_op jit(solution)/shard_map/ppermute | solution.py:603
  139.4 0.0 copy-done.11
  139.4 4.6 %collective-permute-start.7 = (bf16[16,2048]{1,0:T(8,128)(2,1)S(1)}, bf16[16,2048]{1,0:T(8,128)(2,1)S(1)}, u32[]{:S(2)}, u32[]{:S(2)}) collective-permute-start(bf16[16,2048]{1,0:T(8,128)(2,1)S(1)} %copy-done.11), channel_id=1, source_target_pairs={{1,0},{2,1},{3,2},{4,3},{5,4},{6,5},{7,6},{8,7},{9,8},{10,9},{11,1... | collective-permute-start | bytes 196616 | tf_op jit(solution)/shard_map/ppermute | solution.py:603
  144.0 0.0 copy-done.10
  144.0 1.3 collective-permute-start.4
  145.3 0.0 copy-done.9
  145.3 1.5 collective-permute-start.5
  146.8 0.0 copy-done.2
  146.8 1.2 pad_bitcast_fusion.turned
  148.0 14.2 %collective-permute-done.6 = bf16[16,2048]{1,0:T(8,128)(2,1)S(1)} collective-permute-done((bf16[16,2048]{1,0:T(8,128)(2,1)S(1)}, bf16[16,2048]{1,0:T(8,128)(2,1)S(1)}, u32[]{:S(2)}, u32[]{:S(2)}) %collective-permute-start.6) | collective-permute-done | bytes 65568 | tf_op jit(solution)/shard_map/ppermute | solution.py:603
  162.2 0.7 reshape.65.refs_7_
  162.9 0.0 collective-permute-done.7
  162.9 0.7 reshape.67.refs_8_
  163.6 0.0 collective-permute-done.4.refs_5_
  163.6 0.0 collective-permute-done.5.refs_6_
  163.6 0.0 copy-start.6
  163.6 0.6 copy-done.5
  164.2 0.0 copy-done.6
  164.3 13.4 %solve_second.1 = f32[512,2048]{1,0:T(8,128)} custom-call(bf16[512,192]{1,0:T(8,128)(2,1)} %pad.8.refs_0_, bf16[192,2048]{1,0:T(8,128)(2,1)} %pad.9.clone.lib_ref.refs_1_, f32[192,192]{1,0:T(8,128)} %inverse.1.refs_2_, f32[1,2048]{1,0:T(1,128)} %bitcast.32, bf16[16,512,128]{2,1,0:T(8,128)(2,1)} %get-tuple-element.15.refs_4_, bf16[32,2048]{1,0:T(8,128)(2,1)} %copy-done.5, ...), custom_call_target="tpu_custom_call" | custom-call | flops 1207959552 | bytes 16777216 | tf_op jit(solution)/shard_map/solve_second/pallas_call | solution.py:303
  177.7 0.0 all-to-all-done.3.mixed
  177.7 5.5 %final.1 = (bf16[4,128,2048]{2,1,0:T(8,128)(2,1)}, f32[4,128,188]{2,1,0:T(8,128)}) custom-call(f32[4,128,2048]{2,1,0:T(8,128)} %bitcast.24, bf16[16,512,128]{2,1,0:T(8,128)(2,1)} %all-to-all-done.3.mixed, bf16[4,128,192]{2,1,0:T(8,128)(2,1)} %bitcast.27, bf16[2048,192]{1,0:T(8,128)(2,1)} %pad_bitcast_fusion.turned), custom_call_target="tpu_custom_call" | custom-call | flops 402653184 | bytes 8388608 | tf_op jit(solution)/shard_map/final/pallas_call | solution.py:576
  (5 shorter events, 0.1 us)
Async XLA Ops:
  44.3 18.9 %copy-start.3 = (bf16[188,2048]{1,0:T(8,128)(2,1)S(1)}, bf16[188,2048]{1,0:T(8,128)(2,1)}, u32[]{:S(2)}) copy-start(bf16[188,2048]{1,0:T(8,128)(2,1)} %param.10) | copy-start | bytes 2310148
  44.3 45.1 %all-to-all-start.1 = ((s16[16,512,128]{2,1,0:T(8,128)(2,1)}), s16[16,512,128]{2,1,0:T(8,128)(2,1)}, u32[]{:S(2)}, u32[]{:S(2)}) async-start(s16[16,512,128]{2,1,0:T(8,128)(2,1)} %get-tuple-element.14), calls=%async_computation.1 | async-start | bytes 4194304 | tf_op jit(solution)/shard_map/all_to_all | solution.py:607
  51.1 27.0 %collective-permute-start = (bf16[32,2048]{1,0:T(8,128)(2,1)S(1)}, bf16[32,2048]{1,0:T(8,128)(2,1)S(1)}, u32[]{:S(2)}, u32[]{:S(2)}) collective-permute-start(bf16[32,2048]{1,0:T(8,128)(2,1)S(1)} %get-tuple-element.27), channel_id=1, source_target_pairs={{0,16},{16,32},{32,48},{48,64},{64,80},{80,96},{96,112},{1,17},{17... | collective-permute-start | bytes 393224 | tf_op jit(solution)/shard_map/ppermute | solution.py:603
  52.4 25.7 %collective-permute-start.1 = (bf16[32,2048]{1,0:T(8,128)(2,1)S(1)}, bf16[32,2048]{1,0:T(8,128)(2,1)S(1)}, u32[]{:S(2)}, u32[]{:S(2)}) collective-permute-start(bf16[32,2048]{1,0:T(8,128)(2,1)S(1)} %get-tuple-element.26), channel_id=1, source_target_pairs={{16,0},{32,16},{48,32},{64,48},{80,64},{96,80},{112,96},{17,1},{33... | collective-permute-start | bytes 393224 | tf_op jit(solution)/shard_map/ppermute | solution.py:603
  55.1 21.5 %collective-permute-start.2 = (bf16[16,2048]{1,0:T(8,128)(2,1)S(1)}, bf16[16,2048]{1,0:T(8,128)(2,1)S(1)}, u32[]{:S(2)}, u32[]{:S(2)}) collective-permute-start(bf16[16,2048]{1,0:T(8,128)(2,1)S(1)} %bitcast.29), channel_id=1, source_target_pairs={{0,1},{1,2},{2,3},{3,4},{4,5},{5,6},{6,7},{7,8},{8,9},{9,10},{10,1... | collective-permute-start | bytes 196616 | tf_op jit(solution)/shard_map/ppermute | solution.py:603
  58.6 18.7 %collective-permute-start.3 = (bf16[16,2048]{1,0:T(8,128)(2,1)S(1)}, bf16[16,2048]{1,0:T(8,128)(2,1)S(1)}, u32[]{:S(2)}, u32[]{:S(2)}) collective-permute-start(bf16[16,2048]{1,0:T(8,128)(2,1)S(1)} %bitcast.30), channel_id=1, source_target_pairs={{1,0},{2,1},{3,2},{4,3},{5,4},{6,5},{7,6},{8,7},{9,8},{10,9},{11,1... | collective-permute-start | bytes 196616 | tf_op jit(solution)/shard_map/ppermute | solution.py:603
  63.7 1.0 copy-start.1
  64.7 1.5 copy-start.4
  78.0 0.7 copy-start.7
  78.0 0.7 copy-start.8
  93.9 32.0 %copy-start = (bf16[512,256]{1,0:T(8,128)(2,1)S(1)}, bf16[512,256]{1,0:T(8,128)(2,1)}, u32[]{:S(2)}) copy-start(bf16[512,256]{1,0:T(8,128)(2,1)} %get-tuple-element.21.weights) | copy-start | bytes 786436
  129.3 6.7 %copy-start.12 = (bf16[16,2048]{1,0:T(8,128)(2,1)S(1)}, bf16[16,2048]{1,0:T(8,128)(2,1)}, u32[]{:S(2)}) copy-start(bf16[16,2048]{1,0:T(8,128)(2,1)} %get-tuple-element.18) | copy-start | bytes 196612
  129.3 10.1 %copy-start.11 = (bf16[16,2048]{1,0:T(8,128)(2,1)S(1)}, bf16[16,2048]{1,0:T(8,128)(2,1)}, u32[]{:S(2)}) copy-start(bf16[16,2048]{1,0:T(8,128)(2,1)} %get-tuple-element.19) | copy-start | bytes 196612
  129.3 14.7 %copy-start.10 = (bf16[32,2048]{1,0:T(8,128)(2,1)S(1)}, bf16[32,2048]{1,0:T(8,128)(2,1)}, u32[]{:S(2)}) copy-start(bf16[32,2048]{1,0:T(8,128)(2,1)} %get-tuple-element.16) | copy-start | bytes 393220
  129.3 16.0 %copy-start.9 = (bf16[32,2048]{1,0:T(8,128)(2,1)S(1)}, bf16[32,2048]{1,0:T(8,128)(2,1)}, u32[]{:S(2)}) copy-start(bf16[32,2048]{1,0:T(8,128)(2,1)} %get-tuple-element.17) | copy-start | bytes 393220
  129.4 17.4 %copy-start.2 = (bf16[188,2048]{0,1:T(8,128)(2,1)S(1)}, bf16[188,2048]{0,1:T(8,128)(2,1)}, u32[]{:S(2)}) copy-start(bf16[188,2048]{0,1:T(8,128)(2,1)} %copy-done.1) | copy-start | bytes 2310148
  129.4 48.3 %all-to-all-start.3 = ((bf16[16,512,128]{2,1,0:T(8,128)(2,1)}), bf16[16,512,128]{2,1,0:T(8,128)(2,1)}, u32[]{:S(2)}, u32[]{:S(2)}) async-start(bf16[16,512,128]{2,1,0:T(8,128)(2,1)} %mix.3), calls=%async_computation.3 | async-start | bytes 4194304 | tf_op jit(solution)/shard_map/all_to_all | solution.py:607
  136.0 26.2 %collective-permute-start.6 = (bf16[16,2048]{1,0:T(8,128)(2,1)S(1)}, bf16[16,2048]{1,0:T(8,128)(2,1)S(1)}, u32[]{:S(2)}, u32[]{:S(2)}) collective-permute-start(bf16[16,2048]{1,0:T(8,128)(2,1)S(1)} %copy-done.12), channel_id=1, source_target_pairs={{0,1},{1,2},{2,3},{3,4},{4,5},{5,6},{6,7},{7,8},{8,9},{9,10},{10,1... | collective-permute-start | bytes 196616 | tf_op jit(solution)/shard_map/ppermute | solution.py:603
  139.4 23.5 %collective-permute-start.7 = (bf16[16,2048]{1,0:T(8,128)(2,1)S(1)}, bf16[16,2048]{1,0:T(8,128)(2,1)S(1)}, u32[]{:S(2)}, u32[]{:S(2)}) collective-permute-start(bf16[16,2048]{1,0:T(8,128)(2,1)S(1)} %copy-done.11), channel_id=1, source_target_pairs={{1,0},{2,1},{3,2},{4,3},{5,4},{6,5},{7,6},{8,7},{9,8},{10,9},{11,1... | collective-permute-start | bytes 196616 | tf_op jit(solution)/shard_map/ppermute | solution.py:603
  144.0 19.6 %collective-permute-start.4 = (bf16[32,2048]{1,0:T(8,128)(2,1)S(1)}, bf16[32,2048]{1,0:T(8,128)(2,1)S(1)}, u32[]{:S(2)}, u32[]{:S(2)}) collective-permute-start(bf16[32,2048]{1,0:T(8,128)(2,1)S(1)} %copy-done.10), channel_id=1, source_target_pairs={{0,16},{16,32},{32,48},{48,64},{64,80},{80,96},{96,112},{1,17},{17... | collective-permute-start | bytes 393224 | tf_op jit(solution)/shard_map/ppermute | solution.py:603
  145.3 18.3 %collective-permute-start.5 = (bf16[32,2048]{1,0:T(8,128)(2,1)S(1)}, bf16[32,2048]{1,0:T(8,128)(2,1)S(1)}, u32[]{:S(2)}, u32[]{:S(2)}) collective-permute-start(bf16[32,2048]{1,0:T(8,128)(2,1)S(1)} %copy-done.9), channel_id=1, source_target_pairs={{16,0},{32,16},{48,32},{64,48},{80,64},{96,80},{112,96},{17,1},{33... | collective-permute-start | bytes 393224 | tf_op jit(solution)/shard_map/ppermute | solution.py:603
  163.6 0.7 copy-start.5
  163.6 0.7 copy-start.6

commit v3 on v2

--- a/solution.py
+++ b/solution.py
@@ -8,7 +8,6 @@
 from jax.sharding import PartitionSpec as P
 
 
-BLOCK_ROWS = 4
 BLOCKS = 4
 MU = 1.0
 GAMMA = 0.6
@@ -18,6 +17,8 @@
 BANDS_PAD = 192
 CODE_SCALE = 64000.0
 CODE_SHIFT = 32768.0
+SLOPE = 4096.0
+BEND = 0.125
 STEPS = 8
 AHEAD = 5
 WIDE = 2
@@ -46,12 +47,24 @@
     return (code.astype(jnp.int32).astype(F32) + CODE_SHIFT) * (1.0 / CODE_SCALE)
 
 
-def encode_float(value):
-    return value.astype(BF16)
-
-
-def decode_float(code):
-    return code.astype(F32)
+def encode_any(value):
+    code = value * (SLOPE / (1.0 + BEND * jnp.abs(value)))
+    return jnp.round(code).astype(jnp.int32).astype(jnp.int16)
+
+
+def decode_any(code):
+    real = code.astype(jnp.int32).astype(F32)
+    return real / (SLOPE - BEND * jnp.abs(real))
+
+
+def encode_positive(value):
+    code = value * (2.0 * SLOPE / (1.0 + BEND * value)) - CODE_SHIFT
+    return jnp.round(code).astype(jnp.int32).astype(jnp.int16)
+
+
+def decode_positive(code):
+    real = code.astype(jnp.int32).astype(F32) + CODE_SHIFT
+    return real / (2.0 * SLOPE - BEND * real)
 
 
 def swapped(a, b):
@@ -213,114 +226,77 @@
 
 def solve_kernel(first, *refs):
     if first:
-        obs, lib, inv, thr, z, up, down, left, right, parts, primal = refs[:11]
-        padded, base, low, back = refs[11:]
+        obs, lib, inv, thr, z, parts, primal, lifted, base, low, back = refs
     else:
-        obs, lib, inv, thr, z, up, down, left, right, old_parts, old_primal, code, parts = refs[:13]
-        padded, base, low, back, mix = refs[13:]
-    i = pl.program_id(0)
-    row = up.shape[0]
-    block = obs.shape[0]
-    peers = padded.shape[0]
-    pixels = padded.shape[1] - 2 * row
-
-    @pl.when(i == 0)
-    def _():
-        for p in range(peers):
-            lanes = slice(p * LANES, (p + 1) * LANES)
-            padded[p, :row, :] = up[:, lanes]
-            padded[p, row + pixels :, :] = down[:, lanes]
-            if first:
-                padded[p, row : row + pixels, :] = z[:, lanes]
-
-        def natural(p, carry):
-            for k in range(STEPS):
-                at = slice(k * pixels // STEPS, (k + 1) * pixels // STEPS)
-                for j, rows in enumerate(unweave(z[p, at, :].astype(F32))):
-                    to = j * block + k * block // STEPS
-                    rows = rows.reshape(-1, LANES)
-                    padded[p, row + to : row + to + rows.shape[0], :] = rows.astype(BF16)
-                for j, rows in enumerate(unweave(decode_fixed(code[p, at, :]))):
-                    to = j * block + k * block // STEPS
-                    rows = rows.reshape(-1, LANES)
-                    mix[p, to : to + rows.shape[0], :] = (GAMMA / TOTAL) * rows
-            return carry
-
-        if not first:
-            lax.fori_loop(0, peers, natural, 0)
-
-    at = pl.multiple_of(i * block, block)
-    base[...] = jnp.dot(obs[...], lib[...], preferred_element_type=F32)
+        obs, lib, inv, thr, old_parts, old_primal, code, parts, base, low, back, kept = refs
+    blocks, row, bands = obs.shape
+    count = blocks * row
+    peers = base.shape[1] // LANES
+    base[...] = jnp.dot(obs[...].reshape(count, bands), lib[...], preferred_element_type=F32)
     for p in range(peers):
         lanes = slice(p * LANES, (p + 1) * LANES)
-        value = base[:, lanes] + MU * padded[p, pl.ds(at + row, block), :].astype(F32)
-        if not first:
-            fresh = jnp.maximum(old_parts[:, lanes] + mix[p, pl.ds(at, block), :], 0.0)
-            value = value + MU * (fresh - old_primal[:, lanes])
+        if first:
+            value = base[:, lanes] + MU * z[:, :, lanes].astype(F32).reshape(count, LANES)
+        else:
+            sums = [a.reshape(row, LANES) for a in unweave(decode_fixed(code[p]))]
+            mixed = (1.0 / TOTAL) * jnp.concatenate(sums, axis=0)
+            fresh = jnp.maximum(old_parts[:, :, lanes].reshape(count, LANES) + mixed, 0.0)
+            here = fresh.astype(BF16)
+            kept[:, lanes] = here
+            dual = fresh - old_primal[:, :, lanes].reshape(count, LANES)
+            value = base[:, lanes] + MU * (here.astype(F32) + dual)
         low[:, lanes] = value.astype(BF16)
     small = times_transposed(low[...], lib[...])
     solved = jnp.dot(
         small, inv[...], precision=lax.Precision.HIGHEST, preferred_element_type=F32
     )
     back[...] = jnp.dot(solved.astype(BF16), lib[...], preferred_element_type=F32)
-    place = lax.broadcasted_iota(jnp.int32, (block, LANES), 0) % row
     for p in range(peers):
         lanes = slice(p * LANES, (p + 1) * LANES)
-        here = padded[p, pl.ds(at + row, block), :].astype(F32)
-        above = padded[p, pl.ds(at, block), :].astype(F32)
-        below = padded[p, pl.ds(at + 2 * row, block), :].astype(F32)
-
-        def edge(halo):
-            return jnp.concatenate(
-                [
-                    jnp.broadcast_to(halo[0, k : k + 1, lanes], (row, LANES))
-                    for k in range(block // row)
-                ],
-                axis=0,
+        if first:
+            here = z[:, :, lanes].astype(F32).reshape(count, LANES)
+        else:
+            here = kept[:, lanes].astype(F32)
+        unmixed = (base[:, lanes] + MU * here - back[:, lanes]) / MU
+        made = unmixed * (1.0 / TOTAL) - thr[:, lanes]
+        parts[:, :, lanes] = made.reshape(blocks, row, LANES)
+        if first:
+            primal[:, :, lanes] = unmixed.reshape(blocks, row, LANES)
+            lifted[p] = encode_any(
+                weave([halves(made[j * row : (j + 1) * row]) for j in range(blocks)])
             )
 
-        before = jnp.where(place == 0, edge(left), pltpu.roll(here, 1, 0))
-        after = jnp.where(place == row - 1, edge(right), pltpu.roll(here, block - 1, 0))
-        spatial = 0.25 * (above + below + before + after)
-        unmixed = (base[:, lanes] + MU * here - back[:, lanes]) / MU
-        if first:
-            primal[:, lanes] = unmixed
-        parts[:, lanes] = (unmixed + ETA * spatial) * (1.0 / TOTAL) - thr[:, lanes]
-
-
-def solve(first, obs, lib, inv, thr, z, halos, carried=()):
-    pixels = obs.shape[0]
+
+def solve(first, row, obs, lib, inv, thr, carried):
+    pixels, bands = obs.shape
     atoms = lib.shape[1]
     peers = atoms // LANES
-    up, down, left, right = halos
-    row = up.shape[0]
-    block = BLOCK_ROWS * row
-    steps = pixels // block
+    block = pixels // BLOCKS
+    count = BLOCKS * row
     whole = lambda a: pl.BlockSpec(a.shape, lambda i, n=a.ndim: (0,) * n)
-    tile = pl.BlockSpec((block, atoms), lambda i: (i, 0))
-    side = pl.BlockSpec((1, BLOCK_ROWS, atoms), lambda i: (i, 0, 0))
-    full = jax.ShapeDtypeStruct((pixels, atoms), F32)
+    tile = pl.BlockSpec((BLOCKS, row, atoms), lambda i: (0, i, 0))
+    piece = pl.BlockSpec((peers, count, LANES), lambda i: (0, i, 0))
+    full = pltpu.HBM((BLOCKS, block, atoms), F32)
+    sent = pltpu.HBM((peers, pixels, LANES), jnp.int16)
     return pl.pallas_call(
         functools.partial(solve_kernel, first),
-        grid=(steps,),
+        grid=(block // row,),
         in_specs=[
-            pl.BlockSpec((block, obs.shape[1]), lambda i: (i, 0)),
-            whole(lib), whole(inv), whole(thr), whole(z), whole(up), whole(down), side, side,
+            pl.BlockSpec((BLOCKS, row, bands), lambda i: (0, i, 0)), whole(lib), whole(inv), whole(thr)
         ]
-        + ([] if first else [tile, tile, whole(carried[2])]),
-        out_specs=[tile, tile] if first else tile,
-        out_shape=[full, full] if first else full,
+        + ([tile] if first else [tile, tile, piece]),
+        out_specs=[tile, tile, piece] if first else tile,
+        out_shape=[full, full, sent] if first else full,
         scratch_shapes=[
-            pltpu.VMEM((peers, pixels + 2 * row, LANES), BF16),
-            pltpu.VMEM((block, atoms), F32),
-            pltpu.VMEM((block, atoms), BF16),
-            pltpu.VMEM((block, atoms), F32),
+            pltpu.VMEM((count, atoms), F32),
+            pltpu.VMEM((count, atoms), BF16),
+            pltpu.VMEM((count, atoms), F32),
         ]
-        + ([] if first else [pltpu.VMEM((peers, pixels, LANES), F32)]),
+        + ([] if first else [pltpu.VMEM((count, atoms), BF16)]),
+        compiler_params=pltpu.CompilerParams(vmem_limit_bytes=63 * MIB),
         cost_estimate=cost(6 * pixels * atoms * BANDS_PAD, 16 * pixels * atoms),
-        compiler_params=pltpu.CompilerParams(vmem_limit_bytes=63 * MIB),
         name="solve_first" if first else "solve_second",
-    )(obs, lib, inv, thr, z, up, down, left, right, *carried)
+    )(obs.reshape(BLOCKS, block, bands), lib, inv, thr, *carried)
 
 
 def weights_of(tables):
@@ -338,165 +314,169 @@
     return jnp.where(rows % 4 == cols % 4, wide, 0.0).astype(BF16)
 
 
-def mix_steps(encode, weights, z, out, made, go):
+def beside(z, above, below, g, across):
+    peers, pixels, _ = z.shape
+    groups = pixels // 16
+
+    def tile(ref, k):
+        return ref[:, k * 16 : (k + 1) * 16, :].astype(F32).reshape(peers, 2, 8, LANES)
+
+    def turned(a, by):
+        return pltpu.roll(a.reshape(2 * peers, 8, LANES), by % 8, 1).reshape(a.shape)
+
+    def part(ref, k):
+        rows = ref[:, k * 8 : (k + 1) * 8, :].astype(F32)
+        return pltpu.roll(rows, 4, 1).reshape(peers, 1, 8, LANES)
+
+    here = tile(z, g)
+    spot = lax.broadcasted_iota(jnp.int32, here.shape, 2)
+    pixel = spot % 4
+    none = jnp.zeros((1, 2, 8, LANES), F32)
+    if g % across:
+        before = tile(z, g - 1)
+    else:
+        before = jnp.concatenate([none, tile(z, g + across - 1)[:-1]], axis=0)
+    if g % across < across - 1:
+        after = tile(z, g + 1)
+    else:
+        after = jnp.concatenate([tile(z, g - across + 1)[1:], none], axis=0)
+    left = jnp.where(pixel == 0, turned(before, -3), turned(here, 1))
+    right = jnp.where(pixel == 3, turned(after, 3), turned(here, -1))
+    if g >= across:
+        up = tile(z, g - across)
+    else:
+        same = turned(tile(z, groups - across + g), 4)
+        halo = part(above, g)
+        up = jnp.where(spot < 4, jnp.concatenate([halo, same[:, :1]], axis=1), same)
+    if g < groups - across:
+        down = tile(z, g + across)
+    else:
+        same = turned(tile(z, g - groups + across), 4)
+        halo = part(below, g - groups + across)
+        down = jnp.where(spot < 4, same, jnp.concatenate([same[:, 1:], halo], axis=1))
+    return (up + down + left + right).reshape(peers, 16, LANES)
+
+
+def mix_kernel(
+    encode, first, across, *refs
+):
+    if first:
+        strip, above_at, below_at, out, table, z, above, below, made, tail, weights, come, go, other = refs
+        quarters = []
+    else:
+        quarters, refs = refs[:4], refs[4:]
+        above_at, below_at, table, out, z, above, below, made, weights, come, go, other = refs
     peers, pixels, _ = made.shape
     size = peers * 16
     step = pixels // STEPS
-
-    def rows_of(i):
-        return pl.ds(pl.multiple_of(i * step, step), step)
-
-    def one(i, carry):
-        for k in range(0, step, 32):
-            at = i * step + k
-            tiles = [
-                z[:, pl.ds(pl.multiple_of(at + d, 16), 16), :].reshape(size, LANES) for d in (0, 16)
-            ]
+    copies = [
+        pltpu.make_async_copy(above_at, above, come.at[0]),
+        pltpu.make_async_copy(below_at, below, come.at[1]),
+    ]
+    for k, quarter in enumerate(quarters):
+        rows = pl.ds(k * quarter.shape[1], quarter.shape[1])
+        copies.append(pltpu.make_async_copy(quarter, z.at[:, rows, :], come.at[2 + k]))
+    if first:
+        copies.append(pltpu.make_async_copy(strip.at[:, pl.ds(0, pixels), :], z, come.at[2]))
+        copies.append(
+            pltpu.make_async_copy(strip.at[:, pl.ds(pixels, TABLE_ROWS), :], tail, other.at[0])
+        )
+    else:
+        copies.append(pltpu.make_async_copy(table, weights, other.at[0]))
+    for copy in copies:
+        copy.start()
+    for copy in copies:
+        copy.wait()
+    if first:
+        weights[...] = weights_of(tail[...].reshape(-1, LANES))
+        keep = pltpu.make_async_copy(weights, table, other.at[1])
+        keep.start()
+    writes = []
+    for i in range(STEPS):
+        rows = pl.ds(i * step, step)
+        writes.append(pltpu.make_async_copy(made.at[:, rows, :], out.at[:, rows, :], go.at[i]))
+        for at in range(i * step, (i + 1) * step, 32):
+            tiles = [z[:, at + d : at + d + 16, :].reshape(size, LANES) for d in (0, 16)]
             both = jnp.dot(
                 weights[...], jnp.concatenate(tiles, axis=1), preferred_element_type=F32
             )
-            coded = encode(both[:size] + both[size:])
+            sums = both[:size] + both[size:]
             for d in (0, 1):
-                made[:, pl.ds(pl.multiple_of(at + 16 * d, 16), 16), :] = coded[
-                    :, d * LANES : (d + 1) * LANES
-                ].reshape(peers, 16, LANES)
-        rows = rows_of(i)
-        pltpu.make_async_copy(made.at[:, rows, :], out.at[:, rows, :], go.at[i]).start()
-        return carry
-
-    lax.fori_loop(0, STEPS, one, 0)
-    for i in range(STEPS):
-        rows = pl.ds(i * step, step)
-        pltpu.make_async_copy(made.at[:, rows, :], out.at[:, rows, :], go.at[i]).wait()
-
-
-def mix_first_kernel(encode, z, out, table, made, weights, go, kept):
-    pixels = made.shape[1]
-    weights[...] = weights_of(z[:, pixels:, :].reshape(-1, LANES))
-    keep = pltpu.make_async_copy(weights, table, kept)
-    keep.start()
-    mix_steps(encode, weights, z, out, made, go)
-    keep.wait()
-
-
-def mix_second_kernel(encode, weights, z, out, made, go):
-    mix_steps(encode, weights, z, out, made, go)
-
-
-def mix(encode, dtype, z, weights=None):
-    peers = z.shape[0]
-    pixels = z.shape[1] // LANES * LANES
+                averaged = sums[:, d * LANES : (d + 1) * LANES].reshape(peers, 16, LANES)
+                around = beside(z, above, below, at // 16 + d, across)
+                made[:, at + 16 * d : at + 16 * d + 16, :] = encode(
+                    GAMMA * averaged + (0.25 * ETA) * around
+                )
+        writes[i].start()
+    for copy in writes:
+        copy.wait()
+    if first:
+        keep.wait()
+
+
+def mix(encode, row, strip, above, below, weights=None):
+    first = weights is None
+    strips = (strip,) if first else strip
+    peers, rows, _ = strips[0].shape
+    pixels = rows - TABLE_ROWS if first else 4 * rows
     size = peers * 16
     hbm = pl.BlockSpec(memory_space=pltpu.HBM)
-    vmem = pl.BlockSpec(memory_space=pltpu.VMEM)
-    shape = pltpu.HBM((peers, pixels, LANES), dtype)
-    made = pltpu.VMEM((peers, pixels, LANES), dtype)
-    go = pltpu.SemaphoreType.DMA((STEPS,))
-    first = weights is None
+    shape = pltpu.HBM((peers, pixels, LANES), jnp.int16)
+    edge = pltpu.VMEM(above.shape, BF16)
     return pl.pallas_call(
-        functools.partial(mix_first_kernel if first else mix_second_kernel, encode),
-        in_specs=[vmem] if first else [vmem, vmem],
+        functools.partial(mix_kernel, encode, first, row // 4),
+        in_specs=[hbm] * (len(strips) + (2 if first else 3)),
         out_specs=[hbm, hbm] if first else hbm,
         out_shape=[shape, pltpu.HBM((2 * size, size), BF16)] if first else shape,
-        scratch_shapes=[made, pltpu.VMEM((2 * size, size), BF16), go, pltpu.SemaphoreType.DMA]
-        if first
-        else [made, go],
-        compiler_params=pltpu.CompilerParams(vmem_limit_bytes=48 * MIB),
-        cost_estimate=cost(4 * size * pixels // 16 * LANES * size, 4 * peers * pixels * LANES),
-        name="mix",
-    )(*(() if first else (weights,)), z)
-
-
-def fresh_kernel(
-    parts, mixed, out, top_at, bottom_at, left_at, right_at,
-    held, code, made, top, bottom, side, left, right, come, came, go, gone,
-):
-    blocks, block, _ = held.shape
-    peers = made.shape[0]
-    step = block // STEPS
-    row = top.shape[0]
-    reads, writes = [], []
-    for i in range(STEPS):
-        at = pl.ds(i * step, step)
-        woven = pl.ds(i * step * blocks, step * blocks)
-        reads.append(
-            (
-                pltpu.make_async_copy(parts.at[:, at, :], held.at[:, at, :], come.at[i]),
-                pltpu.make_async_copy(mixed.at[:, woven, :], code.at[:, woven, :], came.at[i]),
-            )
-        )
-        writes.append(pltpu.make_async_copy(made.at[:, woven, :], out.at[:, woven, :], go.at[i]))
-    edges = ((top, top_at), (bottom, bottom_at), (left, left_at), (right, right_at))
-    edges = [pltpu.make_async_copy(a, b, gone.at[k]) for k, (a, b) in enumerate(edges)]
-    for pair in reads[:AHEAD]:
-        for copy in pair:
-            copy.start()
-    for i in range(STEPS):
-        for copy in reads[i]:
-            copy.wait()
-        if i + AHEAD < STEPS:
-            for copy in reads[i + AHEAD]:
-                copy.start()
-        first = i * step
-        at = slice(first, first + step)
-        woven = slice(first * blocks, (first + step) * blocks)
-        for p in range(peers):
-            lanes = slice(p * LANES, (p + 1) * LANES)
-            sums = unweave(decode_fixed(code[p, woven, :]))
-            values = [
-                jnp.maximum(halves(held[j, at, lanes]) + (GAMMA / TOTAL) * sums[j], 0.0)
-                for j in range(blocks)
-            ]
-            made[p, woven, :] = weave(values).astype(BF16)
-            if first < row:
-                top[at, lanes] = values[0].reshape(step, LANES).astype(BF16)
-            if first >= block - row:
-                into = slice(first - block + row, first - block + row + step)
-                bottom[into, lanes] = values[-1].reshape(step, LANES).astype(BF16)
-            for j in range(blocks):
-                line = j * BLOCK_ROWS + first // row
-                if first % row == 0:
-                    side[0, line : line + 1, lanes] = values[j][0, :1, :]
-                if (first + step) % row == 0:
-                    side[1, line : line + 1, lanes] = values[j][-1, 7:, :]
-        writes[i].start()
-    left[...] = side[0].astype(BF16)
-    right[...] = side[1].astype(BF16)
-    for copy in edges:
-        copy.start()
-    for copy in edges + writes:
-        copy.wait()
-
-
-def fresh_pieces(parts, mixed, tile_rows, tile_cols):
-    peers, pixels, _ = mixed.shape
-    atoms = parts.shape[1]
-    hbm = pl.BlockSpec(memory_space=pltpu.HBM)
-    shaped = parts.reshape(BLOCKS, pixels // BLOCKS, atoms)
-    ends = ((tile_cols, atoms), (tile_cols, atoms), (tile_rows, atoms), (tile_rows, atoms))
-    return pl.pallas_call(
-        fresh_kernel,
-        in_specs=[hbm, hbm],
-        out_specs=[hbm] * 5,
-        out_shape=[pltpu.HBM((peers, pixels, LANES), BF16)] + [pltpu.HBM(a, BF16) for a in ends],
         scratch_shapes=[
-            pltpu.VMEM(shaped.shape, F32),
-            pltpu.VMEM((peers, pixels, LANES), mixed.dtype),
-            pltpu.VMEM((peers, pixels, LANES), BF16),
-            pltpu.VMEM(ends[0], BF16),
-            pltpu.VMEM(ends[1], BF16),
-            pltpu.VMEM((2, tile_rows, atoms), F32),
-            pltpu.VMEM(ends[2], BF16),
-            pltpu.VMEM(ends[3], BF16),
+            pltpu.VMEM((peers, pixels, LANES), BF16), edge, edge,
+            pltpu.VMEM((peers, pixels, LANES), jnp.int16),
+        ]
+        + ([pltpu.VMEM((peers, TABLE_ROWS, LANES), BF16)] if first else [])
+        + [
+            pltpu.VMEM((2 * size, size), BF16),
+            pltpu.SemaphoreType.DMA((2 + len(strips),)),
             pltpu.SemaphoreType.DMA((STEPS,)),
-            pltpu.SemaphoreType.DMA((STEPS,)),
-            pltpu.SemaphoreType.DMA((STEPS,)),
-            pltpu.SemaphoreType.DMA((4,)),
+            pltpu.SemaphoreType.DMA((2,)),
         ],
         compiler_params=pltpu.CompilerParams(vmem_limit_bytes=63 * MIB),
-        cost_estimate=cost(4 * pixels * atoms, 8 * pixels * atoms),
-        name="fresh",
-    )(shaped, mixed)
+        cost_estimate=cost(4 * size * pixels // 16 * LANES * size, 4 * peers * pixels * LANES),
+        name="mix_first" if first else "mix_second",
+    )(*strips, above, below, *(() if first else (weights,)))
+
+
+def half_of(rows, h):
+    return rows.reshape(-1, 2, 8, LANES)[:, h].reshape(-1, LANES)
+
+
+def advance_kernel(strip_a, sums_a, strip_b, sums_b, out_a, out_b, *ends):
+    for q in range(strip_a.shape[0]):
+        for k, (strip, sums, out) in enumerate(
+            ((strip_a, sums_a, out_a), (strip_b, sums_b, out_b))
+        ):
+            value = decode_any(strip[q]) + (1.0 / TOTAL) * decode_fixed(sums[q])
+            value = jnp.maximum(value, 0.0)
+            out[q] = value.astype(BF16)
+            if ends:
+                ends[k][q] = half_of(value, k).astype(BF16)
+
+
+def advance(strip, sums, quarters, edge, with_ends):
+    peers, pixels, _ = strip.shape
+    step = 4
+    specs = [pl.BlockSpec((step, edge, LANES), lambda i, k=k: (i, k, 0)) for k in quarters]
+    whole = lambda n: pl.BlockSpec((step, n, LANES), lambda i: (i, 0, 0))
+    sizes = [edge, edge] + ([edge // 2, edge // 2] if with_ends else [])
+    return pl.pallas_call(
+        advance_kernel,
+        grid=(peers // step,),
+        in_specs=[specs[0], specs[0], specs[1], specs[1]],
+        out_specs=[whole(n) for n in sizes],
+        out_shape=[pltpu.HBM((peers, n, LANES), BF16) for n in sizes],
+        compiler_params=pltpu.CompilerParams(vmem_limit_bytes=63 * MIB),
+        cost_estimate=cost(8 * peers * pixels * LANES, 3 * peers * pixels * LANES),
+        name="advance_ends" if with_ends else "advance_middle",
+    )(strip, sums, strip, sums)
 
 
 def final_kernel(
@@ -538,9 +518,9 @@
         woven = slice(i * step * blocks, (i + 1) * step * blocks)
         for p in range(mixed.shape[0]):
             lanes = slice(p * LANES, (p + 1) * LANES)
-            sums = unweave(decode_float(code[p, woven, :]))
+            sums = unweave(decode_positive(code[p, woven, :]))
             for j in range(blocks):
-                value = halves(held[j, at, lanes]) + (GAMMA / TOTAL) * sums[j]
+                value = halves(held[j, at, lanes]) + (1.0 / TOTAL) * sums[j]
                 made[j, at, lanes] = jnp.maximum(value, 0.0).reshape(step, LANES).astype(BF16)
         writes[i].start()
         if i == 0:
@@ -568,9 +548,8 @@
 
 def final(parts, mixed, obs, turned, bands):
     peers, pixels, _ = mixed.shape
-    atoms = parts.shape[1]
-    by_block = lambda a: a.reshape(BLOCKS, pixels // BLOCKS, a.shape[1])
-    parts, obs = by_block(parts), by_block(obs)
+    atoms = parts.shape[2]
+    obs = obs.reshape(BLOCKS, pixels // BLOCKS, obs.shape[1])
     hbm = pl.BlockSpec(memory_space=pltpu.HBM)
     left = (BLOCKS, pixels // BLOCKS, bands)
     return pl.pallas_call(
@@ -607,13 +586,16 @@
     return lax.all_to_all(pieces, "col", 0, 0, tiled=True)
 
 
-def halos_of(top, bottom, left, right):
-    up = shifted(bottom, "row", True)
-    down = shifted(top, "row", False)
-    before = shifted(right, "col", True)
-    after = shifted(left, "col", False)
-    by_block = lambda a: a.astype(F32).reshape(BLOCKS, BLOCK_ROWS, -1)
-    return up, down, by_block(before), by_block(after)
+def strip_ends(strip, pixels, edge):
+    tiles = strip[:, :pixels].reshape(strip.shape[0], pixels // 16, 2, 8, LANES)
+    rows = lambda a: a.reshape(strip.shape[0], edge // 2, LANES)
+    return rows(tiles[:, : edge // 16, 0]), rows(tiles[:, (pixels - edge) // 16 :, 1])
+
+
+def strip_halos(first, last):
+    above = shifted(last, "row", True)
+    below = shifted(first, "row", False)
+    return above, below
 
 
 def local(
@@ -630,21 +612,25 @@
         match_peer, match_slot, match_count, match_weight, wanted,
     )
     strip = exchanged(pieces)
-    halos = halos_of(warm[0], warm[-1], warm[:, 0], warm[:, -1])
     lib = jnp.pad(library, ((0, BANDS_PAD - bands), (0, 0)))
     obs = jnp.pad(observed.reshape(pixels, bands), ((0, 0), (0, BANDS_PAD - bands)))
     inv = gram_inverse(lib)
     thr = threshold[None, :]
 
-    sums, weights = mix(encode_fixed, jnp.int16, strip)
+    by_block = flat.reshape(BLOCKS, pixels // BLOCKS, atoms)
+    parts, primal, lifted = solve(True, tile_cols, obs, lib, inv, thr, (by_block,))
+    strip_parts = exchanged(lifted)
+    edge = BLOCKS * tile_cols
+    above, below = strip_halos(*strip_ends(strip, pixels, edge))
+    sums, weights = mix(encode_fixed, tile_cols, strip, above, below)
     mixed = exchanged(sums)
-    parts, primal = solve(True, obs, lib, inv, thr, flat, halos)
-    pieces, *edges = fresh_pieces(parts, mixed, tile_rows, tile_cols)
-    strip = exchanged(pieces)
-    halos = halos_of(*edges)
-    sums = mix(encode_float, BF16, strip, weights)
+    first, last, *ends = advance(strip_parts, sums, (0, 3), edge, True)
+    above, below = strip_halos(*ends)
+    middle = advance(strip_parts, sums, (1, 2), edge, False)
+    strip = (first, *middle, last)
+    sums = mix(encode_positive, tile_cols, strip, above, below, weights)
     mixed_again = exchanged(sums)
-    parts = solve(False, obs, lib, inv, thr, pieces, halos, (parts, primal, mixed))
+    parts = solve(False, tile_cols, obs, lib, inv, thr, (parts, primal, mixed))
     abundance, misfit = final(parts, mixed_again, obs, lib.T, bands)
     return (
         abundance.reshape(tile_rows, tile_cols, atoms),

time: 185 us -> 147 us (0.79)
  the two profiles are of different devices: /device:TPU:2 before, /device:TPU:0 now
where the time goes in v3:
time: 147 us
  Pallas kernels  57.1 us (39%)
  waiting for transfers between devices  53.5 us (36%)
  starting transfers between devices  26.9 us (18%)
  local copies, waits for them, and re-layouts  8.24 us (6%)
    all_to_all x4, waiting for transfers between devices, exchanged(): return lax.all_to_all(pieces, 'col', 0, 0, tiled=True)  49.5 us
    all_to_all x4, starting transfers between devices, exchanged(): return lax.all_to_all(pieces, 'col', 0, 0, tiled=True)  21.5 us
    pallas_call x2, Pallas kernels, solve(): pl.pallas_call(functools.partial(solve_kernel, first), grid=(block // row...  19.3 us
    pallas_call x2, Pallas kernels, mix(): pl.pallas_call(functools.partial(mix_kernel, encode, first, row // 4), in...  12.8 us
    pallas_call x2, Pallas kernels, advance(): pl.pallas_call(advance_kernel, grid=(peers // step,), in_specs=[specs[0],...  8.16 us
    pallas_call x1, Pallas kernels, gram_inverse(): pl.pallas_call(inverse_kernel, out_shape=jax.ShapeDtypeStruct((size, size...  7.67 us
    pallas_call x1, Pallas kernels, final(): pl.pallas_call(final_kernel, in_specs=[hbm, hbm, hbm, hbm], out_specs=[hb...  5.57 us
    ppermute x4, starting transfers between devices, shifted(): lax.ppermute(array, axis, pairs if up else [(b, a) for a, b in pairs])  5.38 us
  transfers between devices with their start and end apart: 8, of which 5 were waited for; matrix products, arithmetic and copies ran while one was open for 4% of the time, Pallas kernels for 33%

profile of v3, /device:TPU:0, one launch (start us, length us, event | category | flops | bytes accessed | tf_op | source)
XLA Modules:
  0.0 146.7 jit_solution(12254680150022202044)
XLA Ops:
  0.6 3.5 %spread.1 = bf16[16,528,128]{2,1,0:T(8,128)(2,1)} custom-call(s32[1,2,16]{2,1,0:T(2,128)} %bitcast.28, s32[4,1,8]{2,1,0:T(1,128)} %peer_at.1, s32[4,1,8]{2,1,0:T(1,128)} %slot_at.1, s32[1,4]{1,0:T(1,128)} %bitcast.29, f32[4,1,8]{2,1,0:T(1,128)} %weight_at.1, bf16[4,128,2048]{2,1,0:T(8,128)(2,1)} %bitcast.23), custom_call_target="tpu_custom_call" | custom-call | flops 1048576 | bytes 4194304 | tf_op jit(solution)/shard_map/spread/pallas_call | solution.py:167
  4.2 0.0 copy-start.2
  4.2 8.2 %all-to-all-start = ((bf16[16,528,128]{2,1,0:T(8,128)(2,1)}), bf16[16,528,128]{2,1,0:T(8,128)(2,1)}, u32[]{:S(2)}, u32[]{:S(2)}) async-start(bf16[16,528,128]{2,1,0:T(8,128)(2,1)} %spread.1), calls=%async_computation | async-start | bytes 4325376 | tf_op jit(solution)/shard_map/all_to_all | solution.py:586
  12.4 0.0 copy-done.2
  12.4 0.5 copy.11
  12.9 0.0 copy-start
  12.9 1.0 copy-done
  13.9 0.0 copy-start.5
  13.9 0.5 copy.19
  14.4 1.0 pad.9.clone.lib_ref.refs_1_
  15.4 0.0 copy-done.5
  15.4 0.7 pad.8
  16.1 7.7 %inverse.1.refs_2_ = f32[192,192]{1,0:T(8,128)} custom-call(bf16[192,2048]{1,0:T(8,128)(2,1)} %pad.9.clone.lib_ref.refs_1_), custom_call_target="tpu_custom_call" | custom-call | flops 849346560 | bytes 147456 | tf_op jit(solution)/shard_map/inverse/pallas_call | solution.py:218
  23.8 9.5 %solve_first.1 = (f32[4,128,2048]{2,1,0:T(8,128)}, f32[4,128,2048]{2,1,0:T(8,128)}, s16[16,512,128]{2,1,0:T(8,128)(2,1)}) custom-call(bf16[4,128,192]{2,1,0:T(8,128)(2,1)} %bitcast.20, bf16[192,2048]{1,0:T(8,128)(2,1)} %pad.9.clone.lib_ref.refs_1_, f32[192,192]{1,0:T(8,128)} %inverse.1.refs_2_, f32[1,2048]{1,0:T(1,128)} %bitcast.26, ...), custom_call_target="tpu_custom_call" | custom-call | flops 1207959552 | bytes 16777216 | tf_op jit(solution)/shard_map/solve_first/pallas_call | solution.py:281
  33.3 10.4 %all-to-all-done.refs_0_ = bf16[16,528,128]{2,1,0:T(8,128)(2,1)} async-done(((bf16[16,528,128]{2,1,0:T(8,128)(2,1)}), bf16[16,528,128]{2,1,0:T(8,128)(2,1)}, u32[]{:S(2)}, u32[]{:S(2)}) %all-to-all-start) | async-done | bytes 2162720 | tf_op jit(solution)/shard_map/all_to_all | solution.py:586
  43.7 4.4 %all-to-all-start.2 = ((s16[16,512,128]{2,1,0:T(8,128)(2,1)}), s16[16,512,128]{2,1,0:T(8,128)(2,1)}, u32[]{:S(2)}, u32[]{:S(2)}) async-start(s16[16,512,128]{2,1,0:T(8,128)(2,1)} %get-tuple-element.18), calls=%async_computation.2 | async-start | bytes 4194304 | tf_op jit(solution)/shard_map/all_to_all | solution.py:586
  48.1 1.7 %slice.12 = bf16[16,512,128]{2,1,0:T(8,128)(2,1)S(1)} slice(bf16[16,528,128]{2,1,0:T(8,128)(2,1)} %all-to-all-done.refs_0_), slice={[0:16], [0:512], [0:128]} | slice | bytes 4194304 | tf_op jit(solution)/shard_map/slice | solution.py:590
  49.9 0.1 slice_bitcast_fusion
  50.0 1.3 collective-permute-start
  51.3 1.3 collective-permute-start.1
  52.6 0.0 collective-permute-done.refs_1_
  52.6 0.0 copy-start.6
  52.6 3.9 %collective-permute-done.1.refs_2_ = bf16[16,64,128]{2,1,0:T(8,128)(2,1)S(1)} collective-permute-done((bf16[16,64,128]{2,1,0:T(8,128)(2,1)S(1)}, bf16[16,64,128]{2,1,0:T(8,128)(2,1)S(1)}, u32[]{:S(2)}, u32[]{:S(2)}) %collective-permute-start.1) | collective-permute-done | bytes 262176 | tf_op jit(solution)/shard_map/ppermute | solution.py:582
  56.5 0.0 copy-done.6
  56.6 0.0 copy-start.7
  56.6 0.7 copy-done.7
  57.3 6.2 %mix_first.1 = (s16[16,512,128]{2,1,0:T(8,128)(2,1)}, bf16[512,256]{1,0:T(8,128)(2,1)}) custom-call(bf16[16,528,128]{2,1,0:T(8,128)(2,1)} %all-to-all-done.refs_0_, bf16[16,64,128]{2,1,0:T(8,128)(2,1)} %copy-done.6, bf16[16,64,128]{2,1,0:T(8,128)(2,1)} %copy-done.7), custom_call_target="tpu_custom_call" | custom-call | flops 1073741824 | bytes 4194304 | tf_op jit(solution)/shard_map/mix_first/pallas_call | solution.py:426
  63.5 12.4 %all-to-all-done.2.strip_a.strip_b = s16[16,512,128]{2,1,0:T(8,128)(2,1)} async-done(((s16[16,512,128]{2,1,0:T(8,128)(2,1)}), s16[16,512,128]{2,1,0:T(8,128)(2,1)}, u32[]{:S(2)}, u32[]{:S(2)}) %all-to-all-start.2) | async-done | bytes 2097184 | tf_op jit(solution)/shard_map/all_to_all | solution.py:586
  75.9 4.4 %all-to-all-start.1 = ((s16[16,512,128]{2,1,0:T(8,128)(2,1)}), s16[16,512,128]{2,1,0:T(8,128)(2,1)}, u32[]{:S(2)}, u32[]{:S(2)}) async-start(s16[16,512,128]{2,1,0:T(8,128)(2,1)} %get-tuple-element.17.sums_a.sums_b), calls=%async_computation.1 | async-start | bytes 4194304 | tf_op jit(solution)/shard_map/all_to_all | solution.py:586
  80.3 4.1 %advance_ends.1 = (bf16[16,128,128]{2,1,0:T(8,128)(2,1)}, bf16[16,128,128]{2,1,0:T(8,128)(2,1)}, bf16[16,64,128]{2,1,0:T(8,128)(2,1)}, bf16[16,64,128]{2,1,0:T(8,128)(2,1)}) custom-call(s16[16,512,128]{2,1,0:T(8,128)(2,1)} %all-to-all-done.2.strip_a.strip_b, s16[16,512,128]{2,1,0:T(8,128)(2,1)} %get-tuple-element.17.sums_a.sums_b, ...), custom_call_target="tpu_custom_call" | custom-call | flops 8388608 | bytes 3145728 | tf_op jit(solution)/shard_map/advance_ends/pallas_call | solution.py:470
  84.4 1.3 collective-permute-start.2
  85.8 1.5 %collective-permute-start.3 = (bf16[16,64,128]{2,1,0:T(8,128)(2,1)}, bf16[16,64,128]{2,1,0:T(8,128)(2,1)S(1)}, u32[]{:S(2)}, u32[]{:S(2)}) collective-permute-start(bf16[16,64,128]{2,1,0:T(8,128)(2,1)} %get-tuple-element.24), channel_id=1, source_target_pairs={{16,0},{32,16},{48,32},{64,48},{80,64},{96,80},{112,96},{17,1},{33... | collective-permute-start | bytes 786440 | tf_op jit(solution)/shard_map/ppermute | solution.py:582
  87.2 4.0 %advance_middle.1 = (bf16[16,128,128]{2,1,0:T(8,128)(2,1)}, bf16[16,128,128]{2,1,0:T(8,128)(2,1)}) custom-call(s16[16,512,128]{2,1,0:T(8,128)(2,1)} %all-to-all-done.2.strip_a.strip_b, s16[16,512,128]{2,1,0:T(8,128)(2,1)} %get-tuple-element.17.sums_a.sums_b, s16[16,512,128]{2,1,0:T(8,128)(2,1)} %all-to-all-done.2.strip_a.strip_b, ...), custom_call_target="tpu_custom_call" | custom-call | flops 8388608 | bytes 3145728 | tf_op jit(solution)/shard_map/advance_middle/pallas_call | solution.py:470
  91.3 0.0 collective-permute-done.2.refs_4_
  91.3 0.0 copy-start.3
  91.3 0.0 collective-permute-done.3.refs_5_
  91.3 0.0 copy-start.4
  91.3 0.7 copy-done.3
  92.0 0.1 copy-done.4
  92.1 6.6 %mix_second.1 = s16[16,512,128]{2,1,0:T(8,128)(2,1)} custom-call(bf16[16,128,128]{2,1,0:T(8,128)(2,1)} %get-tuple-element.19.refs_0_, bf16[16,128,128]{2,1,0:T(8,128)(2,1)} %get-tuple-element.20.refs_1_, bf16[16,128,128]{2,1,0:T(8,128)(2,1)} %get-tuple-element.21.refs_2_, bf16[16,128,128]{2,1,0:T(8,128)(2,1)} %get-tuple-element.22.refs_3_, ...), custom_call_target="tpu_custom_call" | custom-call | flops 1073741824 | bytes 4194304 | tf_op jit(solution)/shard_map/mix_second/pallas_call | solution.py:426
  98.7 0.0 copy-start.1
  98.7 9.3 %all-to-all-done.1.refs_6_ = s16[16,512,128]{2,1,0:T(8,128)(2,1)} async-done(((s16[16,512,128]{2,1,0:T(8,128)(2,1)}), s16[16,512,128]{2,1,0:T(8,128)(2,1)}, u32[]{:S(2)}, u32[]{:S(2)}) %all-to-all-start.1) | async-done | bytes 2097184 | tf_op jit(solution)/shard_map/all_to_all | solution.py:586
  108.0 4.4 %all-to-all-start.3 = ((s16[16,512,128]{2,1,0:T(8,128)(2,1)}), s16[16,512,128]{2,1,0:T(8,128)(2,1)}, u32[]{:S(2)}, u32[]{:S(2)}) async-start(s16[16,512,128]{2,1,0:T(8,128)(2,1)} %mix_second.1), calls=%async_computation.3 | async-start | bytes 4194304 | tf_op jit(solution)/shard_map/all_to_all | solution.py:586
  112.5 0.0 copy-done.1
  112.5 1.2 pad_bitcast_fusion.turned
  113.7 9.8 %solve_second.1.parts = f32[4,128,2048]{2,1,0:T(8,128)} custom-call(bf16[4,128,192]{2,1,0:T(8,128)(2,1)} %bitcast.21, bf16[192,2048]{1,0:T(8,128)(2,1)} %pad.9.clone.lib_ref.refs_1_, f32[192,192]{1,0:T(8,128)} %inverse.1.refs_2_, f32[1,2048]{1,0:T(1,128)} %bitcast.27, f32[4,128,2048]{2,1,0:T(8,128)} %get-tuple-element.15.refs_4_, ...), custom_call_target="tpu_custom_call" | custom-call | flops 1207959552 | bytes 16777216 | tf_op jit(solution)/shard_map/solve_second/pallas_call | solution.py:281
  123.5 17.4 %all-to-all-done.3.mixed = s16[16,512,128]{2,1,0:T(8,128)(2,1)} async-done(((s16[16,512,128]{2,1,0:T(8,128)(2,1)}), s16[16,512,128]{2,1,0:T(8,128)(2,1)}, u32[]{:S(2)}, u32[]{:S(2)}) %all-to-all-start.3) | async-done | bytes 2097184 | tf_op jit(solution)/shard_map/all_to_all | solution.py:586
  140.9 5.6 %final.1 = (bf16[4,128,2048]{2,1,0:T(8,128)(2,1)}, f32[4,128,188]{2,1,0:T(8,128)}) custom-call(f32[4,128,2048]{2,1,0:T(8,128)} %solve_second.1.parts, s16[16,512,128]{2,1,0:T(8,128)(2,1)} %all-to-all-done.3.mixed, bf16[4,128,192]{2,1,0:T(8,128)(2,1)} %bitcast.22, bf16[2048,192]{1,0:T(8,128)(2,1)} %pad_bitcast_fusion.turned), custom_call_target="tpu_custom_call" | custom-call | flops 402653184 | bytes 8388608 | tf_op jit(solution)/shard_map/final/pallas_call | solution.py:555
Async XLA Ops:
  4.2 8.2 %copy-start.2 = (bf16[188,2048]{1,0:T(8,128)(2,1)S(1)}, bf16[188,2048]{1,0:T(8,128)(2,1)}, u32[]{:S(2)}) copy-start(bf16[188,2048]{1,0:T(8,128)(2,1)} %param.10) | copy-start | bytes 2310148
  4.2 39.5 %all-to-all-start = ((bf16[16,528,128]{2,1,0:T(8,128)(2,1)}), bf16[16,528,128]{2,1,0:T(8,128)(2,1)}, u32[]{:S(2)}, u32[]{:S(2)}) async-start(bf16[16,528,128]{2,1,0:T(8,128)(2,1)} %spread.1), calls=%async_computation | async-start | bytes 4325376 | tf_op jit(solution)/shard_map/all_to_all | solution.py:586
  12.9 1.0 copy-start
  13.9 1.5 copy-start.5
  43.7 32.2 %all-to-all-start.2 = ((s16[16,512,128]{2,1,0:T(8,128)(2,1)}), s16[16,512,128]{2,1,0:T(8,128)(2,1)}, u32[]{:S(2)}, u32[]{:S(2)}) async-start(s16[16,512,128]{2,1,0:T(8,128)(2,1)} %get-tuple-element.18), calls=%async_computation.2 | async-start | bytes 4194304 | tf_op jit(solution)/shard_map/all_to_all | solution.py:586
  50.0 2.6 %collective-permute-start = (bf16[16,64,128]{2,1,0:T(8,128)(2,1)S(1)}, bf16[16,64,128]{2,1,0:T(8,128)(2,1)S(1)}, u32[]{:S(2)}, u32[]{:S(2)}) collective-permute-start(bf16[16,64,128]{2,1,0:T(8,128)(2,1)S(1)} %get-tuple-element.29), channel_id=1, source_target_pairs={{0,16},{16,32},{32,48},{48,64},{64,80},{80,96},{96,112},{1,17},{17... | collective-permute-start | bytes 786440 | tf_op jit(solution)/shard_map/ppermute | solution.py:582
  51.3 5.2 %collective-permute-start.1 = (bf16[16,64,128]{2,1,0:T(8,128)(2,1)S(1)}, bf16[16,64,128]{2,1,0:T(8,128)(2,1)S(1)}, u32[]{:S(2)}, u32[]{:S(2)}) collective-permute-start(bf16[16,64,128]{2,1,0:T(8,128)(2,1)S(1)} %get-tuple-element.28), channel_id=1, source_target_pairs={{16,0},{32,16},{48,32},{64,48},{80,64},{96,80},{112,96},{17,1},{33... | collective-permute-start | bytes 786440 | tf_op jit(solution)/shard_map/ppermute | solution.py:582
  52.6 3.9 %copy-start.6 = (bf16[16,64,128]{2,1,0:T(8,128)(2,1)}, bf16[16,64,128]{2,1,0:T(8,128)(2,1)S(1)}, u32[]{:S(2)}) copy-start(bf16[16,64,128]{2,1,0:T(8,128)(2,1)S(1)} %collective-permute-done.refs_1_) | copy-start | bytes 786436
  56.6 0.7 copy-start.7
  75.9 32.2 %all-to-all-start.1 = ((s16[16,512,128]{2,1,0:T(8,128)(2,1)}), s16[16,512,128]{2,1,0:T(8,128)(2,1)}, u32[]{:S(2)}, u32[]{:S(2)}) async-start(s16[16,512,128]{2,1,0:T(8,128)(2,1)} %get-tuple-element.17.sums_a.sums_b), calls=%async_computation.1 | async-start | bytes 4194304 | tf_op jit(solution)/shard_map/all_to_all | solution.py:586
  84.4 6.8 %collective-permute-start.2 = (bf16[16,64,128]{2,1,0:T(8,128)(2,1)}, bf16[16,64,128]{2,1,0:T(8,128)(2,1)S(1)}, u32[]{:S(2)}, u32[]{:S(2)}) collective-permute-start(bf16[16,64,128]{2,1,0:T(8,128)(2,1)} %get-tuple-element.23), channel_id=1, source_target_pairs={{0,16},{16,32},{32,48},{48,64},{64,80},{80,96},{96,112},{1,17},{17... | collective-permute-start | bytes 786440 | tf_op jit(solution)/shard_map/ppermute | solution.py:582
  85.8 5.5 %collective-permute-start.3 = (bf16[16,64,128]{2,1,0:T(8,128)(2,1)}, bf16[16,64,128]{2,1,0:T(8,128)(2,1)S(1)}, u32[]{:S(2)}, u32[]{:S(2)}) collective-permute-start(bf16[16,64,128]{2,1,0:T(8,128)(2,1)} %get-tuple-element.24), channel_id=1, source_target_pairs={{16,0},{32,16},{48,32},{64,48},{80,64},{96,80},{112,96},{17,1},{33... | collective-permute-start | bytes 786440 | tf_op jit(solution)/shard_map/ppermute | solution.py:582
  91.3 0.7 copy-start.3
  91.3 0.8 copy-start.4
  98.7 13.8 %copy-start.1 = (bf16[188,2048]{0,1:T(8,128)(2,1)S(1)}, bf16[188,2048]{0,1:T(8,128)(2,1)}, u32[]{:S(2)}) copy-start(bf16[188,2048]{0,1:T(8,128)(2,1)} %copy-done) | copy-start | bytes 2310148
  108.0 32.9 %all-to-all-start.3 = ((s16[16,512,128]{2,1,0:T(8,128)(2,1)}), s16[16,512,128]{2,1,0:T(8,128)(2,1)}, u32[]{:S(2)}, u32[]{:S(2)}) async-start(s16[16,512,128]{2,1,0:T(8,128)(2,1)} %mix_second.1), calls=%async_computation.3 | async-start | bytes 4194304 | tf_op jit(solution)/shard_map/all_to_all | solution.py:586

commit v4 on v3

--- a/solution.py
+++ b/solution.py
@@ -22,7 +22,7 @@
 STEPS = 8
 AHEAD = 5
 WIDE = 2
-TABLE_ROWS = 16
+TABLE_ROWS = 8
 MIB = 1024 * 1024
 
 F32 = jnp.float32
@@ -299,18 +299,20 @@
     )(obs.reshape(BLOCKS, block, bands), lib, inv, thr, *carried)
 
 
-def weights_of(tables):
-    size, spots = tables.shape
-    rows = lax.broadcasted_iota(jnp.int32, (2 * size, size), 0)
-    cols = lax.broadcasted_iota(jnp.int32, (2 * size, size), 1)
+def weights_of(tables, size):
+    lines, spots = tables.shape
+    rows = lax.broadcasted_iota(jnp.int32, (2 * size, lines), 0)
+    cols = lax.broadcasted_iota(jnp.int32, (2 * size, lines), 1)
     inner = rows % size
-    line = inner // 16 * 16 + inner % 16 // 4 + BLOCKS * (rows // size)
+    line = inner // 16 * TABLE_ROWS + inner % 16 // 4 + BLOCKS * (rows // size)
     pick = jnp.where(cols == line, 1.0, 0.0).astype(BF16)
     lines = jnp.dot(pick, tables, preferred_element_type=F32).astype(BF16)
     spot = lax.broadcasted_iota(jnp.int32, (spots, size), 0)
     col = lax.broadcasted_iota(jnp.int32, (spots, size), 1)
     widen = jnp.where(spot == col // 4, 1.0, 0.0).astype(BF16)
     wide = jnp.dot(lines, widen, preferred_element_type=F32)
+    rows = lax.broadcasted_iota(jnp.int32, (2 * size, size), 0)
+    cols = lax.broadcasted_iota(jnp.int32, (2 * size, size), 1)
     return jnp.where(rows % 4 == cols % 4, wide, 0.0).astype(BF16)
 
 
@@ -388,7 +390,8 @@
     for copy in copies:
         copy.wait()
     if first:
-        weights[...] = weights_of(tail[...].reshape(-1, LANES))
+        tables = tail[...].astype(F32).reshape(-1, LANES).astype(BF16)
+        weights[...] = weights_of(tables, size)
         keep = pltpu.make_async_copy(weights, table, other.at[1])
         keep.start()
     writes = []
@@ -587,9 +590,11 @@
 
 
 def strip_ends(strip, pixels, edge):
-    tiles = strip[:, :pixels].reshape(strip.shape[0], pixels // 16, 2, 8, LANES)
-    rows = lambda a: a.reshape(strip.shape[0], edge // 2, LANES)
-    return rows(tiles[:, : edge // 16, 0]), rows(tiles[:, (pixels - edge) // 16 :, 1])
+    def rows(a, h):
+        tiles = a.reshape(a.shape[0], edge // 16, 2, 8, LANES)
+        return tiles[:, :, h].reshape(a.shape[0], edge // 2, LANES)
+
+    return rows(strip[:, :edge], 0), rows(strip[:, pixels - edge : pixels], 1)
 
 
 def strip_halos(first, last):

time: 147 us -> 147 us (level)
  no operation moved by 1% of the time
where the time goes in v4:
time: 147 us; the launch traced here: 146 us
  Pallas kernels  57 us (39%)
  waiting for transfers between devices  53.6 us (36%)
  starting transfers between devices  26.9 us (18%)
  local copies, waits for them, and re-layouts  7.73 us (5%)
    all_to_all x4, waiting for transfers between devices, exchanged(): return lax.all_to_all(pieces, 'col', 0, 0, tiled=True)  49.7 us
    all_to_all x4, starting transfers between devices, exchanged(): return lax.all_to_all(pieces, 'col', 0, 0, tiled=True)  21.5 us
    pallas_call x2, Pallas kernels, solve(): pl.pallas_call(functools.partial(solve_kernel, first), grid=(block // row...  19.3 us
    pallas_call x2, Pallas kernels, mix(): pl.pallas_call(functools.partial(mix_kernel, encode, first, row // 4), in...  12.8 us
    pallas_call x2, Pallas kernels, advance(): pl.pallas_call(advance_kernel, grid=(peers // step,), in_specs=[specs[0],...  8.16 us
    pallas_call x1, Pallas kernels, gram_inverse(): pl.pallas_call(inverse_kernel, out_shape=jax.ShapeDtypeStruct((size, size...  7.67 us
    pallas_call x1, Pallas kernels, final(): pl.pallas_call(final_kernel, in_specs=[hbm, hbm, hbm, hbm], out_specs=[hb...  5.57 us
    ppermute x4, starting transfers between devices, shifted(): lax.ppermute(array, axis, pairs if up else [(b, a) for a, b in pairs])  5.38 us
  transfers between devices with their start and end apart: 8, of which 5 were waited for; matrix products, arithmetic and copies ran while one was open for 4% of the time, Pallas kernels for 33%

profile of v4, /device:TPU:0, one launch (start us, length us, event | category | flops | bytes accessed | tf_op | source)
XLA Modules:
  0.0 146.2 jit_solution(16935471224401390911)
XLA Ops:
  0.6 3.5 %spread.1 = bf16[16,520,128]{2,1,0:T(8,128)(2,1)} custom-call(s32[1,2,16]{2,1,0:T(2,128)} %bitcast.30, s32[4,1,8]{2,1,0:T(1,128)} %peer_at.1, s32[4,1,8]{2,1,0:T(1,128)} %slot_at.1, s32[1,4]{1,0:T(1,128)} %bitcast.31, f32[4,1,8]{2,1,0:T(1,128)} %weight_at.1, bf16[4,128,2048]{2,1,0:T(8,128)(2,1)} %bitcast.23), custom_call_target="tpu_custom_call" | custom-call | flops 1048576 | bytes 4194304 | tf_op jit(solution)/shard_map/spread/pallas_call | solution.py:167
  4.2 0.0 copy-start.2
  4.2 8.2 %all-to-all-start = ((bf16[16,520,128]{2,1,0:T(8,128)(2,1)}), bf16[16,520,128]{2,1,0:T(8,128)(2,1)}, u32[]{:S(2)}, u32[]{:S(2)}) async-start(bf16[16,520,128]{2,1,0:T(8,128)(2,1)} %spread.1), calls=%async_computation | async-start | bytes 4259840 | tf_op jit(solution)/shard_map/all_to_all | solution.py:589
  12.4 0.0 copy-done.2
  12.4 0.5 copy.11
  12.9 0.0 copy-start
  12.9 1.0 copy-done
  13.9 0.0 copy-start.5
  13.9 0.5 copy.19
  14.4 1.0 pad.9.clone.lib_ref.refs_1_
  15.4 0.0 copy-done.5
  15.4 0.7 pad.8
  16.1 7.7 %inverse.1.refs_2_ = f32[192,192]{1,0:T(8,128)} custom-call(bf16[192,2048]{1,0:T(8,128)(2,1)} %pad.9.clone.lib_ref.refs_1_), custom_call_target="tpu_custom_call" | custom-call | flops 849346560 | bytes 147456 | tf_op jit(solution)/shard_map/inverse/pallas_call | solution.py:218
  23.8 9.5 %solve_first.1 = (f32[4,128,2048]{2,1,0:T(8,128)}, f32[4,128,2048]{2,1,0:T(8,128)}, s16[16,512,128]{2,1,0:T(8,128)(2,1)}) custom-call(bf16[4,128,192]{2,1,0:T(8,128)(2,1)} %bitcast.20, bf16[192,2048]{1,0:T(8,128)(2,1)} %pad.9.clone.lib_ref.refs_1_, f32[192,192]{1,0:T(8,128)} %inverse.1.refs_2_, f32[1,2048]{1,0:T(1,128)} %bitcast.28, ...), custom_call_target="tpu_custom_call" | custom-call | flops 1207959552 | bytes 16777216 | tf_op jit(solution)/shard_map/solve_first/pallas_call | solution.py:281
  33.3 10.0 %all-to-all-done.refs_0_ = bf16[16,520,128]{2,1,0:T(8,128)(2,1)} async-done(((bf16[16,520,128]{2,1,0:T(8,128)(2,1)}), bf16[16,520,128]{2,1,0:T(8,128)(2,1)}, u32[]{:S(2)}, u32[]{:S(2)}) %all-to-all-start) | async-done | bytes 2129952 | tf_op jit(solution)/shard_map/all_to_all | solution.py:589
  43.2 4.4 %all-to-all-start.2 = ((s16[16,512,128]{2,1,0:T(8,128)(2,1)}), s16[16,512,128]{2,1,0:T(8,128)(2,1)}, u32[]{:S(2)}, u32[]{:S(2)}) async-start(s16[16,512,128]{2,1,0:T(8,128)(2,1)} %get-tuple-element.18), calls=%async_computation.2 | async-start | bytes 4194304 | tf_op jit(solution)/shard_map/all_to_all | solution.py:589
  47.7 1.3 fusion
  49.0 1.3 collective-permute-start
  50.4 1.3 collective-permute-start.1
  51.7 0.0 collective-permute-done.refs_1_
  51.7 0.0 copy-start.6
  51.7 3.9 %collective-permute-done.1.refs_2_ = bf16[16,64,128]{2,1,0:T(8,128)(2,1)S(1)} collective-permute-done((bf16[16,64,128]{2,1,0:T(8,128)(2,1)S(1)}, bf16[16,64,128]{2,1,0:T(8,128)(2,1)S(1)}, u32[]{:S(2)}, u32[]{:S(2)}) %collective-permute-start.1) | collective-permute-done | bytes 262176 | tf_op jit(solution)/shard_map/ppermute | solution.py:585
  55.6 0.0 copy-done.6
  55.6 0.0 copy-start.7
  55.6 0.7 copy-done.7
  56.3 6.2 %mix_first.1 = (s16[16,512,128]{2,1,0:T(8,128)(2,1)}, bf16[512,256]{1,0:T(8,128)(2,1)}) custom-call(bf16[16,520,128]{2,1,0:T(8,128)(2,1)} %all-to-all-done.refs_0_, bf16[16,64,128]{2,1,0:T(8,128)(2,1)} %copy-done.6, bf16[16,64,128]{2,1,0:T(8,128)(2,1)} %copy-done.7), custom_call_target="tpu_custom_call" | custom-call | flops 1073741824 | bytes 4194304 | tf_op jit(solution)/shard_map/mix_first/pallas_call | solution.py:429
  62.5 12.9 %all-to-all-done.2.strip_a.strip_b = s16[16,512,128]{2,1,0:T(8,128)(2,1)} async-done(((s16[16,512,128]{2,1,0:T(8,128)(2,1)}), s16[16,512,128]{2,1,0:T(8,128)(2,1)}, u32[]{:S(2)}, u32[]{:S(2)}) %all-to-all-start.2) | async-done | bytes 2097184 | tf_op jit(solution)/shard_map/all_to_all | solution.py:589
  75.5 4.4 %all-to-all-start.1 = ((s16[16,512,128]{2,1,0:T(8,128)(2,1)}), s16[16,512,128]{2,1,0:T(8,128)(2,1)}, u32[]{:S(2)}, u32[]{:S(2)}) async-start(s16[16,512,128]{2,1,0:T(8,128)(2,1)} %get-tuple-element.17.sums_a.sums_b), calls=%async_computation.1 | async-start | bytes 4194304 | tf_op jit(solution)/shard_map/all_to_all | solution.py:589
  79.9 4.1 %advance_ends.1 = (bf16[16,128,128]{2,1,0:T(8,128)(2,1)}, bf16[16,128,128]{2,1,0:T(8,128)(2,1)}, bf16[16,64,128]{2,1,0:T(8,128)(2,1)}, bf16[16,64,128]{2,1,0:T(8,128)(2,1)}) custom-call(s16[16,512,128]{2,1,0:T(8,128)(2,1)} %all-to-all-done.2.strip_a.strip_b, s16[16,512,128]{2,1,0:T(8,128)(2,1)} %get-tuple-element.17.sums_a.sums_b, ...), custom_call_target="tpu_custom_call" | custom-call | flops 8388608 | bytes 3145728 | tf_op jit(solution)/shard_map/advance_ends/pallas_call | solution.py:473
  84.0 1.3 collective-permute-start.2
  85.3 1.5 %collective-permute-start.3 = (bf16[16,64,128]{2,1,0:T(8,128)(2,1)}, bf16[16,64,128]{2,1,0:T(8,128)(2,1)S(1)}, u32[]{:S(2)}, u32[]{:S(2)}) collective-permute-start(bf16[16,64,128]{2,1,0:T(8,128)(2,1)} %get-tuple-element.24), channel_id=1, source_target_pairs={{16,0},{32,16},{48,32},{64,48},{80,64},{96,80},{112,96},{17,1},{33... | collective-permute-start | bytes 786440 | tf_op jit(solution)/shard_map/ppermute | solution.py:585
  86.8 4.0 %advance_middle.1 = (bf16[16,128,128]{2,1,0:T(8,128)(2,1)}, bf16[16,128,128]{2,1,0:T(8,128)(2,1)}) custom-call(s16[16,512,128]{2,1,0:T(8,128)(2,1)} %all-to-all-done.2.strip_a.strip_b, s16[16,512,128]{2,1,0:T(8,128)(2,1)} %get-tuple-element.17.sums_a.sums_b, s16[16,512,128]{2,1,0:T(8,128)(2,1)} %all-to-all-done.2.strip_a.strip_b, ...), custom_call_target="tpu_custom_call" | custom-call | flops 8388608 | bytes 3145728 | tf_op jit(solution)/shard_map/advance_middle/pallas_call | solution.py:473
  90.9 0.0 collective-permute-done.2.refs_4_
  90.9 0.0 copy-start.3
  90.9 0.0 collective-permute-done.3.refs_5_
  90.9 0.0 copy-start.4
  90.9 0.7 copy-done.3
  91.6 0.1 copy-done.4
  91.7 6.6 %mix_second.1 = s16[16,512,128]{2,1,0:T(8,128)(2,1)} custom-call(bf16[16,128,128]{2,1,0:T(8,128)(2,1)} %get-tuple-element.19.refs_0_, bf16[16,128,128]{2,1,0:T(8,128)(2,1)} %get-tuple-element.20.refs_1_, bf16[16,128,128]{2,1,0:T(8,128)(2,1)} %get-tuple-element.21.refs_2_, bf16[16,128,128]{2,1,0:T(8,128)(2,1)} %get-tuple-element.22.refs_3_, ...), custom_call_target="tpu_custom_call" | custom-call | flops 1073741824 | bytes 4194304 | tf_op jit(solution)/shard_map/mix_second/pallas_call | solution.py:429
  98.3 0.0 copy-start.1
  98.3 9.3 %all-to-all-done.1.refs_6_ = s16[16,512,128]{2,1,0:T(8,128)(2,1)} async-done(((s16[16,512,128]{2,1,0:T(8,128)(2,1)}), s16[16,512,128]{2,1,0:T(8,128)(2,1)}, u32[]{:S(2)}, u32[]{:S(2)}) %all-to-all-start.1) | async-done | bytes 2097184 | tf_op jit(solution)/shard_map/all_to_all | solution.py:589
  107.6 4.4 %all-to-all-start.3 = ((s16[16,512,128]{2,1,0:T(8,128)(2,1)}), s16[16,512,128]{2,1,0:T(8,128)(2,1)}, u32[]{:S(2)}, u32[]{:S(2)}) async-start(s16[16,512,128]{2,1,0:T(8,128)(2,1)} %mix_second.1), calls=%async_computation.3 | async-start | bytes 4194304 | tf_op jit(solution)/shard_map/all_to_all | solution.py:589
  112.1 0.0 copy-done.1
  112.1 1.2 pad_bitcast_fusion.turned
  113.2 9.8 %solve_second.1.parts = f32[4,128,2048]{2,1,0:T(8,128)} custom-call(bf16[4,128,192]{2,1,0:T(8,128)(2,1)} %bitcast.21, bf16[192,2048]{1,0:T(8,128)(2,1)} %pad.9.clone.lib_ref.refs_1_, f32[192,192]{1,0:T(8,128)} %inverse.1.refs_2_, f32[1,2048]{1,0:T(1,128)} %bitcast.29, f32[4,128,2048]{2,1,0:T(8,128)} %get-tuple-element.15.refs_4_, ...), custom_call_target="tpu_custom_call" | custom-call | flops 1207959552 | bytes 16777216 | tf_op jit(solution)/shard_map/solve_second/pallas_call | solution.py:281
  123.1 17.4 %all-to-all-done.3.mixed = s16[16,512,128]{2,1,0:T(8,128)(2,1)} async-done(((s16[16,512,128]{2,1,0:T(8,128)(2,1)}), s16[16,512,128]{2,1,0:T(8,128)(2,1)}, u32[]{:S(2)}, u32[]{:S(2)}) %all-to-all-start.3) | async-done | bytes 2097184 | tf_op jit(solution)/shard_map/all_to_all | solution.py:589
  140.5 5.6 %final.1 = (bf16[4,128,2048]{2,1,0:T(8,128)(2,1)}, f32[4,128,188]{2,1,0:T(8,128)}) custom-call(f32[4,128,2048]{2,1,0:T(8,128)} %solve_second.1.parts, s16[16,512,128]{2,1,0:T(8,128)(2,1)} %all-to-all-done.3.mixed, bf16[4,128,192]{2,1,0:T(8,128)(2,1)} %bitcast.22, bf16[2048,192]{1,0:T(8,128)(2,1)} %pad_bitcast_fusion.turned), custom_call_target="tpu_custom_call" | custom-call | flops 402653184 | bytes 8388608 | tf_op jit(solution)/shard_map/final/pallas_call | solution.py:558
  (2 shorter events, 0.1 us)
Async XLA Ops:
  4.2 8.2 %copy-start.2 = (bf16[188,2048]{1,0:T(8,128)(2,1)S(1)}, bf16[188,2048]{1,0:T(8,128)(2,1)}, u32[]{:S(2)}) copy-start(bf16[188,2048]{1,0:T(8,128)(2,1)} %param.10) | copy-start | bytes 2310148
  4.2 39.0 %all-to-all-start = ((bf16[16,520,128]{2,1,0:T(8,128)(2,1)}), bf16[16,520,128]{2,1,0:T(8,128)(2,1)}, u32[]{:S(2)}, u32[]{:S(2)}) async-start(bf16[16,520,128]{2,1,0:T(8,128)(2,1)} %spread.1), calls=%async_computation | async-start | bytes 4259840 | tf_op jit(solution)/shard_map/all_to_all | solution.py:589
  12.9 1.0 copy-start
  13.9 1.5 copy-start.5
  43.2 32.2 %all-to-all-start.2 = ((s16[16,512,128]{2,1,0:T(8,128)(2,1)}), s16[16,512,128]{2,1,0:T(8,128)(2,1)}, u32[]{:S(2)}, u32[]{:S(2)}) async-start(s16[16,512,128]{2,1,0:T(8,128)(2,1)} %get-tuple-element.18), calls=%async_computation.2 | async-start | bytes 4194304 | tf_op jit(solution)/shard_map/all_to_all | solution.py:589
  49.0 2.7 %collective-permute-start = (bf16[16,64,128]{2,1,0:T(8,128)(2,1)S(1)}, bf16[16,64,128]{2,1,0:T(8,128)(2,1)S(1)}, u32[]{:S(2)}, u32[]{:S(2)}) collective-permute-start(bf16[16,64,128]{2,1,0:T(8,128)(2,1)S(1)} %slice_bitcast_fusion.1), channel_id=1, source_target_pairs={{0,16},{16,32},{32,48},{48,64},{64,80},{80,96},{96,112},{1,17},{17... | collective-permute-start | bytes 786440 | tf_op jit(solution)/shard_map/ppermute | solution.py:585
  50.4 5.2 %collective-permute-start.1 = (bf16[16,64,128]{2,1,0:T(8,128)(2,1)S(1)}, bf16[16,64,128]{2,1,0:T(8,128)(2,1)S(1)}, u32[]{:S(2)}, u32[]{:S(2)}) collective-permute-start(bf16[16,64,128]{2,1,0:T(8,128)(2,1)S(1)} %slice_bitcast_fusion), channel_id=1, source_target_pairs={{16,0},{32,16},{48,32},{64,48},{80,64},{96,80},{112,96},{17,1},{33... | collective-permute-start | bytes 786440 | tf_op jit(solution)/shard_map/ppermute | solution.py:585
  51.7 3.9 %copy-start.6 = (bf16[16,64,128]{2,1,0:T(8,128)(2,1)}, bf16[16,64,128]{2,1,0:T(8,128)(2,1)S(1)}, u32[]{:S(2)}) copy-start(bf16[16,64,128]{2,1,0:T(8,128)(2,1)S(1)} %collective-permute-done.refs_1_) | copy-start | bytes 786436
  55.6 0.7 copy-start.7
  75.5 32.2 %all-to-all-start.1 = ((s16[16,512,128]{2,1,0:T(8,128)(2,1)}), s16[16,512,128]{2,1,0:T(8,128)(2,1)}, u32[]{:S(2)}, u32[]{:S(2)}) async-start(s16[16,512,128]{2,1,0:T(8,128)(2,1)} %get-tuple-element.17.sums_a.sums_b), calls=%async_computation.1 | async-start | bytes 4194304 | tf_op jit(solution)/shard_map/all_to_all | solution.py:589
  84.0 6.8 %collective-permute-start.2 = (bf16[16,64,128]{2,1,0:T(8,128)(2,1)}, bf16[16,64,128]{2,1,0:T(8,128)(2,1)S(1)}, u32[]{:S(2)}, u32[]{:S(2)}) collective-permute-start(bf16[16,64,128]{2,1,0:T(8,128)(2,1)} %get-tuple-element.23), channel_id=1, source_target_pairs={{0,16},{16,32},{32,48},{48,64},{64,80},{80,96},{96,112},{1,17},{17... | collective-permute-start | bytes 786440 | tf_op jit(solution)/shard_map/ppermute | solution.py:585
  85.3 5.5 %collective-permute-start.3 = (bf16[16,64,128]{2,1,0:T(8,128)(2,1)}, bf16[16,64,128]{2,1,0:T(8,128)(2,1)S(1)}, u32[]{:S(2)}, u32[]{:S(2)}) collective-permute-start(bf16[16,64,128]{2,1,0:T(8,128)(2,1)} %get-tuple-element.24), channel_id=1, source_target_pairs={{16,0},{32,16},{48,32},{64,48},{80,64},{96,80},{112,96},{17,1},{33... | collective-permute-start | bytes 786440 | tf_op jit(solution)/shard_map/ppermute | solution.py:585
  90.9 0.7 copy-start.3
  90.9 0.8 copy-start.4
  98.3 13.8 %copy-start.1 = (bf16[188,2048]{0,1:T(8,128)(2,1)S(1)}, bf16[188,2048]{0,1:T(8,128)(2,1)}, u32[]{:S(2)}) copy-start(bf16[188,2048]{0,1:T(8,128)(2,1)} %copy-done) | copy-start | bytes 2310148
  107.6 32.9 %all-to-all-start.3 = ((s16[16,512,128]{2,1,0:T(8,128)(2,1)}), s16[16,512,128]{2,1,0:T(8,128)(2,1)}, u32[]{:S(2)}, u32[]{:S(2)}) async-start(s16[16,512,128]{2,1,0:T(8,128)(2,1)} %mix_second.1), calls=%async_computation.3 | async-start | bytes 4194304 | tf_op jit(solution)/shard_map/all_to_all | solution.py:589
